TPU v7x, 512 devices: a whole 4x4x16 slice. The times are simulated.
512 devices in a mesh: tex: 16 (over z_lo, core), smp: 32 (over z_hi, y, x).
Axes of the slice: x: 4, y: 4, z: 16 (z_hi: 2, z_lo: 8; z = z_hi * 8 + z_lo), core: 2. Of those that a mesh axis runs over, the one named last changes fastest.
Arguments:
- blocks: int32 [16, 32, 2, 2], P('tex', 'smp'), may hold values from -1 to 3, as said below
- observed: float32 [16, 32, 512, 256], P('tex', 'smp'), may hold values from 0.05 to 1.5
- w_factor: float32 [64, 16384], P('smp', 'tex'), may hold values from 0.03 to 0.5
- h_factor: float32 [64, 32768], P('tex', 'smp'), may hold values from 0.03 to 0.5
Outputs:
- w_final: float32 [64, 16384], P('smp', 'tex')
- h_final: float32 [64, 32768], P('tex', 'smp')
Inputs may be any that keep to these rules, and one draw needn't show every extreme that they name: blocks[t, s, 0, j] is a block row (below 4) and blocks[t, s, 1, j] a block column (below 4) of device (t, s)'s tile, or both are -1 for an empty slot; live slots come first and name different blocks; each device has at least one live slot and some device has 2; every block row of texels is observed on some device along smp, and every block column of samples on some device along tex.
All inputs are finite; a program needn't handle non-finite values.
Results may differ from a plain program's by a relative error of at most 0.0003.
Values sent between devices are 32-bit elements; how exact they have to be, the bound alone decides.
No kernel may reach another device: no remote copies, remote signals or barrier semaphores. Data moves between devices by JAX's collectives and lax.ppermute only.
A program may use at most 64 MiB of HBM per device.

v0:
```python
import jax
import jax.numpy as jnp
from jax import lax
from jax.sharding import PartitionSpec as P

BS = 256
RB = 4
CB = 4
CAP = 2
ITERS = 2


highest = lax.Precision.HIGHEST


def from_everyone(x, axis):
    copies = jnp.broadcast_to(x, (lax.axis_size(axis), *x.shape))
    return lax.all_to_all(copies, axis, split_axis=0, concat_axis=0, tiled=True)


def laid_out(tiles, dim):
    shape = list(tiles.shape[1:])
    shape[dim] *= tiles.shape[0]
    return jnp.moveaxis(tiles, 0, dim).reshape(shape)


def gather_directly(x, axis, dim):
    tiles = from_everyone(x, axis)
    return laid_out(tiles, dim)


def split_up(x, dim, length):
    shape = x.shape
    tiles = x.reshape(*shape[:dim], length, shape[dim] // length, *shape[dim + 1 :])
    return jnp.moveaxis(tiles, dim, 0)


def sent_and_summed(x, axis, dim):
    tiles = split_up(x, dim, lax.axis_size(axis))
    arrived = lax.all_to_all(tiles, axis, split_axis=0, concat_axis=0, tiled=True)
    return arrived.sum(axis=0)


def in_one_piece(arrays, axis, dim, along):
    ends, at = ([], 0)
    for a in arrays[:-1]:
        at += a.shape[along]
        ends.append(at)
    both = jnp.concatenate(arrays, axis=along)
    return tuple(jnp.split(sent_and_summed(both, axis, dim), ends, axis=along))


def pick_tables(listing, rows_count, cols_count):
    rows = listing[0]
    cols = listing[1]
    live = (rows >= 0).astype(jnp.float32)
    row_pick = (jnp.maximum(rows, 0)[:, None] == jnp.arange(rows_count)[None, :]).astype(
        jnp.float32
    ) * live[:, None]
    col_pick = (jnp.maximum(cols, 0)[:, None] == jnp.arange(cols_count)[None, :]).astype(
        jnp.float32
    )
    return (row_pick, col_pick)


def block_factors(w_tile, h_tile, row_pick, col_pick):
    rank = w_tile.shape[0]
    w_blocks = jnp.einsum(
        "sr,krb->skb", row_pick, w_tile.reshape(rank, row_pick.shape[1], -1), precision=highest
    )
    h_blocks = jnp.einsum(
        "sc,kcb->skb", col_pick, h_tile.reshape(rank, col_pick.shape[1], -1), precision=highest
    )
    approx = jnp.einsum("ska,skb->sab", w_blocks, h_blocks, precision=highest)
    return (w_blocks, h_blocks, approx)


def basis_terms(w_tile, h_tile, row_pick, col_pick, values):
    w_blocks, h_blocks, approx = block_factors(w_tile, h_tile, row_pick, col_pick)
    upper = jnp.einsum("ska,sab->skb", w_blocks, values, precision=highest)
    lower = jnp.einsum("ska,sab->skb", w_blocks, approx, precision=highest)
    upper = jnp.einsum("sc,skb->kcb", col_pick, upper, precision=highest)
    lower = jnp.einsum("sc,skb->kcb", col_pick, lower, precision=highest)
    return (upper.reshape(h_tile.shape), lower.reshape(h_tile.shape))


def weight_terms(w_tile, h_tile, row_pick, col_pick, values):
    w_blocks, h_blocks, approx = block_factors(w_tile, h_tile, row_pick, col_pick)
    upper = jnp.einsum("skb,sab->ska", h_blocks, values, precision=highest)
    lower = jnp.einsum("skb,sab->ska", h_blocks, approx, precision=highest)
    upper = jnp.einsum("sr,ska->kra", row_pick, upper, precision=highest)
    lower = jnp.einsum("sr,ska->kra", row_pick, lower, precision=highest)
    return (upper.reshape(w_tile.shape), lower.reshape(w_tile.shape))


def per_device(blocks, observed, w_factor, h_factor):
    row_pick, col_pick = pick_tables(blocks[0, 0], RB, CB)
    values = observed[0, 0].reshape(CAP, BS, BS)
    w_full = gather_directly(w_factor, "smp", 0)
    h_full = gather_directly(h_factor, "tex", 0)
    w_share = w_factor
    h_share = h_factor
    for sweep in range(ITERS):
        upper, lower = basis_terms(w_full, h_full, row_pick, col_pick, values)
        upper, lower = in_one_piece((upper, lower), "tex", 0, 1)
        h_share = h_share * upper / lower
        h_full = lax.all_gather(h_share, "tex", axis=0, tiled=True)
        upper, lower = weight_terms(w_full, h_full, row_pick, col_pick, values)
        upper, lower = in_one_piece((upper, lower), "smp", 0, 1)
        w_share = w_share * upper / lower
        if sweep + 1 < ITERS:
            w_full = gather_directly(w_share, "smp", 0)
    return (w_share, h_share)


def solution(mesh):
    in_specs = (
        P("tex", "smp", None, None),
        P("tex", "smp", None, None),
        P("smp", "tex"),
        P("tex", "smp"),
    )
    out_specs = (P("smp", "tex"), P("tex", "smp"))
    return jax.shard_map(
        per_device, mesh=mesh, in_specs=in_specs, out_specs=out_specs, check_vma=False
    )
```

profile of v0, /device:TPU:1, one launch (start us, length us, event | category | flops | bytes accessed | tf_op | source)
XLA Modules:
  0.0 299.6 jit_solution(6733936560634182078)
XLA Ops:
  0.6 0.8 broadcast_in_dim.7
  1.5 30.8 %all_to_all.35 = f32[16,4,1024]{2,1,0:T(4,128)S(1)} all-to-all(f32[16,4,1024]{2,1,0:T(4,128)S(1)} %broadcast_in_dim.7), channel_id=1, replica_groups=mesh['tex'=16,'smp'=32] {'tex'}, dimensions={0} | all-to-all | bytes 524288 | tf_op jit(solution)/shard_map/all_to_all | solution.py:18
  32.3 0.8 broadcast_in_dim.6
  33.1 12.9 %all-to-all-start = ((f32[32,2,1024]{2,1,0:T(2,128)}), f32[32,2,1024]{2,1,0:T(2,128)S(1)}, u32[]{:S(2)}, u32[]{:S(2)}) async-start(f32[32,2,1024]{2,1,0:T(2,128)} %broadcast_in_dim.6), calls=%async_computation | async-start | bytes 524288 | tf_op jit(solution)/shard_map/all_to_all | solution.py:18
  46.7 17.1 %all-to-all-done = f32[32,2,1024]{2,1,0:T(2,128)S(1)} async-done(((f32[32,2,1024]{2,1,0:T(2,128)}), f32[32,2,1024]{2,1,0:T(2,128)S(1)}, u32[]{:S(2)}, u32[]{:S(2)}) %all-to-all-start) | async-done | bytes 262176 | tf_op jit(solution)/shard_map/all_to_all | solution.py:18
  64.0 0.6 fusion.61
  65.8 0.6 fusion.7
  67.7 39.3 %all_to_all.36 = f32[16,4,2048]{2,1,0:T(4,128)S(1)} all-to-all(f32[16,4,2048]{2,1,0:T(4,128)S(1)} %pad_maximum_fusion), channel_id=1, replica_groups=mesh['tex'=16,'smp'=32] {'tex'}, dimensions={0} | all-to-all | bytes 1048576 | tf_op jit(solution)/shard_map/all_to_all | solution.py:40
  107.1 0.6 copy-done.1
  107.7 31.7 %all-gather = f32[16,4,1024]{2,1,0:T(4,128)S(1)} all-gather(f32[1,4,1024]{2,1,0:T(4,128)S(1)} %bitcast.65), channel_id=1, replica_groups=mesh['tex'=16,'smp'=32] {'tex'}, dimensions={0}, use_global_device_ids=true | all-gather | bytes 278528 | tf_op jit(solution)/shard_map/all_gather | solution.py:107
  140.6 0.6 fusion.26
  141.2 0.7 convolution_bitcast_fusion.7
  142.8 0.7 convolution_bitcast_fusion.6
  144.0 24.7 %all_to_all.37 = f32[32,2,2048]{2,1,0:T(2,128)S(1)} all-to-all(f32[32,2,2048]{2,1,0:T(2,128)S(1)} %pad_maximum_fusion.1), channel_id=1, replica_groups=mesh['tex'=16,'smp'=32] {'smp'}, dimensions={0} | all-to-all | bytes 1048576 | tf_op jit(solution)/shard_map/all_to_all | solution.py:40
  168.9 30.5 %all_to_all.38 = f32[32,2,1024]{2,1,0:T(2,128)S(1)} all-to-all(f32[32,2,1024]{2,1,0:T(2,128)S(1)} %broadcast_in_dim.16), channel_id=1, replica_groups=mesh['tex'=16,'smp'=32] {'smp'}, dimensions={0} | all-to-all | bytes 524288 | tf_op jit(solution)/shard_map/all_to_all | solution.py:18
  199.6 0.6 fusion.57
  200.7 0.6 fusion.19
  203.3 34.6 %all_to_all.39 = f32[16,4,2048]{2,1,0:T(4,128)S(1)} all-to-all(f32[16,4,2048]{2,1,0:T(4,128)S(1)} %pad_maximum_fusion.2), channel_id=1, replica_groups=mesh['tex'=16,'smp'=32] {'tex'}, dimensions={0} | all-to-all | bytes 1048576 | tf_op jit(solution)/shard_map/all_to_all | solution.py:40
  238.0 31.7 %all-gather.1 = f32[16,4,1024]{2,1,0:T(4,128)S(1)} all-gather(f32[1,4,1024]{2,1,0:T(4,128)S(1)} %bitcast.66), channel_id=1, replica_groups=mesh['tex'=16,'smp'=32] {'tex'}, dimensions={0}, use_global_device_ids=true | all-gather | bytes 278528 | tf_op jit(solution)/shard_map/all_gather | solution.py:107
  270.9 0.6 fusion.12
  271.5 0.7 convolution_bitcast_fusion.5
  273.0 0.7 convolution_bitcast_fusion.4
  274.3 24.6 %all_to_all.40 = f32[32,2,2048]{2,1,0:T(2,128)S(1)} all-to-all(f32[32,2,2048]{2,1,0:T(2,128)S(1)} %pad_maximum_fusion.3), channel_id=1, replica_groups=mesh['tex'=16,'smp'=32] {'smp'}, dimensions={0} | all-to-all | bytes 1048576 | tf_op jit(solution)/shard_map/all_to_all | solution.py:40
  299.0 0.6 slice_divide_fusion.2
  (51 shorter events, 11.5 us)
Async XLA Ops:
  0.6 64.0 %copy-start = (f32[1,1,512,256]{3,2,1,0:T(8,128)S(1)}, f32[1,1,512,256]{3,2,1,0:T(8,128)}, u32[]{:S(2)}) copy-start(f32[1,1,512,256]{3,2,1,0:T(8,128)} %param.5) | copy-start | bytes 1572868
  1.5 30.9 %copy-start.3 = (f32[2,1024]{1,0:T(2,128)S(1)}, f32[2,1024]{1,0:T(2,128)}, u32[]{:S(2)}) copy-start(f32[2,1024]{1,0:T(2,128)} %param.6) | copy-start | bytes 24580
  33.1 12.9 %copy-start.4 = (s32[1,1,2,2]{3,2,1,0:T(2,128)S(1)}, s32[1,1,2,2]{3,2,1,0:T(2,128)}, u32[]{:S(2)}) copy-start(s32[1,1,2,2]{3,2,1,0:T(2,128)} %param.4) | copy-start | bytes 52
  33.1 30.7 %all-to-all-start = ((f32[32,2,1024]{2,1,0:T(2,128)}), f32[32,2,1024]{2,1,0:T(2,128)S(1)}, u32[]{:S(2)}, u32[]{:S(2)}) async-start(f32[32,2,1024]{2,1,0:T(2,128)} %broadcast_in_dim.6), calls=%async_computation | async-start | bytes 524288 | tf_op jit(solution)/shard_map/all_to_all | solution.py:18
  107.0 0.7 copy-start.1
  238.0 31.7 %copy-start.2 = (f32[4,1024]{1,0:T(4,128)}, f32[4,1024]{1,0:T(4,128)S(1)}, u32[]{:S(2)}) copy-start(f32[4,1024]{1,0:T(4,128)S(1)} %slice_divide_fusion) | copy-start | bytes 49156
where the time goes:
time: 300 us
  blocking collectives  248 us (83%)
  waiting for transfers between devices  17.1 us (6%)
  matrix products  13.9 us (5%)
  starting transfers between devices  12.9 us (4%)
  local copies, waits for them, and re-layouts  4.99 us (2%)
    all_to_all x4, blocking collectives, sent_and_summed(): lax.all_to_all(tiles, axis, split_axis=0, concat_axis=0, tiled=True)  123 us
    all_gather x2, blocking collectives, per_device(): h_full = lax.all_gather(h_share, 'tex', axis=0, tiled=True)  63.4 us
    all_to_all x2, blocking collectives, from_everyone(): return lax.all_to_all(copies, axis, split_axis=0, concat_axis=0, tiled=True)  61.3 us
    all_to_all x1, waiting for transfers between devices, from_everyone(): return lax.all_to_all(copies, axis, split_axis=0, concat_axis=0, tiled=True)  17.1 us
    all_to_all x1, starting transfers between devices, from_everyone(): return lax.all_to_all(copies, axis, split_axis=0, concat_axis=0, tiled=True)  12.9 us
  transfers between devices with their start and end apart: 1, of which 1 were waited for; matrix products, arithmetic and copies ran while one was open for 0% of the time, Pallas kernels for 0%

commit v1 on v0

v1 whole, which is shorter than its diff:
```python
import jax
import jax.numpy as jnp
from jax import lax
from jax.experimental import pallas as pl
from jax.experimental.pallas import tpu as pltpu
from jax.sharding import Mesh, PartitionSpec as P

RANK = 64
BS = 256
CAP = 2
NB = 4
TAB = 128

FINE = ("z4", "z2", "z1", "core", "zh", "y", "x")
HALF = ("z2", "z1", "core")
PLANE = ("y", "x")
TEX = HALF + ("z4",)
SMP = PLANE + ("zh",)
NH = 8
NP = 16

NN = (((1,), (0,)), ((), ()))
NT = (((1,), (1,)), ((), ()))


def exchange(x, axes):
    return lax.all_to_all(x, axes, split_axis=0, concat_axis=0, tiled=True)


def swap(x, axis):
    return lax.ppermute(x, axis, [(0, 1), (1, 0)])


def halves(x):
    hi = x.astype(jnp.bfloat16)
    lo = (x - hi.astype(jnp.float32)).astype(jnp.bfloat16)
    return hi, lo


def product(a, b, dims):
    dot = lambda x, y: lax.dot_general(x, y, dims, preferred_element_type=jnp.float32)
    return dot(a[0], b[0]) + (dot(a[0], b[1]) + dot(a[1], b[0]))


def sums(left, right, values, dims, live):
    whole = halves(left)
    left = halves(left * live)
    upper = product(left, halves(values), dims)
    gram = product(left, whole, NT)
    lower = product(halves(gram), halves(right), NN)
    return upper, lower


def live_of(blk, j):
    return jnp.where(blk[0, j] >= 0, 1.0, 0.0).astype(jnp.float32)


def block_of(blk, d, j):
    return jnp.maximum(blk[d, j], 0)


def send_h(out, j, upper, lower):
    for q in range(NH):
        out[q, 16 * j : 16 * j + 8, :] = upper[8 * q : 8 * q + 8, :]
        out[q, 16 * j + 8 : 16 * j + 16, :] = lower[8 * q : 8 * q + 8, :]


def first_kernel(blk, pos, w0, h0, values, w_slots, h_own, w_own, out):
    for j in range(CAP):
        at = pl.multiple_of(block_of(blk, 0, j) * BS, BS)
        for q in range(2 * NP):
            w_slots[j, 2 * q : 2 * q + 2, :] = w0[q, :, pl.ds(at, BS)]
        at = pl.multiple_of(block_of(blk, 1, j) * BS, BS)
        rows = []
        for q in range(NH):
            for high in range(2):
                for z in range(2):
                    rows.append(h0[2 * q + z, 2 * high : 2 * high + 2, pl.ds(at, BS)])
        upper, lower = sums(
            w_slots[j], jnp.concatenate(rows, axis=0), values[j * BS : (j + 1) * BS, :], NN, live_of(blk, j)
        )
        send_h(out, j, upper, lower)
    for b in range(NB):
        for z in range(2):
            w_own[b, 2 * z : 2 * z + 2, :] = w0[2 * pos[1] + z, :, b * BS : (b + 1) * BS]
            for high in range(2):
                h_own[b, 4 * high + 2 * z : 4 * high + 2 * z + 2, :] = h0[
                    2 * pos[0] + z, 2 * high : 2 * high + 2, b * BS : (b + 1) * BS
                ]


def h_slot(got, j):
    return got[:, 8 * j : 8 * j + 8, :].reshape(RANK, BS)


def w_slot(got, j):
    return jnp.concatenate([got[q, 4 * j : 4 * j + 4, :] for q in range(NP)], axis=0)


def w_terms_kernel(blk, h_got, w_slots, values, out):
    share = out.shape[1] // (2 * CAP)
    for j in range(CAP):
        upper, lower = sums(h_slot(h_got, j), w_slots[j], values[j * BS : (j + 1) * BS, :], NT, live_of(blk, j))
        for q in range(out.shape[0]):
            at = 2 * share * j
            out[q, at : at + share, :] = upper[share * q : share * (q + 1), :]
            out[q, at + share : at + 2 * share, :] = lower[share * q : share * (q + 1), :]


def h_terms_kernel(blk, w_got, h_got, values, w_slots, out):
    for j in range(CAP):
        w_slots[j] = w_slot(w_got, j)
        upper, lower = sums(w_slots[j], h_slot(h_got, j), values[j * BS : (j + 1) * BS, :], NN, live_of(blk, j))
        send_h(out, j, upper, lower)


def peer_block(table, pos, which, q, j):
    return jnp.maximum(table[(2 * q + pos[which]) * CAP + j], 0)


def collect_kernel(which, table, pos, got, out):
    rows = out.shape[1]
    out[...] = jnp.zeros(out.shape, out.dtype)
    for q in range(got.shape[0]):
        for j in range(CAP):
            b = peer_block(table, pos, which, q, j)
            out[b] = out[b] + got[q, rows * j : rows * (j + 1), :]


def updated(own, mine, theirs):
    rows = own.shape[1]
    upper = mine[:, :rows, :] + theirs[:, :rows, :]
    lower = mine[:, rows:, :] + theirs[:, rows:, :]
    return own[...] * upper / lower


def update_kernel(which, table, pos, own, mine, theirs, new, out):
    rows = own.shape[1]
    new[...] = updated(own, mine, theirs)
    for q in range(out.shape[0]):
        for j in range(CAP):
            out[q, rows * j : rows * (j + 1), :] = new[peer_block(table, pos, which, q, j)]


def last_kernel(table, pos, own, got, out, acc):
    acc[...] = jnp.zeros(acc.shape, acc.dtype)
    for q in range(2 * NP):
        for j in range(CAP):
            b = jnp.maximum(table[q * CAP + j], 0)
            acc[b] = acc[b] + got[q, 4 * j : 4 * j + 4, :]
    z = pos[3]
    for b in range(NB):
        mine = jnp.where(z == 0, own[b, 0:2, :], own[b, 2:4, :])
        out[:, b * BS : (b + 1) * BS] = mine * acc[b, 0:2, :] / acc[b, 2:4, :]


def call(body, scalars, arrays, outs, scratch=(), name=None):
    smem = pl.BlockSpec(memory_space=pltpu.SMEM)
    vmem = pl.BlockSpec(memory_space=pltpu.VMEM)
    shapes = [jax.ShapeDtypeStruct(s, jnp.float32) for s in outs]
    return pl.pallas_call(
        body,
        in_specs=[smem] * len(scalars) + [vmem] * len(arrays),
        out_specs=[vmem] * len(outs),
        out_shape=shapes,
        scratch_shapes=[pltpu.VMEM(s, jnp.float32) for s in scratch],
        name=name,
    )(*scalars, *arrays)


def with_list(factor, listing, copies):
    listed = jnp.zeros((factor.shape[0], TAB), jnp.float32)
    listed = listed.at[:, :CAP].set(listing.astype(jnp.float32)[None, :])
    message = jnp.concatenate([factor, listed], axis=1)
    return jnp.broadcast_to(message, (copies, *message.shape))


def table_of(got):
    return got[:, 0, NB * BS : NB * BS + CAP].astype(jnp.int32).reshape(-1)


def per_device(blocks, observed, w_factor, h_factor):
    blk = blocks[0, 0]
    values = observed[0, 0]
    half = lax.axis_index(HALF)
    plane = lax.axis_index(PLANE)
    pos = jnp.stack([half, plane, lax.axis_index("z4"), lax.axis_index("zh")]).astype(jnp.int32)

    h_got0 = exchange(with_list(h_factor, blk[1], 2 * NH), TEX)
    w_got0 = exchange(with_list(w_factor, blk[0], 2 * NP), SMP)
    cols = table_of(h_got0)
    rows = table_of(w_got0)

    def h_round(sent, own, name):
        got = exchange(sent, HALF)
        (mine,) = call(lambda *r: collect_kernel(2, *r), (cols, pos), (got,), [(NB, 16, BS)], name=name + "_collect")
        theirs = swap(mine, "z4")
        own, out = call(
            lambda *r: update_kernel(2, *r),
            (cols, pos),
            (own, mine, theirs),
            [(NB, 8, BS), (NH, 16, BS)],
            name=name + "_update",
        )
        return own, exchange(out, HALF)

    w_slots, h_own, w_own, sent = call(
        first_kernel,
        (blk, pos),
        (w_got0, h_got0, values),
        [(CAP, RANK, BS), (NB, 8, BS), (NB, 4, BS), (NH, 32, BS)],
        name="h1_terms",
    )
    h_own, h_got = h_round(sent, h_own, "h1")

    (sent,) = call(w_terms_kernel, (blk,), (h_got, w_slots, values), [(NP, 16, BS)], name="w1_terms")
    got = exchange(sent, PLANE)
    (mine,) = call(lambda *r: collect_kernel(3, *r), (rows, pos), (got,), [(NB, 8, BS)], name="w1_collect")
    theirs = swap(mine, "zh")
    w_own, out = call(
        lambda *r: update_kernel(3, *r),
        (rows, pos),
        (w_own, mine, theirs),
        [(NB, 4, BS), (NP, 8, BS)],
        name="w1_update",
    )
    w_got = exchange(out, PLANE)

    w_slots, sent = call(
        h_terms_kernel,
        (blk,),
        (w_got, h_got, values),
        [(CAP, RANK, BS), (NH, 32, BS)],
        name="h2_terms",
    )
    h_own, h_got = h_round(sent, h_own, "h2")

    (sent,) = call(w_terms_kernel, (blk,), (h_got, w_slots, values), [(2 * NP, 8, BS)], name="w2_terms")
    got = exchange(sent, SMP)
    (w_final,) = call(
        last_kernel, (rows, pos), (w_own, got), [(2, NB * BS)], scratch=[(NB, 4, BS)], name="w2_update"
    )
    z = lax.axis_index("z4")
    h_rows = h_own.reshape(NB, 2, 2, 2, BS)
    h_rows = lax.dynamic_index_in_dim(h_rows, z, axis=2, keepdims=False)
    h_final = jnp.moveaxis(h_rows.reshape(NB, 4, BS), 0, 1).reshape(4, NB * BS)
    return w_final, h_final


def solution(mesh):
    fine = Mesh(mesh.devices.reshape(2, 2, 2, 2, 2, 4, 4), FINE)
    tex = ("z4",) + HALF
    smp = ("zh",) + PLANE
    in_specs = (P(tex, smp, None, None), P(tex, smp, None, None), P(smp, tex), P(tex, smp))
    out_specs = (P(smp, tex), P(tex, smp))
    return jax.shard_map(per_device, mesh=fine, in_specs=in_specs, out_specs=out_specs, check_vma=False)
```

time: 300 us -> 245 us (0.82)
  the two profiles are of different devices: /device:TPU:1 before, /device:TPU:32 now
where the time goes in v1:
time: 245 us; the launch traced here: 243 us
  waiting for transfers between devices  114 us (47%)
  blocking collectives  49.3 us (20%)
  starting transfers between devices  46.2 us (19%)
  Pallas kernels  21.6 us (9%)
  local copies, waits for them, and re-layouts  8.14 us (3%)
  other arithmetic  3.47 us (1%)
    all_to_all x5, waiting for transfers between devices, exchange(): return lax.all_to_all(x, axes, split_axis=0, concat_axis=0, tiled=True)  84.7 us
    all_to_all x4, blocking collectives, exchange(): return lax.all_to_all(x, axes, split_axis=0, concat_axis=0, tiled=True)  49.3 us
    all_to_all x5, starting transfers between devices, exchange(): return lax.all_to_all(x, axes, split_axis=0, concat_axis=0, tiled=True)  36.7 us
    ppermute x3, waiting for transfers between devices, swap(): return lax.ppermute(x, axis, [(0, 1), (1, 0)])  29.2 us
    pallas_call x11, Pallas kernels, call(): pl.pallas_call(body, in_specs=[smem] * len(scalars) + [vmem] * len(arrays...  21.6 us
    ppermute x3, starting transfers between devices, swap(): return lax.ppermute(x, axis, [(0, 1), (1, 0)])  9.42 us
    unnamed x26, local copies, waits for them, and re-layouts  5.31 us
  transfers between devices with their start and end apart: 8, of which 8 were waited for; matrix products, arithmetic and copies ran while one was open for 2% of the time, Pallas kernels for 0%

profile of v1, /device:TPU:32, one launch (start us, length us, event | category | flops | bytes accessed | tf_op | source)
XLA Modules:
  0.0 243.3 jit_solution(10870288469873676048)
XLA Ops:
  2.8 12.8 %all-to-all-start.1 = ((f32[16,4,1152]{2,1,0:T(4,128)}), f32[16,4,1152]{2,1,0:T(4,128)S(1)}, u32[]{:S(2)}, u32[]{:S(2)}) async-start(f32[16,4,1152]{2,1,0:T(4,128)} %broadcast_in_dim.5), calls=%async_computation.1 | async-start | bytes 589824 | tf_op jit(solution)/shard_map/all_to_all | solution.py:27
  15.6 18.4 %all-to-all-done.1.h0 = f32[16,4,1152]{2,1,0:T(4,128)S(1)} async-done(((f32[16,4,1152]{2,1,0:T(4,128)}), f32[16,4,1152]{2,1,0:T(4,128)S(1)}, u32[]{:S(2)}, u32[]{:S(2)}) %all-to-all-start.1) | async-done | bytes 294944 | tf_op jit(solution)/shard_map/all_to_all | solution.py:27
  34.8 13.1 %all-to-all-start = ((f32[32,2,1152]{2,1,0:T(2,128)}), f32[32,2,1152]{2,1,0:T(2,128)S(1)}, u32[]{:S(2)}, u32[]{:S(2)}) async-start(f32[32,2,1152]{2,1,0:T(2,128)} %broadcast_in_dim.4), calls=%async_computation | async-start | bytes 589824 | tf_op jit(solution)/shard_map/all_to_all | solution.py:27
  48.4 26.8 %all-to-all-done.w0 = f32[32,2,1152]{2,1,0:T(2,128)S(1)} async-done(((f32[32,2,1152]{2,1,0:T(2,128)}), f32[32,2,1152]{2,1,0:T(2,128)S(1)}, u32[]{:S(2)}, u32[]{:S(2)}) %all-to-all-start) | async-done | bytes 294944 | tf_op jit(solution)/shard_map/all_to_all | solution.py:27
  75.9 2.5 %h1_terms.1 = (f32[2,64,256]{2,1,0:T(8,128)}, f32[4,8,256]{2,1,0:T(8,128)}, f32[4,4,256]{2,1,0:T(4,128)}, f32[8,32,256]{2,1,0:T(8,128)}) custom-call(s32[2,2]{1,0:T(2,128)} %bitcast.20, s32[4]{0:T(128)} %pad_add_fusion.pos.r_1_, f32[32,2,1152]{2,1,0:T(2,128)} %copy-done, f32[16,4,1152]{2,1,0:T(4,128)} %copy-done.1, f32[512,256]{1,0:T(8,128)} %bitcast.15), custom_call_target="tpu_custom_call" | custom-call | tf_op jit(solution)/shard_map/h1_terms/pallas_call | solution.py:161
  78.4 3.4 %all-to-all-start.2 = ((f32[8,32,256]{2,1,0:T(8,128)}), f32[8,32,256]{2,1,0:T(8,128)S(1)}, u32[]{:S(2)}, u32[]{:S(2)}) async-start(f32[8,32,256]{2,1,0:T(8,128)} %get-tuple-element.40), calls=%async_computation.2 | async-start | bytes 524288 | tf_op jit(solution)/shard_map/all_to_all | solution.py:27
  83.2 6.3 %all-to-all-done.2.r_2_ = f32[8,32,256]{2,1,0:T(8,128)S(1)} async-done(((f32[8,32,256]{2,1,0:T(8,128)}), f32[8,32,256]{2,1,0:T(8,128)S(1)}, u32[]{:S(2)}, u32[]{:S(2)}) %all-to-all-start.2) | async-done | bytes 262176 | tf_op jit(solution)/shard_map/all_to_all | solution.py:27
  91.8 3.6 %collective-permute-start = (f32[4,16,256]{2,1,0:T(8,128)}, f32[4,16,256]{2,1,0:T(8,128)S(1)}, u32[]{:S(2)}, u32[]{:S(2)}) collective-permute-start(f32[4,16,256]{2,1,0:T(8,128)} %h1_collect.1.r_3_), channel_id=1, source_target_pairs={{0,256},{256,0},{1,257},{257,1},{2,258},{258,2},{3,259},{259,3},{4... | collective-permute-start | bytes 196616 | tf_op jit(solution)/shard_map/ppermute | solution.py:31
  95.4 8.4 %collective-permute-done.r_4_ = f32[4,16,256]{2,1,0:T(8,128)S(1)} collective-permute-done((f32[4,16,256]{2,1,0:T(8,128)}, f32[4,16,256]{2,1,0:T(8,128)S(1)}, u32[]{:S(2)}, u32[]{:S(2)}) %collective-permute-start) | collective-permute-done | bytes 65568 | tf_op jit(solution)/shard_map/ppermute | solution.py:31
  106.0 12.1 %all_to_all.45.h_got = f32[8,16,256]{2,1,0:T(8,128)} all-to-all(f32[8,16,256]{2,1,0:T(8,128)} %get-tuple-element.41), channel_id=1, replica_groups=mesh['z4'=2,'z2'=2,'z1'=2,'core'=2,'zh'=2,'y'=4,'x'=4] {'z2','z1','core'}, dimensions={0} | all-to-all | bytes 262144 | tf_op jit(solution)/shard_map/all_to_all | solution.py:27
  118.2 2.4 %w1_terms.1 = f32[16,16,256]{2,1,0:T(8,128)} custom-call(s32[2,2]{1,0:T(2,128)} %bitcast.21, f32[8,16,256]{2,1,0:T(8,128)} %all_to_all.45.h_got, f32[2,64,256]{2,1,0:T(8,128)} %get-tuple-element.42.w_slots, f32[512,256]{1,0:T(8,128)} %bitcast.16), custom_call_target="tpu_custom_call" | custom-call | tf_op jit(solution)/shard_map/w1_terms/pallas_call | solution.py:161
  120.6 3.5 %all-to-all-start.4 = ((f32[16,16,256]{2,1,0:T(8,128)}), f32[16,16,256]{2,1,0:T(8,128)S(1)}, u32[]{:S(2)}, u32[]{:S(2)}) async-start(f32[16,16,256]{2,1,0:T(8,128)} %w1_terms.1), calls=%async_computation.4 | async-start | bytes 524288 | tf_op jit(solution)/shard_map/all_to_all | solution.py:27
  125.6 7.3 %all-to-all-done.4.r_2_ = f32[16,16,256]{2,1,0:T(8,128)S(1)} async-done(((f32[16,16,256]{2,1,0:T(8,128)}), f32[16,16,256]{2,1,0:T(8,128)S(1)}, u32[]{:S(2)}, u32[]{:S(2)}) %all-to-all-start.4) | async-done | bytes 262176 | tf_op jit(solution)/shard_map/all_to_all | solution.py:27
  135.4 2.6 %collective-permute-start.1 = (f32[4,8,256]{2,1,0:T(8,128)}, f32[4,8,256]{2,1,0:T(8,128)S(1)}, u32[]{:S(2)}, u32[]{:S(2)}) collective-permute-start(f32[4,8,256]{2,1,0:T(8,128)} %w1_collect.1.r_3_), channel_id=1, source_target_pairs={{0,16},{16,0},{1,17},{17,1},{2,18},{18,2},{3,19},{19,3},{4,20},{20... | collective-permute-start | bytes 98312 | tf_op jit(solution)/shard_map/ppermute | solution.py:31
  137.9 12.1 %collective-permute-done.1.r_4_ = f32[4,8,256]{2,1,0:T(8,128)S(1)} collective-permute-done((f32[4,8,256]{2,1,0:T(8,128)}, f32[4,8,256]{2,1,0:T(8,128)S(1)}, u32[]{:S(2)}, u32[]{:S(2)}) %collective-permute-start.1) | collective-permute-done | bytes 32800 | tf_op jit(solution)/shard_map/ppermute | solution.py:31
  152.2 12.1 %all_to_all.46.w_got = f32[16,8,256]{2,1,0:T(8,128)} all-to-all(f32[16,8,256]{2,1,0:T(8,128)} %get-tuple-element.45), channel_id=1, replica_groups=mesh['z4'=2,'z2'=2,'z1'=2,'core'=2,'zh'=2,'y'=4,'x'=4] {'y','x'}, dimensions={0} | all-to-all | bytes 262144 | tf_op jit(solution)/shard_map/all_to_all | solution.py:27
  164.3 2.5 %h2_terms.1 = (f32[2,64,256]{2,1,0:T(8,128)}, f32[8,32,256]{2,1,0:T(8,128)}) custom-call(s32[2,2]{1,0:T(2,128)} %bitcast.22, f32[16,8,256]{2,1,0:T(8,128)} %all_to_all.46.w_got, f32[8,16,256]{2,1,0:T(8,128)} %all_to_all.45.h_got, f32[512,256]{1,0:T(8,128)} %bitcast.17), custom_call_target="tpu_custom_call" | custom-call | tf_op jit(solution)/shard_map/h2_terms/pallas_call | solution.py:161
  166.8 12.8 %all_to_all.47.r_2_ = f32[8,32,256]{2,1,0:T(8,128)} all-to-all(f32[8,32,256]{2,1,0:T(8,128)} %get-tuple-element.46), channel_id=1, replica_groups=mesh['z4'=2,'z2'=2,'z1'=2,'core'=2,'zh'=2,'y'=4,'x'=4] {'z2','z1','core'}, dimensions={0} | all-to-all | bytes 524288 | tf_op jit(solution)/shard_map/all_to_all | solution.py:27
  181.2 3.3 %collective-permute-start.2 = (f32[4,16,256]{2,1,0:T(8,128)}, f32[4,16,256]{2,1,0:T(8,128)S(1)}, u32[]{:S(2)}, u32[]{:S(2)}) collective-permute-start(f32[4,16,256]{2,1,0:T(8,128)} %h2_collect.1.r_3_), channel_id=1, source_target_pairs={{0,256},{256,0},{1,257},{257,1},{2,258},{258,2},{3,259},{259,3},{4... | collective-permute-start | bytes 196616 | tf_op jit(solution)/shard_map/ppermute | solution.py:31
  184.5 8.7 %collective-permute-done.2.r_4_ = f32[4,16,256]{2,1,0:T(8,128)S(1)} collective-permute-done((f32[4,16,256]{2,1,0:T(8,128)}, f32[4,16,256]{2,1,0:T(8,128)S(1)}, u32[]{:S(2)}, u32[]{:S(2)}) %collective-permute-start.2) | collective-permute-done | bytes 65568 | tf_op jit(solution)/shard_map/ppermute | solution.py:31
  195.4 12.2 %all_to_all.48.h_got = f32[8,16,256]{2,1,0:T(8,128)} all-to-all(f32[8,16,256]{2,1,0:T(8,128)} %get-tuple-element.47), channel_id=1, replica_groups=mesh['z4'=2,'z2'=2,'z1'=2,'core'=2,'zh'=2,'y'=4,'x'=4] {'z2','z1','core'}, dimensions={0} | all-to-all | bytes 262144 | tf_op jit(solution)/shard_map/all_to_all | solution.py:27
  207.6 2.5 %w2_terms.1 = f32[32,8,256]{2,1,0:T(8,128)} custom-call(s32[2,2]{1,0:T(2,128)} %bitcast.23, f32[8,16,256]{2,1,0:T(8,128)} %all_to_all.48.h_got, f32[2,64,256]{2,1,0:T(8,128)} %get-tuple-element.48.w_slots, f32[512,256]{1,0:T(8,128)} %bitcast.18), custom_call_target="tpu_custom_call" | custom-call | tf_op jit(solution)/shard_map/w2_terms/pallas_call | solution.py:161
  210.0 4.0 %all-to-all-start.8 = ((f32[32,8,256]{2,1,0:T(8,128)}), f32[32,8,256]{2,1,0:T(8,128)S(1)}, u32[]{:S(2)}, u32[]{:S(2)}) async-start(f32[32,8,256]{2,1,0:T(8,128)} %w2_terms.1), calls=%async_computation.8 | async-start | bytes 524288 | tf_op jit(solution)/shard_map/all_to_all | solution.py:27
  214.7 26.0 %all-to-all-done.8.got = f32[32,8,256]{2,1,0:T(8,128)S(1)} async-done(((f32[32,8,256]{2,1,0:T(8,128)}), f32[32,8,256]{2,1,0:T(8,128)S(1)}, u32[]{:S(2)}, u32[]{:S(2)}) %all-to-all-start.8) | async-done | bytes 262176 | tf_op jit(solution)/shard_map/all_to_all | solution.py:27
  (47 shorter events, 23.3 us)
Async XLA Ops:
  0.6 0.7 copy-start.9
  0.6 1.3 copy-start.10
  2.8 12.8 %copy-start.11 = (f32[2,1024]{1,0:T(2,128)S(1)}, f32[2,1024]{1,0:T(2,128)}, u32[]{:S(2)}) copy-start(f32[2,1024]{1,0:T(2,128)} %param.10) | copy-start | bytes 24580
  2.8 31.2 %all-to-all-start.1 = ((f32[16,4,1152]{2,1,0:T(4,128)}), f32[16,4,1152]{2,1,0:T(4,128)S(1)}, u32[]{:S(2)}, u32[]{:S(2)}) async-start(f32[16,4,1152]{2,1,0:T(4,128)} %broadcast_in_dim.5), calls=%async_computation.1 | async-start | bytes 589824 | tf_op jit(solution)/shard_map/all_to_all | solution.py:27
  33.9 0.8 copy-start.1
  34.8 40.4 %all-to-all-start = ((f32[32,2,1152]{2,1,0:T(2,128)}), f32[32,2,1152]{2,1,0:T(2,128)S(1)}, u32[]{:S(2)}, u32[]{:S(2)}) async-start(f32[32,2,1152]{2,1,0:T(2,128)} %broadcast_in_dim.4), calls=%async_computation | async-start | bytes 589824 | tf_op jit(solution)/shard_map/all_to_all | solution.py:27
  75.2 0.7 copy-start
  78.4 11.1 %all-to-all-start.2 = ((f32[8,32,256]{2,1,0:T(8,128)}), f32[8,32,256]{2,1,0:T(8,128)S(1)}, u32[]{:S(2)}, u32[]{:S(2)}) async-start(f32[8,32,256]{2,1,0:T(8,128)} %get-tuple-element.40), calls=%async_computation.2 | async-start | bytes 524288 | tf_op jit(solution)/shard_map/all_to_all | solution.py:27
  89.5 0.7 copy-start.2
  91.8 12.0 %collective-permute-start = (f32[4,16,256]{2,1,0:T(8,128)}, f32[4,16,256]{2,1,0:T(8,128)S(1)}, u32[]{:S(2)}, u32[]{:S(2)}) collective-permute-start(f32[4,16,256]{2,1,0:T(8,128)} %h1_collect.1.r_3_), channel_id=1, source_target_pairs={{0,256},{256,0},{1,257},{257,1},{2,258},{258,2},{3,259},{259,3},{4... | collective-permute-start | bytes 196616 | tf_op jit(solution)/shard_map/ppermute | solution.py:31
  103.8 0.6 copy-start.6
  120.6 12.3 %all-to-all-start.4 = ((f32[16,16,256]{2,1,0:T(8,128)}), f32[16,16,256]{2,1,0:T(8,128)S(1)}, u32[]{:S(2)}, u32[]{:S(2)}) async-start(f32[16,16,256]{2,1,0:T(8,128)} %w1_terms.1), calls=%async_computation.4 | async-start | bytes 524288 | tf_op jit(solution)/shard_map/all_to_all | solution.py:27
  132.9 0.7 copy-start.4
  135.4 14.7 %collective-permute-start.1 = (f32[4,8,256]{2,1,0:T(8,128)}, f32[4,8,256]{2,1,0:T(8,128)S(1)}, u32[]{:S(2)}, u32[]{:S(2)}) collective-permute-start(f32[4,8,256]{2,1,0:T(8,128)} %w1_collect.1.r_3_), channel_id=1, source_target_pairs={{0,16},{16,0},{1,17},{17,1},{2,18},{18,2},{3,19},{19,3},{4,20},{20... | collective-permute-start | bytes 98312 | tf_op jit(solution)/shard_map/ppermute | solution.py:31
  150.1 0.6 copy-start.8
  181.2 11.9 %collective-permute-start.2 = (f32[4,16,256]{2,1,0:T(8,128)}, f32[4,16,256]{2,1,0:T(8,128)S(1)}, u32[]{:S(2)}, u32[]{:S(2)}) collective-permute-start(f32[4,16,256]{2,1,0:T(8,128)} %h2_collect.1.r_3_), channel_id=1, source_target_pairs={{0,256},{256,0},{1,257},{257,1},{2,258},{258,2},{3,259},{259,3},{4... | collective-permute-start | bytes 196616 | tf_op jit(solution)/shard_map/ppermute | solution.py:31
  193.2 0.6 copy-start.5
  210.0 4.0 %copy-start.7 = (f32[4,8,256]{2,1,0:T(8,128)S(1)}, f32[4,8,256]{2,1,0:T(8,128)}, u32[]{:S(2)}) copy-start(f32[4,8,256]{2,1,0:T(8,128)} %get-tuple-element.49) | copy-start | bytes 98308
  210.0 30.6 %all-to-all-start.8 = ((f32[32,8,256]{2,1,0:T(8,128)}), f32[32,8,256]{2,1,0:T(8,128)S(1)}, u32[]{:S(2)}, u32[]{:S(2)}) async-start(f32[32,8,256]{2,1,0:T(8,128)} %w2_terms.1), calls=%async_computation.8 | async-start | bytes 524288 | tf_op jit(solution)/shard_map/all_to_all | solution.py:27
  240.7 0.7 copy-start.3

commit v2 on v1

--- a/solution.py
+++ b/solution.py
@@ -14,7 +14,6 @@
 FINE = ("z4", "z2", "z1", "core", "zh", "y", "x")
 HALF = ("z2", "z1", "core")
 PLANE = ("y", "x")
-TEX = HALF + ("z4",)
 SMP = PLANE + ("zh",)
 NH = 8
 NP = 16
@@ -65,28 +64,44 @@
         out[q, 16 * j + 8 : 16 * j + 16, :] = lower[8 * q : 8 * q + 8, :]
 
 
+def pack_kernel(blk, w, h, w_msg, h_msg):
+    for d, factor, message in ((0, w, w_msg), (1, h, h_msg)):
+        rows = factor.shape[0]
+        message[:, : NB * BS] = factor[...]
+        lane = lax.broadcasted_iota(jnp.int32, (rows, TAB), 1)
+        message[:, NB * BS :] = jnp.where(lane == 0, blk[d, 0], blk[d, 1]).astype(jnp.float32)
+
+
+def w_pair_kernel(pos, mine, theirs, out):
+    first = pos[3] == 0
+    both = jnp.concatenate(
+        [jnp.where(first, mine[...], theirs[...]), jnp.where(first, theirs[...], mine[...])], axis=0
+    )
+    for q in range(NP):
+        out[q] = both
+
+
+def h_pair_kernel(pos, mine, theirs, out):
+    first = pos[2] == 0
+    low = jnp.where(first, mine[...], theirs[...])
+    high = jnp.where(first, theirs[...], mine[...])
+    both = jnp.concatenate([low[0:2], high[0:2], low[2:4], high[2:4]], axis=0)
+    for q in range(NH):
+        out[q] = both
+
+
 def first_kernel(blk, pos, w0, h0, values, w_slots, h_own, w_own, out):
     for j in range(CAP):
         at = pl.multiple_of(block_of(blk, 0, j) * BS, BS)
-        for q in range(2 * NP):
-            w_slots[j, 2 * q : 2 * q + 2, :] = w0[q, :, pl.ds(at, BS)]
+        for q in range(NP):
+            w_slots[j, 4 * q : 4 * q + 4, :] = w0[q, :, pl.ds(at, BS)]
         at = pl.multiple_of(block_of(blk, 1, j) * BS, BS)
-        rows = []
-        for q in range(NH):
-            for high in range(2):
-                for z in range(2):
-                    rows.append(h0[2 * q + z, 2 * high : 2 * high + 2, pl.ds(at, BS)])
-        upper, lower = sums(
-            w_slots[j], jnp.concatenate(rows, axis=0), values[j * BS : (j + 1) * BS, :], NN, live_of(blk, j)
-        )
+        right = h0[:, :, pl.ds(at, BS)].reshape(RANK, BS)
+        upper, lower = sums(w_slots[j], right, values[j * BS : (j + 1) * BS, :], NN, live_of(blk, j))
         send_h(out, j, upper, lower)
     for b in range(NB):
-        for z in range(2):
-            w_own[b, 2 * z : 2 * z + 2, :] = w0[2 * pos[1] + z, :, b * BS : (b + 1) * BS]
-            for high in range(2):
-                h_own[b, 4 * high + 2 * z : 4 * high + 2 * z + 2, :] = h0[
-                    2 * pos[0] + z, 2 * high : 2 * high + 2, b * BS : (b + 1) * BS
-                ]
+        w_own[b] = w0[pos[1], :, b * BS : (b + 1) * BS]
+        h_own[b] = h0[pos[0], :, b * BS : (b + 1) * BS]
 
 
 def h_slot(got, j):
@@ -154,29 +169,22 @@
         out[:, b * BS : (b + 1) * BS] = mine * acc[b, 0:2, :] / acc[b, 2:4, :]
 
 
-def call(body, scalars, arrays, outs, scratch=(), name=None):
+def call(body, scalars, arrays, outs, scratch=(), last=False, name=None):
     smem = pl.BlockSpec(memory_space=pltpu.SMEM)
     vmem = pl.BlockSpec(memory_space=pltpu.VMEM)
-    shapes = [jax.ShapeDtypeStruct(s, jnp.float32) for s in outs]
+    kind = jax.ShapeDtypeStruct if last else pltpu.VMEM
     return pl.pallas_call(
         body,
         in_specs=[smem] * len(scalars) + [vmem] * len(arrays),
         out_specs=[vmem] * len(outs),
-        out_shape=shapes,
+        out_shape=[kind(s, jnp.float32) for s in outs],
         scratch_shapes=[pltpu.VMEM(s, jnp.float32) for s in scratch],
         name=name,
-    )(*scalars, *arrays)
-
-
-def with_list(factor, listing, copies):
-    listed = jnp.zeros((factor.shape[0], TAB), jnp.float32)
-    listed = listed.at[:, :CAP].set(listing.astype(jnp.float32)[None, :])
-    message = jnp.concatenate([factor, listed], axis=1)
-    return jnp.broadcast_to(message, (copies, *message.shape))
+    )(*scalars, *(pltpu.with_memory_space_constraint(a, pltpu.VMEM) for a in arrays))
 
 
 def table_of(got):
-    return got[:, 0, NB * BS : NB * BS + CAP].astype(jnp.int32).reshape(-1)
+    return got[:, 0:4:2, NB * BS : NB * BS + CAP].astype(jnp.int32).reshape(-1)
 
 
 def per_device(blocks, observed, w_factor, h_factor):
@@ -186,8 +194,15 @@
     plane = lax.axis_index(PLANE)
     pos = jnp.stack([half, plane, lax.axis_index("z4"), lax.axis_index("zh")]).astype(jnp.int32)
 
-    h_got0 = exchange(with_list(h_factor, blk[1], 2 * NH), TEX)
-    w_got0 = exchange(with_list(w_factor, blk[0], 2 * NP), SMP)
+    w_msg, h_msg = call(
+        pack_kernel, (blk,), (w_factor, h_factor), [(2, NB * BS + TAB), (4, NB * BS + TAB)], name="pack"
+    )
+    w_other = swap(w_msg, "zh")
+    h_other = swap(h_msg, "z4")
+    (h_pair,) = call(h_pair_kernel, (pos,), (h_msg, h_other), [(NH, 8, NB * BS + TAB)], name="h_pair")
+    h_got0 = exchange(h_pair, HALF)
+    (w_pair,) = call(w_pair_kernel, (pos,), (w_msg, w_other), [(NP, 4, NB * BS + TAB)], name="w_pair")
+    w_got0 = exchange(w_pair, PLANE)
     cols = table_of(h_got0)
     rows = table_of(w_got0)
 
@@ -238,7 +253,7 @@
     (sent,) = call(w_terms_kernel, (blk,), (h_got, w_slots, values), [(2 * NP, 8, BS)], name="w2_terms")
     got = exchange(sent, SMP)
     (w_final,) = call(
-        last_kernel, (rows, pos), (w_own, got), [(2, NB * BS)], scratch=[(NB, 4, BS)], name="w2_update"
+        last_kernel, (rows, pos), (w_own, got), [(2, NB * BS)], scratch=[(NB, 4, BS)], last=True, name="w2_update"
     )
     z = lax.axis_index("z4")
     h_rows = h_own.reshape(NB, 2, 2, 2, BS)

time: 245 us -> 216 us (0.88)
  waiting for transfers between devices: 114 us -> 55.9 us
  starting transfers between devices: 46.2 us -> 80.3 us
  blocking collectives: 49.3 us -> 57.9 us
  Pallas kernels: 21.6 us -> 15.9 us
  local copies, waits for them, and re-layouts: 8.14 us -> 3.42 us
  other arithmetic: 3.47 us -> 0.62 us
    all_to_all x5 -> x4, waiting for transfers between devices: 84.7 us -> 40.8 us  [exchange(): return lax.all_to_all(x, axes, split_axis=0, concat_axis=0, tiled=True)]
    ppermute x3 -> x5, starting transfers between devices: 9.42 us -> 49.7 us  [swap(): return lax.ppermute(x, axis, [(0, 1), (1, 0)])]
    ppermute x3 -> x5, waiting for transfers between devices: 29.2 us -> 15.1 us  [swap(): return lax.ppermute(x, axis, [(0, 1), (1, 0)])]
    all_to_all x4 -> x5, blocking collectives: 49.3 us -> 57.9 us  [exchange(): return lax.all_to_all(x, axes, split_axis=0, concat_axis=0, tiled=True)]
    all_to_all x5 -> x4, starting transfers between devices: 36.7 us -> 30.6 us  [exchange(): return lax.all_to_all(x, axes, split_axis=0, concat_axis=0, tiled=True)]
    pallas_call x11 -> x14, Pallas kernels: 21.6 us -> 15.9 us  [call(): pl.pallas_call(body, in_specs=[smem] * len(scalars) + [vmem] * len(arrays...]
    unnamed x26 -> x8, local copies, waits for them, and re-layouts: 5.31 us -> 2.03 us
  transfers between devices with their start and end apart: 8 -> 9, of which waited for: 8 -> 8; matrix products, arithmetic and copies ran while one was open for 2% -> 1% of each run, Pallas kernels for 0% -> 0%
where the time goes in v2:
time: 216 us; the launch traced here: 215 us
  starting transfers between devices  80.3 us (37%)
  blocking collectives  57.9 us (27%)
  waiting for transfers between devices  55.9 us (26%)
  Pallas kernels  15.9 us (7%)
  local copies, waits for them, and re-layouts  3.42 us (2%)
    all_to_all x5, blocking collectives, exchange(): return lax.all_to_all(x, axes, split_axis=0, concat_axis=0, tiled=True)  57.9 us
    ppermute x5, starting transfers between devices, swap(): return lax.ppermute(x, axis, [(0, 1), (1, 0)])  49.7 us
    all_to_all x4, waiting for transfers between devices, exchange(): return lax.all_to_all(x, axes, split_axis=0, concat_axis=0, tiled=True)  40.8 us
    all_to_all x4, starting transfers between devices, exchange(): return lax.all_to_all(x, axes, split_axis=0, concat_axis=0, tiled=True)  30.6 us
    pallas_call x14, Pallas kernels, call(): pl.pallas_call(body, in_specs=[smem] * len(scalars) + [vmem] * len(arrays...  15.9 us
    ppermute x5, waiting for transfers between devices, swap(): return lax.ppermute(x, axis, [(0, 1), (1, 0)])  15.1 us
  transfers between devices with their start and end apart: 9, of which 8 were waited for; matrix products, arithmetic and copies ran while one was open for 1% of the time, Pallas kernels for 0%

profile of v2, /device:TPU:32, one launch (start us, length us, event | category | flops | bytes accessed | tf_op | source)
XLA Modules:
  0.0 214.9 jit_solution(8340166842964337415)
XLA Ops:
  2.7 14.8 %collective-permute-start = (f32[2,1152]{1,0:T(2,128)S(1)}, f32[2,1152]{1,0:T(2,128)S(1)}, u32[]{:S(2)}, u32[]{:S(2)}) collective-permute-start(f32[2,1152]{1,0:T(2,128)S(1)} %get-tuple-element.16.mine), channel_id=1, source_target_pairs={{0,16},{16,0},{1,17},{17,1},{2,18},{18,2},{3,19},{19,3},{4,20},{20... | collective-permute-start | bytes 27656 | tf_op jit(solution)/shard_map/ppermute | solution.py:30
  20.6 7.0 %all-to-all-start = ((f32[16,4,1152]{2,1,0:T(4,128)}), f32[16,4,1152]{2,1,0:T(4,128)S(1)}, u32[]{:S(2)}, u32[]{:S(2)}) async-start(f32[16,4,1152]{2,1,0:T(4,128)} %w_pair.1), calls=%async_computation | async-start | bytes 589824 | tf_op jit(solution)/shard_map/all_to_all | solution.py:26
  27.7 7.0 %collective-permute-start.1 = (f32[4,1152]{1,0:T(4,128)S(1)}, f32[4,1152]{1,0:T(4,128)S(1)}, u32[]{:S(2)}, u32[]{:S(2)}) collective-permute-start(f32[4,1152]{1,0:T(4,128)S(1)} %get-tuple-element.17.mine), channel_id=1, source_target_pairs={{0,256},{256,0},{1,257},{257,1},{2,258},{258,2},{3,259},{259,3},{4... | collective-permute-start | bytes 55304 | tf_op jit(solution)/shard_map/ppermute | solution.py:30
  34.7 2.7 %collective-permute-done.1.theirs = f32[4,1152]{1,0:T(4,128)S(1)} collective-permute-done((f32[4,1152]{1,0:T(4,128)S(1)}, f32[4,1152]{1,0:T(4,128)S(1)}, u32[]{:S(2)}, u32[]{:S(2)}) %collective-permute-start.1) | collective-permute-done | bytes 18464 | tf_op jit(solution)/shard_map/ppermute | solution.py:30
  38.1 13.7 %all_to_all.45.h0 = f32[8,8,1152]{2,1,0:T(8,128)S(1)} all-to-all(f32[8,8,1152]{2,1,0:T(8,128)S(1)} %h_pair.1), channel_id=1, replica_groups=mesh['z4'=2,'z2'=2,'z1'=2,'core'=2,'zh'=2,'y'=4,'x'=4] {'z2','z1','core'}, dimensions={0} | all-to-all | bytes 589824 | tf_op jit(solution)/shard_map/all_to_all | solution.py:26
  51.8 2.0 h1_terms.1
  53.8 4.9 %all-to-all-start.2 = ((f32[8,32,256]{2,1,0:T(8,128)}), f32[8,32,256]{2,1,0:T(8,128)S(1)}, u32[]{:S(2)}, u32[]{:S(2)}) async-start(f32[8,32,256]{2,1,0:T(8,128)} %get-tuple-element.20), calls=%async_computation.2 | async-start | bytes 524288 | tf_op jit(solution)/shard_map/all_to_all | solution.py:26
  59.3 7.1 %all-to-all-done.2.r_2_ = f32[8,32,256]{2,1,0:T(8,128)S(1)} async-done(((f32[8,32,256]{2,1,0:T(8,128)}), f32[8,32,256]{2,1,0:T(8,128)S(1)}, u32[]{:S(2)}, u32[]{:S(2)}) %all-to-all-start.2) | async-done | bytes 262176 | tf_op jit(solution)/shard_map/all_to_all | solution.py:26
  67.2 7.8 %collective-permute-start.2 = (f32[4,16,256]{2,1,0:T(8,128)S(1)}, f32[4,16,256]{2,1,0:T(8,128)S(1)}, u32[]{:S(2)}, u32[]{:S(2)}) collective-permute-start(f32[4,16,256]{2,1,0:T(8,128)S(1)} %h1_collect.1.r_3_), channel_id=1, source_target_pairs={{0,256},{256,0},{1,257},{257,1},{2,258},{258,2},{3,259},{259,3},{4... | collective-permute-start | bytes 196616 | tf_op jit(solution)/shard_map/ppermute | solution.py:30
  75.0 3.9 %collective-permute-done.2.r_4_ = f32[4,16,256]{2,1,0:T(8,128)S(1)} collective-permute-done((f32[4,16,256]{2,1,0:T(8,128)S(1)}, f32[4,16,256]{2,1,0:T(8,128)S(1)}, u32[]{:S(2)}, u32[]{:S(2)}) %collective-permute-start.2) | collective-permute-done | bytes 65568 | tf_op jit(solution)/shard_map/ppermute | solution.py:30
  79.7 11.0 %all_to_all.46.h_got = f32[8,16,256]{2,1,0:T(8,128)S(1)} all-to-all(f32[8,16,256]{2,1,0:T(8,128)S(1)} %get-tuple-element.21), channel_id=1, replica_groups=mesh['z4'=2,'z2'=2,'z1'=2,'core'=2,'zh'=2,'y'=4,'x'=4] {'z2','z1','core'}, dimensions={0} | all-to-all | bytes 262144 | tf_op jit(solution)/shard_map/all_to_all | solution.py:26
  90.7 1.9 w1_terms.1
  92.7 7.2 %all-to-all-start.4 = ((f32[16,16,256]{2,1,0:T(8,128)}), f32[16,16,256]{2,1,0:T(8,128)S(1)}, u32[]{:S(2)}, u32[]{:S(2)}) async-start(f32[16,16,256]{2,1,0:T(8,128)} %w1_terms.1), calls=%async_computation.4 | async-start | bytes 524288 | tf_op jit(solution)/shard_map/all_to_all | solution.py:26
  100.6 7.9 %all-to-all-done.4.r_2_ = f32[16,16,256]{2,1,0:T(8,128)S(1)} async-done(((f32[16,16,256]{2,1,0:T(8,128)}), f32[16,16,256]{2,1,0:T(8,128)S(1)}, u32[]{:S(2)}, u32[]{:S(2)}) %all-to-all-start.4) | async-done | bytes 262176 | tf_op jit(solution)/shard_map/all_to_all | solution.py:26
  109.4 11.2 %collective-permute-start.3 = (f32[4,8,256]{2,1,0:T(8,128)S(1)}, f32[4,8,256]{2,1,0:T(8,128)S(1)}, u32[]{:S(2)}, u32[]{:S(2)}) collective-permute-start(f32[4,8,256]{2,1,0:T(8,128)S(1)} %w1_collect.1.r_3_), channel_id=1, source_target_pairs={{0,16},{16,0},{1,17},{17,1},{2,18},{18,2},{3,19},{19,3},{4,20},{20... | collective-permute-start | bytes 98312 | tf_op jit(solution)/shard_map/ppermute | solution.py:30
  120.6 3.5 %collective-permute-done.3.r_4_ = f32[4,8,256]{2,1,0:T(8,128)S(1)} collective-permute-done((f32[4,8,256]{2,1,0:T(8,128)S(1)}, f32[4,8,256]{2,1,0:T(8,128)S(1)}, u32[]{:S(2)}, u32[]{:S(2)}) %collective-permute-start.3) | collective-permute-done | bytes 32800 | tf_op jit(solution)/shard_map/ppermute | solution.py:30
  124.9 10.8 %all_to_all.47.w_got = f32[16,8,256]{2,1,0:T(8,128)S(1)} all-to-all(f32[16,8,256]{2,1,0:T(8,128)S(1)} %get-tuple-element.25), channel_id=1, replica_groups=mesh['z4'=2,'z2'=2,'z1'=2,'core'=2,'zh'=2,'y'=4,'x'=4] {'y','x'}, dimensions={0} | all-to-all | bytes 262144 | tf_op jit(solution)/shard_map/all_to_all | solution.py:26
  136.9 11.3 %all_to_all.48.r_2_ = f32[8,32,256]{2,1,0:T(8,128)S(1)} all-to-all(f32[8,32,256]{2,1,0:T(8,128)S(1)} %get-tuple-element.26), channel_id=1, replica_groups=mesh['z4'=2,'z2'=2,'z1'=2,'core'=2,'zh'=2,'y'=4,'x'=4] {'z2','z1','core'}, dimensions={0} | all-to-all | bytes 524288 | tf_op jit(solution)/shard_map/all_to_all | solution.py:26
  148.9 8.8 %collective-permute-start.4 = (f32[4,16,256]{2,1,0:T(8,128)S(1)}, f32[4,16,256]{2,1,0:T(8,128)S(1)}, u32[]{:S(2)}, u32[]{:S(2)}) collective-permute-start(f32[4,16,256]{2,1,0:T(8,128)S(1)} %h2_collect.1.r_3_), channel_id=1, source_target_pairs={{0,256},{256,0},{1,257},{257,1},{2,258},{258,2},{3,259},{259,3},{4... | collective-permute-start | bytes 196616 | tf_op jit(solution)/shard_map/ppermute | solution.py:30
  157.8 4.0 %collective-permute-done.4.r_4_ = f32[4,16,256]{2,1,0:T(8,128)S(1)} collective-permute-done((f32[4,16,256]{2,1,0:T(8,128)S(1)}, f32[4,16,256]{2,1,0:T(8,128)S(1)}, u32[]{:S(2)}, u32[]{:S(2)}) %collective-permute-start.4) | collective-permute-done | bytes 65568 | tf_op jit(solution)/shard_map/ppermute | solution.py:30
  162.5 11.0 %all_to_all.49.h_got = f32[8,16,256]{2,1,0:T(8,128)S(1)} all-to-all(f32[8,16,256]{2,1,0:T(8,128)S(1)} %get-tuple-element.27), channel_id=1, replica_groups=mesh['z4'=2,'z2'=2,'z1'=2,'core'=2,'zh'=2,'y'=4,'x'=4] {'z2','z1','core'}, dimensions={0} | all-to-all | bytes 262144 | tf_op jit(solution)/shard_map/all_to_all | solution.py:26
  173.5 2.0 w2_terms.1
  175.4 11.5 %all-to-all-start.8 = ((f32[32,8,256]{2,1,0:T(8,128)}), f32[32,8,256]{2,1,0:T(8,128)S(1)}, u32[]{:S(2)}, u32[]{:S(2)}) async-start(f32[32,8,256]{2,1,0:T(8,128)} %w2_terms.1), calls=%async_computation.8 | async-start | bytes 524288 | tf_op jit(solution)/shard_map/all_to_all | solution.py:26
  187.6 25.7 %all-to-all-done.8.got = f32[32,8,256]{2,1,0:T(8,128)S(1)} async-done(((f32[32,8,256]{2,1,0:T(8,128)}), f32[32,8,256]{2,1,0:T(8,128)S(1)}, u32[]{:S(2)}, u32[]{:S(2)}) %all-to-all-start.8) | async-done | bytes 262176 | tf_op jit(solution)/shard_map/all_to_all | solution.py:26
  (30 shorter events, 15.2 us)
Async XLA Ops:
  0.6 0.7 copy-start.1
  1.3 0.7 copy-start.2
  2.7 16.5 %collective-permute-start = (f32[2,1152]{1,0:T(2,128)S(1)}, f32[2,1152]{1,0:T(2,128)S(1)}, u32[]{:S(2)}, u32[]{:S(2)}) collective-permute-start(f32[2,1152]{1,0:T(2,128)S(1)} %get-tuple-element.16.mine), channel_id=1, source_target_pairs={{0,16},{16,0},{1,17},{17,1},{2,18},{18,2},{3,19},{19,3},{4,20},{20... | collective-permute-start | bytes 27656 | tf_op jit(solution)/shard_map/ppermute | solution.py:30
  20.6 17.4 %all-to-all-start = ((f32[16,4,1152]{2,1,0:T(4,128)}), f32[16,4,1152]{2,1,0:T(4,128)S(1)}, u32[]{:S(2)}, u32[]{:S(2)}) async-start(f32[16,4,1152]{2,1,0:T(4,128)} %w_pair.1), calls=%async_computation | async-start | bytes 589824 | tf_op jit(solution)/shard_map/all_to_all | solution.py:26
  27.7 24.2 %copy-start = (f32[1,1,512,256]{3,2,1,0:T(8,128)S(1)}, f32[1,1,512,256]{3,2,1,0:T(8,128)}, u32[]{:S(2)}) copy-start(f32[1,1,512,256]{3,2,1,0:T(8,128)} %param.5) | copy-start | bytes 1572868
  27.7 9.7 %collective-permute-start.1 = (f32[4,1152]{1,0:T(4,128)S(1)}, f32[4,1152]{1,0:T(4,128)S(1)}, u32[]{:S(2)}, u32[]{:S(2)}) collective-permute-start(f32[4,1152]{1,0:T(4,128)S(1)} %get-tuple-element.17.mine), channel_id=1, source_target_pairs={{0,256},{256,0},{1,257},{257,1},{2,258},{258,2},{3,259},{259,3},{4... | collective-permute-start | bytes 55304 | tf_op jit(solution)/shard_map/ppermute | solution.py:30
  53.8 12.7 %all-to-all-start.2 = ((f32[8,32,256]{2,1,0:T(8,128)}), f32[8,32,256]{2,1,0:T(8,128)S(1)}, u32[]{:S(2)}, u32[]{:S(2)}) async-start(f32[8,32,256]{2,1,0:T(8,128)} %get-tuple-element.20), calls=%async_computation.2 | async-start | bytes 524288 | tf_op jit(solution)/shard_map/all_to_all | solution.py:26
  67.2 11.8 %collective-permute-start.2 = (f32[4,16,256]{2,1,0:T(8,128)S(1)}, f32[4,16,256]{2,1,0:T(8,128)S(1)}, u32[]{:S(2)}, u32[]{:S(2)}) collective-permute-start(f32[4,16,256]{2,1,0:T(8,128)S(1)} %h1_collect.1.r_3_), channel_id=1, source_target_pairs={{0,256},{256,0},{1,257},{257,1},{2,258},{258,2},{3,259},{259,3},{4... | collective-permute-start | bytes 196616 | tf_op jit(solution)/shard_map/ppermute | solution.py:30
  92.7 15.9 %all-to-all-start.4 = ((f32[16,16,256]{2,1,0:T(8,128)}), f32[16,16,256]{2,1,0:T(8,128)S(1)}, u32[]{:S(2)}, u32[]{:S(2)}) async-start(f32[16,16,256]{2,1,0:T(8,128)} %w1_terms.1), calls=%async_computation.4 | async-start | bytes 524288 | tf_op jit(solution)/shard_map/all_to_all | solution.py:26
  109.4 14.7 %collective-permute-start.3 = (f32[4,8,256]{2,1,0:T(8,128)S(1)}, f32[4,8,256]{2,1,0:T(8,128)S(1)}, u32[]{:S(2)}, u32[]{:S(2)}) collective-permute-start(f32[4,8,256]{2,1,0:T(8,128)S(1)} %w1_collect.1.r_3_), channel_id=1, source_target_pairs={{0,16},{16,0},{1,17},{17,1},{2,18},{18,2},{3,19},{19,3},{4,20},{20... | collective-permute-start | bytes 98312 | tf_op jit(solution)/shard_map/ppermute | solution.py:30
  148.9 12.8 %collective-permute-start.4 = (f32[4,16,256]{2,1,0:T(8,128)S(1)}, f32[4,16,256]{2,1,0:T(8,128)S(1)}, u32[]{:S(2)}, u32[]{:S(2)}) collective-permute-start(f32[4,16,256]{2,1,0:T(8,128)S(1)} %h2_collect.1.r_3_), channel_id=1, source_target_pairs={{0,256},{256,0},{1,257},{257,1},{2,258},{258,2},{3,259},{259,3},{4... | collective-permute-start | bytes 196616 | tf_op jit(solution)/shard_map/ppermute | solution.py:30
  175.4 37.9 %all-to-all-start.8 = ((f32[32,8,256]{2,1,0:T(8,128)}), f32[32,8,256]{2,1,0:T(8,128)S(1)}, u32[]{:S(2)}, u32[]{:S(2)}) async-start(f32[32,8,256]{2,1,0:T(8,128)} %w2_terms.1), calls=%async_computation.8 | async-start | bytes 524288 | tf_op jit(solution)/shard_map/all_to_all | solution.py:26

commit v3 on v2

v3 whole, which is shorter than its diff:
```python
import jax
import jax.numpy as jnp
from jax import lax
from jax.experimental import pallas as pl
from jax.experimental.pallas import tpu as pltpu
from jax.sharding import Mesh, PartitionSpec as P


RANK = 64
BS = 256
CAP = 2
NB = 4
TAB = 128

FINE = ("z4", "z2", "z1", "core", "zh", "y", "x")
HALF = ("z2", "z1", "core")
PLANE = ("y", "x")
NH = 8
NP = 16

NN = (((1,), (0,)), ((), ()))
NT = (((1,), (1,)), ((), ()))


def exchange(x, axes):
    return lax.all_to_all(x, axes, split_axis=0, concat_axis=0, tiled=True)


def swap(x, axis):
    return lax.ppermute(x, axis, [(0, 1), (1, 0)])


def halves(x):
    hi = x.astype(jnp.bfloat16)
    lo = (x - hi.astype(jnp.float32)).astype(jnp.bfloat16)
    return hi, lo


def product(a, b, dims):
    dot = lambda x, y: lax.dot_general(x, y, dims, preferred_element_type=jnp.float32)
    return dot(a[0], b[0]) + (dot(a[0], b[1]) + dot(a[1], b[0]))


def sums(left, right, values, dims, live):
    whole = halves(left)
    left = halves(left * live)
    upper = product(left, halves(values), dims)
    gram = product(left, whole, NT)
    lower = product(halves(gram), halves(right), NN)
    return upper, lower


def live_of(blk, j):
    return jnp.where(blk[0, j] >= 0, 1.0, 0.0).astype(jnp.float32)


def block_of(blk, d, j):
    return jnp.maximum(blk[d, j], 0)


def send_h(out, j, upper, lower):
    for q in range(NH):
        out[q, 16 * j : 16 * j + 8, :] = upper[8 * q : 8 * q + 8, :]
        out[q, 16 * j + 8 : 16 * j + 16, :] = lower[8 * q : 8 * q + 8, :]


def with_list(rows, blk, d, lists):
    lane = lax.broadcasted_iota(jnp.int32, (rows.shape[0], TAB), 1)
    lists[:, : NB * BS] = rows
    lists[:, NB * BS :] = jnp.where(lane == 0, blk[d, 0], blk[d, 1]).astype(jnp.float32)


def w_pair_kernel(blk, mine, theirs, out, message):
    first = lax.axis_index("zh") == 0
    low = jnp.where(first, mine[...], theirs[...])
    high = jnp.where(first, theirs[...], mine[...])
    with_list(jnp.concatenate([low, high], axis=0), blk, 0, message)
    for q in range(NP):
        out[q] = message[...]


def h_pair_kernel(blk, mine, theirs, out, message):
    first = lax.axis_index("z4") == 0
    low = jnp.where(first, mine[...], theirs[...])
    high = jnp.where(first, theirs[...], mine[...])
    with_list(jnp.concatenate([low[0:2], high[0:2], low[2:4], high[2:4]], axis=0), blk, 1, message)
    for q in range(NH):
        out[q] = message[...]


def first_kernel(blk, w0, h0, values, w_slots, h_own, w_own, out, rows, cols):
    for j in range(CAP):
        at = pl.multiple_of(block_of(blk, 0, j) * BS, BS)
        for q in range(NP):
            w_slots[j, 4 * q : 4 * q + 4, :] = w0[q, :, pl.ds(at, BS)]
        at = pl.multiple_of(block_of(blk, 1, j) * BS, BS)
        right = h0[:, :, pl.ds(at, BS)].reshape(RANK, BS)
        upper, lower = sums(w_slots[j], right, values[j * BS : (j + 1) * BS, :], NN, live_of(blk, j))
        send_h(out, j, upper, lower)
    half = lax.axis_index(HALF)
    plane = lax.axis_index(PLANE)
    for b in range(NB):
        w_own[b] = w0[plane, :, b * BS : (b + 1) * BS]
        h_own[b] = h0[half, :, b * BS : (b + 1) * BS]
    for got, table in ((w0, rows), (h0, cols)):
        for q in range(got.shape[0]):
            for j in range(CAP):
                at = NB * BS + j
                table[q * CAP + j] = jnp.maximum(got[q, 0:1, at : at + 1].astype(jnp.int32)[0, 0], 0)


def h_slot(got, j):
    return got[:, 8 * j : 8 * j + 8, :].reshape(RANK, BS)


def w_slot(got, j):
    return jnp.concatenate([got[q, 4 * j : 4 * j + 4, :] for q in range(NP)], axis=0)


def w_terms_kernel(blk, h_got, w_slots, values, out):
    share = out.shape[1] // (2 * CAP)
    for j in range(CAP):
        upper, lower = sums(h_slot(h_got, j), w_slots[j], values[j * BS : (j + 1) * BS, :], NT, live_of(blk, j))
        for q in range(out.shape[0]):
            at = 2 * share * j
            out[q, at : at + share, :] = upper[share * q : share * (q + 1), :]
            out[q, at + share : at + 2 * share, :] = lower[share * q : share * (q + 1), :]


def h_terms_kernel(blk, w_got, h_got, values, w_slots, out):
    for j in range(CAP):
        w_slots[j] = w_slot(w_got, j)
        upper, lower = sums(w_slots[j], h_slot(h_got, j), values[j * BS : (j + 1) * BS, :], NN, live_of(blk, j))
        send_h(out, j, upper, lower)


def collect_kernel(table, got, out):
    rows = out.shape[1]
    out[...] = jnp.zeros(out.shape, out.dtype)
    for q in range(got.shape[0]):
        for j in range(CAP):
            b = table[q * CAP + j]
            out[b] = out[b] + got[q, rows * j : rows * (j + 1), :]


def updated(own, mine, theirs):
    rows = own.shape[1]
    upper = mine[:, :rows, :] + theirs[:, :rows, :]
    lower = mine[:, rows:, :] + theirs[:, rows:, :]
    return own[...] * upper / lower


def update_kernel(table, own, mine, theirs, new, out):
    rows = own.shape[1]
    new[...] = updated(own, mine, theirs)
    for q in range(out.shape[0]):
        for j in range(CAP):
            out[q, rows * j : rows * (j + 1), :] = new[table[q * CAP + j]]


def last_h_kernel(table, own, mine, theirs, final, out, new):
    update_kernel(table, own, mine, theirs, new, out)
    first = lax.axis_index("z4") == 0
    for b in range(NB):
        for high in range(2):
            pair = new[b, 4 * high : 4 * high + 4, :]
            final[2 * high : 2 * high + 2, b * BS : (b + 1) * BS] = jnp.where(first, pair[0:2], pair[2:4])


def last_w_kernel(own, mine, theirs, final, new):
    new[...] = updated(own, mine, theirs)
    first = lax.axis_index("zh") == 0
    for b in range(NB):
        final[:, b * BS : (b + 1) * BS] = jnp.where(first, new[b, 0:2, :], new[b, 2:4, :])


def call(body, scalars, arrays, outs, tables=(), scratch=()):
    smem = pl.BlockSpec(memory_space=pltpu.SMEM)
    vmem = pl.BlockSpec(memory_space=pltpu.VMEM)
    return pl.pallas_call(
        body,
        in_specs=[smem] * len(scalars) + [vmem] * len(arrays),
        out_specs=[vmem] * len(outs) + [smem] * len(tables),
        out_shape=[pltpu.VMEM(s, jnp.float32) for s in outs] + [pltpu.SMEM(s, jnp.int32) for s in tables],
        scratch_shapes=[pltpu.VMEM(s, jnp.float32) for s in scratch],
    )(
        *(pltpu.with_memory_space_constraint(a, pltpu.SMEM) for a in scalars),
        *(pltpu.with_memory_space_constraint(a, pltpu.VMEM) for a in arrays),
    )


def per_device(blocks, observed, w_factor, h_factor):
    blk = blocks[0, 0]
    values = observed[0, 0]
    wide = NB * BS + TAB

    w_other = swap(w_factor, "zh")
    h_other = swap(h_factor, "z4")
    (h_pair,) = call(h_pair_kernel, (blk,), (h_factor, h_other), [(NH, 8, wide)], scratch=[(8, wide)])
    h_got0 = exchange(h_pair, HALF)
    w_other, h_got0 = lax.optimization_barrier((w_other, h_got0))
    (w_pair,) = call(w_pair_kernel, (blk,), (w_factor, w_other), [(NP, 4, wide)], scratch=[(4, wide)])
    w_got0 = exchange(w_pair, PLANE)

    w_slots, h_own, w_own, sent, rows, cols = call(
        first_kernel,
        (blk,),
        (w_got0, h_got0, values),
        [(CAP, RANK, BS), (NB, 8, BS), (NB, 4, BS), (NH, 32, BS)],
        tables=[(NP * CAP,), (NH * CAP,)],
    )
    got = exchange(sent, HALF)
    (mine,) = call(collect_kernel, (cols,), (got,), [(NB, 16, BS)])
    theirs = swap(mine, "z4")
    h_own, out = call(update_kernel, (cols,), (h_own, mine, theirs), [(NB, 8, BS), (NH, 16, BS)])
    h_got = exchange(out, HALF)

    (sent,) = call(w_terms_kernel, (blk,), (h_got, w_slots, values), [(NP, 16, BS)])
    got = exchange(sent, PLANE)
    (mine,) = call(collect_kernel, (rows,), (got,), [(NB, 8, BS)])
    theirs = swap(mine, "zh")
    w_own, out = call(update_kernel, (rows,), (w_own, mine, theirs), [(NB, 4, BS), (NP, 8, BS)])
    w_got = exchange(out, PLANE)

    w_slots, sent = call(h_terms_kernel, (blk,), (w_got, h_got, values), [(CAP, RANK, BS), (NH, 32, BS)])
    got = exchange(sent, HALF)
    (mine,) = call(collect_kernel, (cols,), (got,), [(NB, 16, BS)])
    theirs = swap(mine, "z4")
    h_final, out = call(
        last_h_kernel, (cols,), (h_own, mine, theirs), [(4, NB * BS), (NH, 16, BS)], scratch=[(NB, 8, BS)]
    )
    h_got = exchange(out, HALF)

    (sent,) = call(w_terms_kernel, (blk,), (h_got, w_slots, values), [(NP, 16, BS)])
    got = exchange(sent, PLANE)
    (mine,) = call(collect_kernel, (rows,), (got,), [(NB, 8, BS)])
    theirs = swap(mine, "zh")
    (w_final,) = call(last_w_kernel, (), (w_own, mine, theirs), [(2, NB * BS)], scratch=[(NB, 4, BS)])
    return w_final, h_final


def solution(mesh):
    fine = Mesh(mesh.devices.reshape(2, 2, 2, 2, 2, 4, 4), FINE)
    tex = ("z4",) + HALF
    smp = ("zh",) + PLANE
    in_specs = (P(tex, smp, None, None), P(tex, smp, None, None), P(smp, tex), P(tex, smp))
    out_specs = (P(smp, tex), P(tex, smp))
    return jax.shard_map(per_device, mesh=fine, in_specs=in_specs, out_specs=out_specs, check_vma=False)
```

time: 216 us -> 192 us (0.89)
  the two profiles are of different devices: /device:TPU:32 before, /device:TPU:128 now
where the time goes in v3:
time: 192 us; the launch traced here: 191 us
  blocking collectives  102 us (53%)
  starting transfers between devices  43.3 us (23%)
  waiting for transfers between devices  35.5 us (18%)
  Pallas kernels  7.66 us (4%)
  local copies, waits for them, and re-layouts  1.94 us (1%)
    all_to_all x8, blocking collectives, exchange(): return lax.all_to_all(x, axes, split_axis=0, concat_axis=0, tiled=True)  102 us
    ppermute x6, starting transfers between devices, swap(): return lax.ppermute(x, axis, [(0, 1), (1, 0)])  37.2 us
    ppermute x6, waiting for transfers between devices, swap(): return lax.ppermute(x, axis, [(0, 1), (1, 0)])  35.5 us
    pallas_call x14, Pallas kernels, call(): pl.pallas_call(body, in_specs=[smem] * len(scalars) + [vmem] * len(arrays...  7.66 us
    all_to_all x1, starting transfers between devices, exchange(): return lax.all_to_all(x, axes, split_axis=0, concat_axis=0, tiled=True)  6.03 us
  transfers between devices with their start and end apart: 7, of which 6 were waited for; matrix products, arithmetic and copies ran while one was open for 0% of the time, Pallas kernels for 0%

profile of v3, /device:TPU:128, one launch (start us, length us, event | category | flops | bytes accessed | tf_op | source)
XLA Modules:
  0.0 191.0 jit_solution(1156762443824892091)
XLA Ops:
  0.6 6.0 %collective-permute-start.1 = (f32[4,1024]{1,0:T(4,128)}, f32[4,1024]{1,0:T(4,128)S(1)}, u32[]{:S(2)}, u32[]{:S(2)}) collective-permute-start(f32[4,1024]{1,0:T(4,128)} %mine.2), channel_id=1, source_target_pairs={{0,256},{256,0},{1,257},{257,1},{2,258},{258,2},{3,259},{259,3},{4... | collective-permute-start | bytes 49160 | tf_op jit(solution)/shard_map/ppermute | solution.py:30
  6.6 3.7 %collective-permute-done.1.theirs = f32[4,1024]{1,0:T(4,128)S(1)} collective-permute-done((f32[4,1024]{1,0:T(4,128)}, f32[4,1024]{1,0:T(4,128)S(1)}, u32[]{:S(2)}, u32[]{:S(2)}) %collective-permute-start.1) | collective-permute-done | bytes 16416 | tf_op jit(solution)/shard_map/ppermute | solution.py:30
  11.1 1.4 shard_map.59
  12.5 6.0 %all-to-all-start = ((f32[8,8,1152]{2,1,0:T(8,128)}), f32[8,8,1152]{2,1,0:T(8,128)S(1)}, u32[]{:S(2)}, u32[]{:S(2)}) async-start(f32[8,8,1152]{2,1,0:T(8,128)} %shard_map.59), calls=%async_computation | async-start | bytes 589824 | tf_op jit(solution)/shard_map/all_to_all | solution.py:26
  18.6 8.6 %collective-permute-start = (f32[2,1024]{1,0:T(2,128)S(1)}, f32[2,1024]{1,0:T(2,128)S(1)}, u32[]{:S(2)}, u32[]{:S(2)}) collective-permute-start(f32[2,1024]{1,0:T(2,128)S(1)} %copy-done.2), channel_id=1, source_target_pairs={{0,16},{16,0},{1,17},{17,1},{2,18},{18,2},{3,19},{19,3},{4,20},{20... | collective-permute-start | bytes 24584 | tf_op jit(solution)/shard_map/ppermute | solution.py:30
  27.2 5.8 %collective-permute-done.theirs = f32[2,1024]{1,0:T(2,128)S(1)} collective-permute-done((f32[2,1024]{1,0:T(2,128)S(1)}, f32[2,1024]{1,0:T(2,128)S(1)}, u32[]{:S(2)}, u32[]{:S(2)}) %collective-permute-start) | collective-permute-done | bytes 8224 | tf_op jit(solution)/shard_map/ppermute | solution.py:30
  33.7 15.7 %all_to_all.45.w0 = f32[16,4,1152]{2,1,0:T(4,128)S(1)} all-to-all(f32[16,4,1152]{2,1,0:T(4,128)S(1)} %shard_map.60), channel_id=1, replica_groups=mesh['z4'=2,'z2'=2,'z1'=2,'core'=2,'zh'=2,'y'=4,'x'=4] {'y','x'}, dimensions={0} | all-to-all | bytes 589824 | tf_op jit(solution)/shard_map/all_to_all | solution.py:26
  49.4 1.3 shard_map.61
  50.7 14.5 %all_to_all.46.got = f32[8,32,256]{2,1,0:T(8,128)S(1)} all-to-all(f32[8,32,256]{2,1,0:T(8,128)S(1)} %get-tuple-element.24), channel_id=1, replica_groups=mesh['z4'=2,'z2'=2,'z1'=2,'core'=2,'zh'=2,'y'=4,'x'=4] {'z2','z1','core'}, dimensions={0} | all-to-all | bytes 524288 | tf_op jit(solution)/shard_map/all_to_all | solution.py:26
  65.3 3.7 %collective-permute-start.2 = (f32[4,16,256]{2,1,0:T(8,128)S(1)}, f32[4,16,256]{2,1,0:T(8,128)S(1)}, u32[]{:S(2)}, u32[]{:S(2)}) collective-permute-start(f32[4,16,256]{2,1,0:T(8,128)S(1)} %shard_map.62.mine), channel_id=1, source_target_pairs={{0,256},{256,0},{1,257},{257,1},{2,258},{258,2},{3,259},{259,3},{4... | collective-permute-start | bytes 196616 | tf_op jit(solution)/shard_map/ppermute | solution.py:30
  69.1 6.3 %collective-permute-done.2.theirs = f32[4,16,256]{2,1,0:T(8,128)S(1)} collective-permute-done((f32[4,16,256]{2,1,0:T(8,128)S(1)}, f32[4,16,256]{2,1,0:T(8,128)S(1)}, u32[]{:S(2)}, u32[]{:S(2)}) %collective-permute-start.2) | collective-permute-done | bytes 65568 | tf_op jit(solution)/shard_map/ppermute | solution.py:30
  75.4 12.4 %all_to_all.47.h_got = f32[8,16,256]{2,1,0:T(8,128)S(1)} all-to-all(f32[8,16,256]{2,1,0:T(8,128)S(1)} %get-tuple-element.25), channel_id=1, replica_groups=mesh['z4'=2,'z2'=2,'z1'=2,'core'=2,'zh'=2,'y'=4,'x'=4] {'z2','z1','core'}, dimensions={0} | all-to-all | bytes 262144 | tf_op jit(solution)/shard_map/all_to_all | solution.py:26
  89.1 11.5 %all_to_all.48.got = f32[16,16,256]{2,1,0:T(8,128)S(1)} all-to-all(f32[16,16,256]{2,1,0:T(8,128)S(1)} %shard_map.64), channel_id=1, replica_groups=mesh['z4'=2,'z2'=2,'z1'=2,'core'=2,'zh'=2,'y'=4,'x'=4] {'y','x'}, dimensions={0} | all-to-all | bytes 524288 | tf_op jit(solution)/shard_map/all_to_all | solution.py:26
  100.7 8.4 %collective-permute-start.3 = (f32[4,8,256]{2,1,0:T(8,128)S(1)}, f32[4,8,256]{2,1,0:T(8,128)S(1)}, u32[]{:S(2)}, u32[]{:S(2)}) collective-permute-start(f32[4,8,256]{2,1,0:T(8,128)S(1)} %shard_map.65.mine), channel_id=1, source_target_pairs={{0,16},{16,0},{1,17},{17,1},{2,18},{18,2},{3,19},{19,3},{4,20},{20... | collective-permute-start | bytes 98312 | tf_op jit(solution)/shard_map/ppermute | solution.py:30
  109.1 6.1 %collective-permute-done.3.theirs = f32[4,8,256]{2,1,0:T(8,128)S(1)} collective-permute-done((f32[4,8,256]{2,1,0:T(8,128)S(1)}, f32[4,8,256]{2,1,0:T(8,128)S(1)}, u32[]{:S(2)}, u32[]{:S(2)}) %collective-permute-start.3) | collective-permute-done | bytes 32800 | tf_op jit(solution)/shard_map/ppermute | solution.py:30
  115.3 10.9 %all_to_all.49.w_got = f32[16,8,256]{2,1,0:T(8,128)S(1)} all-to-all(f32[16,8,256]{2,1,0:T(8,128)S(1)} %get-tuple-element.29), channel_id=1, replica_groups=mesh['z4'=2,'z2'=2,'z1'=2,'core'=2,'zh'=2,'y'=4,'x'=4] {'y','x'}, dimensions={0} | all-to-all | bytes 262144 | tf_op jit(solution)/shard_map/all_to_all | solution.py:26
  126.2 1.2 shard_map.67
  127.4 12.7 %all_to_all.50.got = f32[8,32,256]{2,1,0:T(8,128)S(1)} all-to-all(f32[8,32,256]{2,1,0:T(8,128)S(1)} %get-tuple-element.30), channel_id=1, replica_groups=mesh['z4'=2,'z2'=2,'z1'=2,'core'=2,'zh'=2,'y'=4,'x'=4] {'z2','z1','core'}, dimensions={0} | all-to-all | bytes 524288 | tf_op jit(solution)/shard_map/all_to_all | solution.py:26
  140.3 2.3 %collective-permute-start.4 = (f32[4,16,256]{2,1,0:T(8,128)S(1)}, f32[4,16,256]{2,1,0:T(8,128)S(1)}, u32[]{:S(2)}, u32[]{:S(2)}) collective-permute-start(f32[4,16,256]{2,1,0:T(8,128)S(1)} %shard_map.68.mine), channel_id=1, source_target_pairs={{0,256},{256,0},{1,257},{257,1},{2,258},{258,2},{3,259},{259,3},{4... | collective-permute-start | bytes 196616 | tf_op jit(solution)/shard_map/ppermute | solution.py:30
  142.5 7.8 %collective-permute-done.4.theirs = f32[4,16,256]{2,1,0:T(8,128)S(1)} collective-permute-done((f32[4,16,256]{2,1,0:T(8,128)S(1)}, f32[4,16,256]{2,1,0:T(8,128)S(1)}, u32[]{:S(2)}, u32[]{:S(2)}) %collective-permute-start.4) | collective-permute-done | bytes 65568 | tf_op jit(solution)/shard_map/ppermute | solution.py:30
  150.4 12.4 %all_to_all.51.h_got = f32[8,16,256]{2,1,0:T(8,128)S(1)} all-to-all(f32[8,16,256]{2,1,0:T(8,128)S(1)} %get-tuple-element.31), channel_id=1, replica_groups=mesh['z4'=2,'z2'=2,'z1'=2,'core'=2,'zh'=2,'y'=4,'x'=4] {'z2','z1','core'}, dimensions={0} | all-to-all | bytes 262144 | tf_op jit(solution)/shard_map/all_to_all | solution.py:26
  164.0 11.8 %all_to_all.52.got = f32[16,16,256]{2,1,0:T(8,128)S(1)} all-to-all(f32[16,16,256]{2,1,0:T(8,128)S(1)} %shard_map.70), channel_id=1, replica_groups=mesh['z4'=2,'z2'=2,'z1'=2,'core'=2,'zh'=2,'y'=4,'x'=4] {'y','x'}, dimensions={0} | all-to-all | bytes 524288 | tf_op jit(solution)/shard_map/all_to_all | solution.py:26
  175.9 8.3 %collective-permute-start.5 = (f32[4,8,256]{2,1,0:T(8,128)S(1)}, f32[4,8,256]{2,1,0:T(8,128)S(1)}, u32[]{:S(2)}, u32[]{:S(2)}) collective-permute-start(f32[4,8,256]{2,1,0:T(8,128)S(1)} %shard_map.71.mine), channel_id=1, source_target_pairs={{0,16},{16,0},{1,17},{17,1},{2,18},{18,2},{3,19},{19,3},{4,20},{20... | collective-permute-start | bytes 98312 | tf_op jit(solution)/shard_map/ppermute | solution.py:30
  184.8 5.6 %collective-permute-done.5.theirs = f32[4,8,256]{2,1,0:T(8,128)S(1)} collective-permute-done((f32[4,8,256]{2,1,0:T(8,128)S(1)}, f32[4,8,256]{2,1,0:T(8,128)S(1)}, u32[]{:S(2)}, u32[]{:S(2)}) %collective-permute-start.5) | collective-permute-done | bytes 32800 | tf_op jit(solution)/shard_map/ppermute | solution.py:30
  (20 shorter events, 5.7 us)
Async XLA Ops:
  0.6 9.8 %collective-permute-start.1 = (f32[4,1024]{1,0:T(4,128)}, f32[4,1024]{1,0:T(4,128)S(1)}, u32[]{:S(2)}, u32[]{:S(2)}) collective-permute-start(f32[4,1024]{1,0:T(4,128)} %mine.2), channel_id=1, source_target_pairs={{0,256},{256,0},{1,257},{257,1},{2,258},{258,2},{3,259},{259,3},{4... | collective-permute-start | bytes 49160 | tf_op jit(solution)/shard_map/ppermute | solution.py:30
  10.4 0.7 copy-start.1
  12.5 6.0 %copy-start.2 = (f32[2,1024]{1,0:T(2,128)S(1)}, f32[2,1024]{1,0:T(2,128)}, u32[]{:S(2)}) copy-start(f32[2,1024]{1,0:T(2,128)} %mine.3) | copy-start | bytes 24580
  12.5 20.5 %all-to-all-start = ((f32[8,8,1152]{2,1,0:T(8,128)}), f32[8,8,1152]{2,1,0:T(8,128)S(1)}, u32[]{:S(2)}, u32[]{:S(2)}) async-start(f32[8,8,1152]{2,1,0:T(8,128)} %shard_map.59), calls=%async_computation | async-start | bytes 589824 | tf_op jit(solution)/shard_map/all_to_all | solution.py:26
  18.6 30.9 %copy-start = (f32[1,1,512,256]{3,2,1,0:T(8,128)S(1)}, f32[1,1,512,256]{3,2,1,0:T(8,128)}, u32[]{:S(2)}) copy-start(f32[1,1,512,256]{3,2,1,0:T(8,128)} %param.5) | copy-start | bytes 1572868
  18.6 14.4 %collective-permute-start = (f32[2,1024]{1,0:T(2,128)S(1)}, f32[2,1024]{1,0:T(2,128)S(1)}, u32[]{:S(2)}, u32[]{:S(2)}) collective-permute-start(f32[2,1024]{1,0:T(2,128)S(1)} %copy-done.2), channel_id=1, source_target_pairs={{0,16},{16,0},{1,17},{17,1},{2,18},{18,2},{3,19},{19,3},{4,20},{20... | collective-permute-start | bytes 24584 | tf_op jit(solution)/shard_map/ppermute | solution.py:30
  65.3 10.1 %collective-permute-start.2 = (f32[4,16,256]{2,1,0:T(8,128)S(1)}, f32[4,16,256]{2,1,0:T(8,128)S(1)}, u32[]{:S(2)}, u32[]{:S(2)}) collective-permute-start(f32[4,16,256]{2,1,0:T(8,128)S(1)} %shard_map.62.mine), channel_id=1, source_target_pairs={{0,256},{256,0},{1,257},{257,1},{2,258},{258,2},{3,259},{259,3},{4... | collective-permute-start | bytes 196616 | tf_op jit(solution)/shard_map/ppermute | solution.py:30
  100.7 14.5 %collective-permute-start.3 = (f32[4,8,256]{2,1,0:T(8,128)S(1)}, f32[4,8,256]{2,1,0:T(8,128)S(1)}, u32[]{:S(2)}, u32[]{:S(2)}) collective-permute-start(f32[4,8,256]{2,1,0:T(8,128)S(1)} %shard_map.65.mine), channel_id=1, source_target_pairs={{0,16},{16,0},{1,17},{17,1},{2,18},{18,2},{3,19},{19,3},{4,20},{20... | collective-permute-start | bytes 98312 | tf_op jit(solution)/shard_map/ppermute | solution.py:30
  140.3 10.1 %collective-permute-start.4 = (f32[4,16,256]{2,1,0:T(8,128)S(1)}, f32[4,16,256]{2,1,0:T(8,128)S(1)}, u32[]{:S(2)}, u32[]{:S(2)}) collective-permute-start(f32[4,16,256]{2,1,0:T(8,128)S(1)} %shard_map.68.mine), channel_id=1, source_target_pairs={{0,256},{256,0},{1,257},{257,1},{2,258},{258,2},{3,259},{259,3},{4... | collective-permute-start | bytes 196616 | tf_op jit(solution)/shard_map/ppermute | solution.py:30
  175.9 14.5 %collective-permute-start.5 = (f32[4,8,256]{2,1,0:T(8,128)S(1)}, f32[4,8,256]{2,1,0:T(8,128)S(1)}, u32[]{:S(2)}, u32[]{:S(2)}) collective-permute-start(f32[4,8,256]{2,1,0:T(8,128)S(1)} %shard_map.71.mine), channel_id=1, source_target_pairs={{0,16},{16,0},{1,17},{17,1},{2,18},{18,2},{3,19},{19,3},{4,20},{20... | collective-permute-start | bytes 98312 | tf_op jit(solution)/shard_map/ppermute | solution.py:30

commit v4 on v3

v4 whole, which is shorter than its diff:
```python
import jax
import jax.numpy as jnp
from jax import lax
from jax.experimental import pallas as pl
from jax.experimental.pallas import tpu as pltpu
from jax.sharding import Mesh, PartitionSpec as P

RANK = 64
BS = 256
CAP = 2
NB = 4
TAB = 128

FINE = ("z4", "z2", "z1", "core", "zh", "y", "x")
HALF = ("z2", "z1", "core")
PLANE = ("y", "x")
NH = 8
COLS = NB * BS // NH
NP = 16

NN = (((1,), (0,)), ((), ()))
NT = (((1,), (1,)), ((), ()))


def exchange(x, axes):
    return lax.all_to_all(x, axes, split_axis=0, concat_axis=0, tiled=True)


def swap(x, axis):
    return lax.ppermute(x, axis, [(0, 1), (1, 0)])


def halves(x):
    hi = x.astype(jnp.bfloat16)
    lo = (x - hi.astype(jnp.float32)).astype(jnp.bfloat16)
    return hi, lo


def product(a, b, dims):
    dot = lambda x, y: lax.dot_general(x, y, dims, preferred_element_type=jnp.float32)
    return dot(a[0], b[0]) + (dot(a[0], b[1]) + dot(a[1], b[0]))


def grams(left, values, dims, live):
    whole = halves(left)
    left = halves(left * live)
    return product(left, halves(values), dims), product(left, whole, NT)


def sums(left, right, values, dims, live):
    upper, gram = grams(left, values, dims, live)
    return upper, product(halves(gram), halves(right), NN)


def live_of(blk, j):
    return jnp.where(blk[0, j] >= 0, 1.0, 0.0).astype(jnp.float32)


def block_of(blk, d, j):
    return jnp.maximum(blk[d, j], 0)


def with_list(rows, blk, d, lists):
    lane = lax.broadcasted_iota(jnp.int32, (rows.shape[0], TAB), 1)
    lists[:, : NB * BS] = rows
    lists[:, NB * BS :] = jnp.where(lane == 0, blk[d, 0], blk[d, 1]).astype(jnp.float32)


def w_pair_kernel(blk, mine, theirs, out, message):
    first = lax.axis_index("zh") == 0
    low = jnp.where(first, mine[...], theirs[...])
    high = jnp.where(first, theirs[...], mine[...])
    with_list(jnp.concatenate([low, high], axis=0), blk, 0, message)
    for q in range(NP):
        out[q] = message[...]


def read_list(table, q, listed):
    for j in range(CAP):
        table[q * CAP + j] = jnp.maximum(listed[:, j : j + 1].astype(jnp.int32)[0, 0], 0)


def h1_terms_kernel(blk, w0, h, values, w_slots, w_own, out, rows):
    out[:, :96, :] = jnp.zeros((NH, 96, COLS), jnp.float32)
    for j in range(CAP):
        at = pl.multiple_of(block_of(blk, 0, j) * BS, BS)
        for q in range(NP):
            w_slots[j, 4 * q : 4 * q + 4, :] = w0[q, :, pl.ds(at, BS)]
        upper, gram = grams(w_slots[j], values[j * BS : (j + 1) * BS, :], NN, live_of(blk, j))
        gram = jnp.concatenate([gram[:32], gram[32:]], axis=1)
        for side in range(2):
            q = 2 * block_of(blk, 1, j) + side
            out[q, :64, :] = out[q, :64, :] + upper[:, COLS * side : COLS * (side + 1)]
            out[q, 64:96, :] = out[q, 64:96, :] + gram
    lane = lax.broadcasted_iota(jnp.int32, (4, COLS), 1)
    listed = jnp.where(lane == 0, blk[1, 0], blk[1, 1]).astype(jnp.float32)
    for q in range(NH):
        out[q, 96:100, :] = h[:, COLS * q : COLS * (q + 1)]
        out[q, 100:104, :] = listed
    plane = lax.axis_index(PLANE)
    for b in range(NB):
        w_own[b] = w0[plane, :, b * BS : (b + 1) * BS]
    for q in range(NP):
        read_list(rows, q, w0[q, 0:1, NB * BS :])


def h1_collect_kernel(got, out, cols):
    total = got[0, :96, :]
    for q in range(1, NH):
        total = total + got[q, :96, :]
    out[:96, :] = total
    for q in range(NH):
        out[96 + 4 * q : 100 + 4 * q, :] = got[q, 96:100, :]
        read_list(cols, q, got[q, 100:101, :])


def h1_update_kernel(mine, theirs, out):
    total = mine[:96, :] + theirs[:96, :]
    gram = jnp.concatenate([total[64:, :64], total[64:, 64:]], axis=0)
    first = lax.axis_index("z4") == 0
    low = jnp.where(first, mine[96:, :], theirs[96:, :])
    high = jnp.where(first, theirs[96:, :], mine[96:, :])
    pairs = []
    for k in range(16):
        pairs += [low[2 * k : 2 * k + 2], high[2 * k : 2 * k + 2]]
    old = jnp.concatenate(pairs, axis=0)
    new = old * total[:64] / product(halves(gram), halves(old), NN)
    for q in range(NH):
        out[q] = new


def whole_block(h_all, b):
    return jnp.concatenate([h_all[2 * b], h_all[2 * b + 1]], axis=1)


def send_w(out, j, upper, lower):
    for q in range(NP):
        out[q, 8 * j : 8 * j + 4, :] = upper[4 * q : 4 * q + 4, :]
        out[q, 8 * j + 4 : 8 * j + 8, :] = lower[4 * q : 4 * q + 4, :]


def w1_terms_kernel(blk, h_all, w_slots, values, out):
    for j in range(CAP):
        h_slot = whole_block(h_all, block_of(blk, 1, j))
        send_w(out, j, *sums(h_slot, w_slots[j], values[j * BS : (j + 1) * BS, :], NT, live_of(blk, j)))


def w2_terms_kernel(blk, h_got, w_slots, values, out):
    for j in range(CAP):
        h_slot = h_got[:, 8 * j : 8 * j + 8, :].reshape(RANK, BS)
        send_w(out, j, *sums(h_slot, w_slots[j], values[j * BS : (j + 1) * BS, :], NT, live_of(blk, j)))


def w_slot(got, j):
    return jnp.concatenate([got[q, 4 * j : 4 * j + 4, :] for q in range(NP)], axis=0)


def h2_terms_kernel(blk, w_got, values, w_slots, out):
    both = []
    for j in range(CAP):
        w_slots[j] = w_slot(w_got, j)
        upper, gram = grams(w_slots[j], values[j * BS : (j + 1) * BS, :], NN, live_of(blk, j))
        both.append(gram)
        for q in range(NH):
            out[q, :, BS * j : BS * (j + 1)] = upper[8 * q : 8 * q + 8, :]
    both = jnp.concatenate(both, axis=1)
    for q in range(NH):
        out[q, :, CAP * BS :] = both[8 * q : 8 * q + 8, :]


def h2_collect_kernel(table, got, out):
    out[...] = jnp.zeros(out.shape, out.dtype)
    lane = lax.broadcasted_iota(jnp.int32, (8, CAP * RANK), 1)
    for q in range(NH):
        gram = got[q, :, CAP * BS :]
        for j in range(CAP):
            b = table[q * CAP + j]
            out[b, :, :BS] = out[b, :, :BS] + got[q, :, BS * j : BS * (j + 1)]
            out[b, :, BS:] = out[b, :, BS:] + jnp.where(lane // RANK == j, gram, 0.0)


def h2_update_kernel(table, h_all, mine, theirs, final, out, new):
    half = lax.axis_index(HALF)
    first = lax.axis_index("z4") == 0
    for b in range(NB):
        total = mine[b] + theirs[b]
        gram = total[:, BS:]
        high = gram.astype(jnp.bfloat16).astype(jnp.float32)
        gram = jnp.concatenate([high, gram - high], axis=0).astype(jnp.bfloat16)
        block = whole_block(h_all, b)
        block = halves(jnp.concatenate([block, block], axis=0))
        most = lax.dot_general(gram, block[0], NN, preferred_element_type=jnp.float32)
        rest = lax.dot_general(gram, block[1], NN, preferred_element_type=jnp.float32)
        lower = most[:8] + (most[8:] + rest[:8])
        at = pl.multiple_of(8 * half, 8)
        own = jnp.concatenate([h_all[2 * b, pl.ds(at, 8), :], h_all[2 * b + 1, pl.ds(at, 8), :]], axis=1)
        rows = own * total[:, :BS] / lower
        new[b] = rows
        for high in range(2):
            pair = rows[4 * high : 4 * high + 4]
            final[2 * high : 2 * high + 2, b * BS : (b + 1) * BS] = jnp.where(first, pair[0:2], pair[2:4])
    for q in range(NH):
        for j in range(CAP):
            out[q, 8 * j : 8 * (j + 1), :] = new[table[q * CAP + j]]


def collect_kernel(table, got, out):
    rows = out.shape[1]
    out[...] = jnp.zeros(out.shape, out.dtype)
    for q in range(got.shape[0]):
        for j in range(CAP):
            b = table[q * CAP + j]
            out[b] = out[b] + got[q, rows * j : rows * (j + 1), :]


def updated(own, mine, theirs):
    rows = own.shape[1]
    upper = mine[:, :rows, :] + theirs[:, :rows, :]
    lower = mine[:, rows:, :] + theirs[:, rows:, :]
    return own[...] * upper / lower


def update_kernel(table, own, mine, theirs, new, out):
    rows = own.shape[1]
    new[...] = updated(own, mine, theirs)
    for q in range(out.shape[0]):
        for j in range(CAP):
            out[q, rows * j : rows * (j + 1), :] = new[table[q * CAP + j]]


def last_w_kernel(own, mine, theirs, final, new):
    new[...] = updated(own, mine, theirs)
    first = lax.axis_index("zh") == 0
    for b in range(NB):
        final[:, b * BS : (b + 1) * BS] = jnp.where(first, new[b, 0:2, :], new[b, 2:4, :])


def call(body, scalars, arrays, outs, tables=(), scratch=(), name=None):
    smem = pl.BlockSpec(memory_space=pltpu.SMEM)
    vmem = pl.BlockSpec(memory_space=pltpu.VMEM)
    return pl.pallas_call(
        body,
        in_specs=[smem] * len(scalars) + [vmem] * len(arrays),
        out_specs=[vmem] * len(outs) + [smem] * len(tables),
        out_shape=[pltpu.VMEM(s, jnp.float32) for s in outs] + [pltpu.SMEM(s, jnp.int32) for s in tables],
        scratch_shapes=[pltpu.VMEM(s, jnp.float32) for s in scratch],
        name=name,
    )(
        *(pltpu.with_memory_space_constraint(a, pltpu.SMEM) for a in scalars),
        *(pltpu.with_memory_space_constraint(a, pltpu.VMEM) for a in arrays),
    )


def per_device(blocks, observed, w_factor, h_factor):
    blk = blocks[0, 0]
    values = observed[0, 0]
    wide = NB * BS + TAB

    w_other = swap(w_factor, "zh")
    (w_pair,) = call(w_pair_kernel, (blk,), (w_factor, w_other), [(NP, 4, wide)], scratch=[(4, wide)], name="w_pair")
    w_got = exchange(w_pair, PLANE)

    w_slots, w_own, sent, rows = call(
        h1_terms_kernel,
        (blk,),
        (w_got, h_factor, values),
        [(CAP, RANK, BS), (NB, 4, BS), (NH, 104, COLS)],
        tables=[(NP * CAP,)],
        name="h1_terms",
    )
    got = exchange(sent, HALF)
    mine, cols = call(h1_collect_kernel, (), (got,), [(128, COLS)], tables=[(NH * CAP,)], name="h1_collect")
    theirs = swap(mine, "z4")
    (out,) = call(h1_update_kernel, (), (mine, theirs), [(NH, RANK, COLS)], name="h1_update")
    h_all = exchange(out, HALF)

    (sent,) = call(w1_terms_kernel, (blk,), (h_all, w_slots, values), [(NP, 16, BS)], name="w1_terms")
    got = exchange(sent, PLANE)
    (mine,) = call(collect_kernel, (rows,), (got,), [(NB, 8, BS)], name="w1_collect")
    theirs = swap(mine, "zh")
    w_own, out = call(
        update_kernel, (rows,), (w_own, mine, theirs), [(NB, 4, BS), (NP, 8, BS)], name="w1_update"
    )
    w_got = exchange(out, PLANE)

    w_slots, sent = call(
        h2_terms_kernel, (blk,), (w_got, values), [(CAP, RANK, BS), (NH, 8, CAP * (BS + RANK))], name="h2_terms"
    )
    got = exchange(sent, HALF)
    (mine,) = call(h2_collect_kernel, (cols,), (got,), [(NB, 8, BS + CAP * RANK)], name="h2_collect")
    theirs = swap(mine, "z4")
    h_final, out = call(
        h2_update_kernel,
        (cols,),
        (h_all, mine, theirs),
        [(4, NB * BS), (NH, 16, BS)],
        scratch=[(NB, 8, BS)],
        name="h2_update",
    )
    h_got = exchange(out, HALF)

    (sent,) = call(w2_terms_kernel, (blk,), (h_got, w_slots, values), [(NP, 16, BS)], name="w2_terms")
    got = exchange(sent, PLANE)
    (mine,) = call(collect_kernel, (rows,), (got,), [(NB, 8, BS)], name="w2_collect")
    theirs = swap(mine, "zh")
    (w_final,) = call(
        last_w_kernel, (), (w_own, mine, theirs), [(2, NB * BS)], scratch=[(NB, 4, BS)], name="w2_update"
    )
    return w_final, h_final


def solution(mesh):
    fine = Mesh(mesh.devices.reshape(2, 2, 2, 2, 2, 4, 4), FINE)
    tex = ("z4",) + HALF
    smp = ("zh",) + PLANE
    in_specs = (P(tex, smp, None, None), P(tex, smp, None, None), P(smp, tex), P(tex, smp))
    out_specs = (P(smp, tex), P(tex, smp))
    return jax.shard_map(per_device, mesh=fine, in_specs=in_specs, out_specs=out_specs, check_vma=False)
```

time: 192 us -> 179 us (0.932)
  the two profiles are of different devices: /device:TPU:128 before, /device:TPU:32 now
where the time goes in v4:
time: 179 us; the launch traced here: 178 us
  blocking collectives  99.1 us (55%)
  starting transfers between devices  54.4 us (30%)
  waiting for transfers between devices  15.3 us (9%)
  Pallas kernels  6.28 us (4%)
  local copies, waits for them, and re-layouts  1.92 us (1%)
    all_to_all x8, blocking collectives, exchange(): return lax.all_to_all(x, axes, split_axis=0, concat_axis=0, tiled=True)  99.1 us
    ppermute x5, starting transfers between devices, swap(): return lax.ppermute(x, axis, [(0, 1), (1, 0)])  54.4 us
    ppermute x5, waiting for transfers between devices, swap(): return lax.ppermute(x, axis, [(0, 1), (1, 0)])  15.3 us
    pallas_call x13, Pallas kernels, call(): pl.pallas_call(body, in_specs=[smem] * len(scalars) + [vmem] * len(arrays...  6.28 us
  transfers between devices with their start and end apart: 5, of which 5 were waited for; matrix products, arithmetic and copies ran while one was open for 0% of the time, Pallas kernels for 0%

profile of v4, /device:TPU:32, one launch (start us, length us, event | category | flops | bytes accessed | tf_op | source)
XLA Modules:
  0.0 177.8 jit_solution(7226496156310877260)
XLA Ops:
  0.6 15.0 %collective-permute-start = (f32[2,1024]{1,0:T(2,128)}, f32[2,1024]{1,0:T(2,128)S(1)}, u32[]{:S(2)}, u32[]{:S(2)}) collective-permute-start(f32[2,1024]{1,0:T(2,128)} %mine.1), channel_id=1, source_target_pairs={{0,16},{16,0},{1,17},{17,1},{2,18},{18,2},{3,19},{19,3},{4,20},{20... | collective-permute-start | bytes 24584 | tf_op jit(solution)/shard_map/ppermute | solution.py:30
  15.6 1.8 %collective-permute-done.theirs = f32[2,1024]{1,0:T(2,128)S(1)} collective-permute-done((f32[2,1024]{1,0:T(2,128)}, f32[2,1024]{1,0:T(2,128)S(1)}, u32[]{:S(2)}, u32[]{:S(2)}) %collective-permute-start) | collective-permute-done | bytes 8224 | tf_op jit(solution)/shard_map/ppermute | solution.py:30
  17.4 0.7 copy-done.2
  18.1 0.7 w_pair.1
  18.9 15.7 %all_to_all.40.w0 = f32[16,4,1152]{2,1,0:T(4,128)S(1)} all-to-all(f32[16,4,1152]{2,1,0:T(4,128)S(1)} %w_pair.1), channel_id=1, replica_groups=mesh['z4'=2,'z2'=2,'z1'=2,'core'=2,'zh'=2,'y'=4,'x'=4] {'y','x'}, dimensions={0} | all-to-all | bytes 589824 | tf_op jit(solution)/shard_map/all_to_all | solution.py:26
  34.6 1.1 h1_terms.1
  35.7 15.3 %all_to_all.41.got = f32[8,104,128]{2,1,0:T(8,128)S(1)} all-to-all(f32[8,104,128]{2,1,0:T(8,128)S(1)} %get-tuple-element.16), channel_id=1, replica_groups=mesh['z4'=2,'z2'=2,'z1'=2,'core'=2,'zh'=2,'y'=4,'x'=4] {'z2','z1','core'}, dimensions={0} | all-to-all | bytes 851968 | tf_op jit(solution)/shard_map/all_to_all | solution.py:26
  51.1 8.7 %collective-permute-start.1 = (f32[128,128]{1,0:T(8,128)S(1)}, f32[128,128]{1,0:T(8,128)S(1)}, u32[]{:S(2)}, u32[]{:S(2)}) collective-permute-start(f32[128,128]{1,0:T(8,128)S(1)} %get-tuple-element.17.mine), channel_id=1, source_target_pairs={{0,256},{256,0},{1,257},{257,1},{2,258},{258,2},{3,259},{259,3},{4... | collective-permute-start | bytes 196616 | tf_op jit(solution)/shard_map/ppermute | solution.py:30
  59.9 4.6 %collective-permute-done.1.theirs = f32[128,128]{1,0:T(8,128)S(1)} collective-permute-done((f32[128,128]{1,0:T(8,128)S(1)}, f32[128,128]{1,0:T(8,128)S(1)}, u32[]{:S(2)}, u32[]{:S(2)}) %collective-permute-start.1) | collective-permute-done | bytes 65568 | tf_op jit(solution)/shard_map/ppermute | solution.py:30
  64.7 12.9 %all_to_all.42.h_all = f32[8,64,128]{2,1,0:T(8,128)S(1)} all-to-all(f32[8,64,128]{2,1,0:T(8,128)S(1)} %h1_update.1), channel_id=1, replica_groups=mesh['z4'=2,'z2'=2,'z1'=2,'core'=2,'zh'=2,'y'=4,'x'=4] {'z2','z1','core'}, dimensions={0} | all-to-all | bytes 524288 | tf_op jit(solution)/shard_map/all_to_all | solution.py:26
  77.6 1.2 w1_terms.1
  78.9 11.5 %all_to_all.43.got = f32[16,16,256]{2,1,0:T(8,128)S(1)} all-to-all(f32[16,16,256]{2,1,0:T(8,128)S(1)} %w1_terms.1), channel_id=1, replica_groups=mesh['z4'=2,'z2'=2,'z1'=2,'core'=2,'zh'=2,'y'=4,'x'=4] {'y','x'}, dimensions={0} | all-to-all | bytes 524288 | tf_op jit(solution)/shard_map/all_to_all | solution.py:26
  90.5 11.5 %collective-permute-start.2 = (f32[4,8,256]{2,1,0:T(8,128)S(1)}, f32[4,8,256]{2,1,0:T(8,128)S(1)}, u32[]{:S(2)}, u32[]{:S(2)}) collective-permute-start(f32[4,8,256]{2,1,0:T(8,128)S(1)} %w1_collect.1.mine), channel_id=1, source_target_pairs={{0,16},{16,0},{1,17},{17,1},{2,18},{18,2},{3,19},{19,3},{4,20},{20... | collective-permute-start | bytes 98312 | tf_op jit(solution)/shard_map/ppermute | solution.py:30
  102.0 3.0 %collective-permute-done.2.theirs = f32[4,8,256]{2,1,0:T(8,128)S(1)} collective-permute-done((f32[4,8,256]{2,1,0:T(8,128)S(1)}, f32[4,8,256]{2,1,0:T(8,128)S(1)}, u32[]{:S(2)}, u32[]{:S(2)}) %collective-permute-start.2) | collective-permute-done | bytes 32800 | tf_op jit(solution)/shard_map/ppermute | solution.py:30
  105.1 10.9 %all_to_all.44.w_got = f32[16,8,256]{2,1,0:T(8,128)S(1)} all-to-all(f32[16,8,256]{2,1,0:T(8,128)S(1)} %get-tuple-element.21), channel_id=1, replica_groups=mesh['z4'=2,'z2'=2,'z1'=2,'core'=2,'zh'=2,'y'=4,'x'=4] {'y','x'}, dimensions={0} | all-to-all | bytes 262144 | tf_op jit(solution)/shard_map/all_to_all | solution.py:26
  116.0 1.0 h2_terms.1
  117.1 10.7 %all_to_all.45.got = f32[8,8,640]{2,1,0:T(8,128)S(1)} all-to-all(f32[8,8,640]{2,1,0:T(8,128)S(1)} %get-tuple-element.22), channel_id=1, replica_groups=mesh['z4'=2,'z2'=2,'z1'=2,'core'=2,'zh'=2,'y'=4,'x'=4] {'z2','z1','core'}, dimensions={0} | all-to-all | bytes 327680 | tf_op jit(solution)/shard_map/all_to_all | solution.py:26
  127.8 8.0 %collective-permute-start.3 = (f32[4,8,384]{2,1,0:T(8,128)S(1)}, f32[4,8,384]{2,1,0:T(8,128)S(1)}, u32[]{:S(2)}, u32[]{:S(2)}) collective-permute-start(f32[4,8,384]{2,1,0:T(8,128)S(1)} %h2_collect.1.mine), channel_id=1, source_target_pairs={{0,256},{256,0},{1,257},{257,1},{2,258},{258,2},{3,259},{259,3},{4... | collective-permute-start | bytes 147464 | tf_op jit(solution)/shard_map/ppermute | solution.py:30
  135.8 3.1 %collective-permute-done.3.theirs = f32[4,8,384]{2,1,0:T(8,128)S(1)} collective-permute-done((f32[4,8,384]{2,1,0:T(8,128)S(1)}, f32[4,8,384]{2,1,0:T(8,128)S(1)}, u32[]{:S(2)}, u32[]{:S(2)}) %collective-permute-start.3) | collective-permute-done | bytes 49184 | tf_op jit(solution)/shard_map/ppermute | solution.py:30
  139.2 10.2 %all_to_all.46.h_got = f32[8,16,256]{2,1,0:T(8,128)S(1)} all-to-all(f32[8,16,256]{2,1,0:T(8,128)S(1)} %get-tuple-element.23), channel_id=1, replica_groups=mesh['z4'=2,'z2'=2,'z1'=2,'core'=2,'zh'=2,'y'=4,'x'=4] {'z2','z1','core'}, dimensions={0} | all-to-all | bytes 262144 | tf_op jit(solution)/shard_map/all_to_all | solution.py:26
  149.4 1.2 w2_terms.1
  150.7 11.8 %all_to_all.47.got = f32[16,16,256]{2,1,0:T(8,128)S(1)} all-to-all(f32[16,16,256]{2,1,0:T(8,128)S(1)} %w2_terms.1), channel_id=1, replica_groups=mesh['z4'=2,'z2'=2,'z1'=2,'core'=2,'zh'=2,'y'=4,'x'=4] {'y','x'}, dimensions={0} | all-to-all | bytes 524288 | tf_op jit(solution)/shard_map/all_to_all | solution.py:26
  162.6 11.3 %collective-permute-start.4 = (f32[4,8,256]{2,1,0:T(8,128)S(1)}, f32[4,8,256]{2,1,0:T(8,128)S(1)}, u32[]{:S(2)}, u32[]{:S(2)}) collective-permute-start(f32[4,8,256]{2,1,0:T(8,128)S(1)} %w2_collect.1.mine), channel_id=1, source_target_pairs={{0,16},{16,0},{1,17},{17,1},{2,18},{18,2},{3,19},{19,3},{4,20},{20... | collective-permute-start | bytes 98312 | tf_op jit(solution)/shard_map/ppermute | solution.py:30
  174.5 2.7 %collective-permute-done.4.theirs = f32[4,8,256]{2,1,0:T(8,128)S(1)} collective-permute-done((f32[4,8,256]{2,1,0:T(8,128)S(1)}, f32[4,8,256]{2,1,0:T(8,128)S(1)}, u32[]{:S(2)}, u32[]{:S(2)}) %collective-permute-start.4) | collective-permute-done | bytes 32800 | tf_op jit(solution)/shard_map/ppermute | solution.py:30
  (15 shorter events, 2.2 us)
Async XLA Ops:
  0.6 34.0 %copy-start = (f32[1,1,512,256]{3,2,1,0:T(8,128)S(1)}, f32[1,1,512,256]{3,2,1,0:T(8,128)}, u32[]{:S(2)}) copy-start(f32[1,1,512,256]{3,2,1,0:T(8,128)} %param.5) | copy-start | bytes 1572868
  0.6 16.8 %collective-permute-start = (f32[2,1024]{1,0:T(2,128)}, f32[2,1024]{1,0:T(2,128)S(1)}, u32[]{:S(2)}, u32[]{:S(2)}) collective-permute-start(f32[2,1024]{1,0:T(2,128)} %mine.1), channel_id=1, source_target_pairs={{0,16},{16,0},{1,17},{17,1},{2,18},{18,2},{3,19},{19,3},{4,20},{20... | collective-permute-start | bytes 24584 | tf_op jit(solution)/shard_map/ppermute | solution.py:30
  17.4 0.7 copy-start.2
  18.9 15.7 %copy-start.1 = (f32[4,1024]{1,0:T(4,128)S(1)}, f32[4,1024]{1,0:T(4,128)}, u32[]{:S(2)}) copy-start(f32[4,1024]{1,0:T(4,128)} %h.1) | copy-start | bytes 49156
  51.1 13.3 %collective-permute-start.1 = (f32[128,128]{1,0:T(8,128)S(1)}, f32[128,128]{1,0:T(8,128)S(1)}, u32[]{:S(2)}, u32[]{:S(2)}) collective-permute-start(f32[128,128]{1,0:T(8,128)S(1)} %get-tuple-element.17.mine), channel_id=1, source_target_pairs={{0,256},{256,0},{1,257},{257,1},{2,258},{258,2},{3,259},{259,3},{4... | collective-permute-start | bytes 196616 | tf_op jit(solution)/shard_map/ppermute | solution.py:30
  90.5 14.5 %collective-permute-start.2 = (f32[4,8,256]{2,1,0:T(8,128)S(1)}, f32[4,8,256]{2,1,0:T(8,128)S(1)}, u32[]{:S(2)}, u32[]{:S(2)}) collective-permute-start(f32[4,8,256]{2,1,0:T(8,128)S(1)} %w1_collect.1.mine), channel_id=1, source_target_pairs={{0,16},{16,0},{1,17},{17,1},{2,18},{18,2},{3,19},{19,3},{4,20},{20... | collective-permute-start | bytes 98312 | tf_op jit(solution)/shard_map/ppermute | solution.py:30
  127.8 11.1 %collective-permute-start.3 = (f32[4,8,384]{2,1,0:T(8,128)S(1)}, f32[4,8,384]{2,1,0:T(8,128)S(1)}, u32[]{:S(2)}, u32[]{:S(2)}) collective-permute-start(f32[4,8,384]{2,1,0:T(8,128)S(1)} %h2_collect.1.mine), channel_id=1, source_target_pairs={{0,256},{256,0},{1,257},{257,1},{2,258},{258,2},{3,259},{259,3},{4... | collective-permute-start | bytes 147464 | tf_op jit(solution)/shard_map/ppermute | solution.py:30
  162.6 14.6 %collective-permute-start.4 = (f32[4,8,256]{2,1,0:T(8,128)S(1)}, f32[4,8,256]{2,1,0:T(8,128)S(1)}, u32[]{:S(2)}, u32[]{:S(2)}) collective-permute-start(f32[4,8,256]{2,1,0:T(8,128)S(1)} %w2_collect.1.mine), channel_id=1, source_target_pairs={{0,16},{16,0},{1,17},{17,1},{2,18},{18,2},{3,19},{19,3},{4,20},{20... | collective-permute-start | bytes 98312 | tf_op jit(solution)/shard_map/ppermute | solution.py:30

commit v5 on v4

v5 whole, which is shorter than its diff:
```python
import jax
import jax.numpy as jnp
from jax import lax
from jax.experimental import pallas as pl
from jax.experimental.pallas import tpu as pltpu
from jax.sharding import Mesh, PartitionSpec as P


RANK = 64
BS = 256
CAP = 2
NB = 4
TAB = 128

FINE = ("z4", "z2", "z1", "core", "zh", "y", "x")
HALF = ("z2", "z1", "core")
PLANE = ("y", "x")
QUAD = ("z2", "z1")
NH = 8
NQ = 4
NP = 16

NN = (((1,), (0,)), ((), ()))
NT = (((1,), (1,)), ((), ()))


def exchange(x, axes):
    return lax.all_to_all(x, axes, split_axis=0, concat_axis=0, tiled=True)


def swap(x, axis):
    return lax.ppermute(x, axis, [(0, 1), (1, 0)])


def halves(x):
    hi = x.astype(jnp.bfloat16)
    lo = (x - hi.astype(jnp.float32)).astype(jnp.bfloat16)
    return hi, lo


def product(a, b, dims):
    dot = lambda x, y: lax.dot_general(x, y, dims, preferred_element_type=jnp.float32)
    return dot(a[0], b[0]) + (dot(a[0], b[1]) + dot(a[1], b[0]))


def grams(left, values, dims, live):
    whole = halves(left)
    left = halves(left * live)
    return product(left, halves(values), dims), product(left, whole, NT)


def sums(left, right, values, dims, live):
    upper, gram = grams(left, values, dims, live)
    return upper, product(halves(gram), halves(right), NN)


def live_of(blk, j):
    return jnp.where(blk[0, j] >= 0, 1.0, 0.0).astype(jnp.float32)


def block_of(blk, d, j):
    return jnp.maximum(blk[d, j], 0)


def with_list(rows, blk, d, lists):
    lane = lax.broadcasted_iota(jnp.int32, (rows.shape[0], TAB), 1)
    lists[:, : NB * BS] = rows
    lists[:, NB * BS :] = jnp.where(lane == 0, blk[d, 0], blk[d, 1]).astype(jnp.float32)


def w_pair_kernel(blk, mine, theirs, out, message):
    first = lax.axis_index("zh") == 0
    low = jnp.where(first, mine[...], theirs[...])
    high = jnp.where(first, theirs[...], mine[...])
    with_list(jnp.concatenate([low, high], axis=0), blk, 0, message)
    for q in range(NP):
        out[q] = message[...]


def read_list(table, q, listed):
    for j in range(CAP):
        table[q * CAP + j] = jnp.maximum(listed[:, j : j + 1].astype(jnp.int32)[0, 0], 0)


def h_pack_kernel(blk, h, out, message):
    with_list(h[...], blk, 1, message)
    for q in range(NQ):
        out[q] = message[...]


def h_arrange_kernel(mine, theirs, h_all):
    first = lax.axis_index("z4") == 0
    for b in range(NB):
        lanes = slice(b * BS, (b + 1) * BS)
        for q in range(NH):
            at = 8 * q
            for high in range(2):
                pair = slice(2 * high, 2 * high + 2)
                here = mine[q % 2, q // 2, pair, lanes]
                there = theirs[q % 2, q // 2, pair, lanes]
                h_all[b, at + 4 * high : at + 4 * high + 2, :] = jnp.where(first, here, there)
                h_all[b, at + 4 * high + 2 : at + 4 * high + 4, :] = jnp.where(first, there, here)


def send_grams(out, uppers, both):
    both = jnp.concatenate(both, axis=1)
    for q in range(NH):
        for j in range(CAP):
            out[q, :, BS * j : BS * (j + 1)] = uppers[j][8 * q : 8 * q + 8, :]
        out[q, :, CAP * BS :] = both[8 * q : 8 * q + 8, :]


def h1_terms_kernel(blk, w0, h_half, values, w_slots, w_own, out, rows, cols):
    terms = []
    for j in range(CAP):
        at = pl.multiple_of(block_of(blk, 0, j) * BS, BS)
        for q in range(NP):
            w_slots[j, 4 * q : 4 * q + 4, :] = w0[q, :, pl.ds(at, BS)]
        terms.append(grams(w_slots[j], values[j * BS : (j + 1) * BS, :], NN, live_of(blk, j)))
    send_grams(out, *zip(*terms))
    plane = lax.axis_index(PLANE)
    for b in range(NB):
        w_own[b] = w0[plane, :, b * BS : (b + 1) * BS]
    for q in range(NP):
        read_list(rows, q, w0[q, 0:1, NB * BS :])
    for q in range(NH):
        read_list(cols, q, h_half[q % 2, q // 2, 0:1, NB * BS :])


def h_updated(h_all, mine, theirs, b, half):
    total = mine[b] + theirs[b]
    gram = total[:, BS:]
    high = gram.astype(jnp.bfloat16).astype(jnp.float32)
    gram = jnp.concatenate([high, gram - high], axis=0).astype(jnp.bfloat16)
    block = h_all[b]
    block = halves(jnp.concatenate([block, block], axis=0))
    most = lax.dot_general(gram, block[0], NN, preferred_element_type=jnp.float32)
    rest = lax.dot_general(gram, block[1], NN, preferred_element_type=jnp.float32)
    own = h_all[b, pl.ds(pl.multiple_of(8 * half, 8), 8), :]
    return own * total[:, :BS] / (most[:8] + (most[8:] + rest[:8]))


def h1_update_kernel(h_all, mine, theirs, out):
    half = lax.axis_index(HALF)
    for b in range(NB):
        rows = h_updated(h_all, mine, theirs, b, half)
        for q in range(NQ):
            out[q, b] = rows


def send_w(out, j, upper, lower):
    for q in range(NP):
        out[q, 8 * j : 8 * j + 4, :] = upper[4 * q : 4 * q + 4, :]
        out[q, 8 * j + 4 : 8 * j + 8, :] = lower[4 * q : 4 * q + 4, :]


def w1_terms_kernel(blk, h_got, w_slots, values, h_all, out):
    for b in range(NB):
        for q in range(NH):
            h_all[b, 8 * q : 8 * q + 8, :] = h_got[q % 2, q // 2, b]
    for j in range(CAP):
        h_slot = h_all[block_of(blk, 1, j)]
        send_w(out, j, *sums(h_slot, w_slots[j], values[j * BS : (j + 1) * BS, :], NT, live_of(blk, j)))


def w2_terms_kernel(blk, h_got, w_slots, values, out):
    for j in range(CAP):
        h_slot = h_got[:, 8 * j : 8 * j + 8, :].reshape(RANK, BS)
        send_w(out, j, *sums(h_slot, w_slots[j], values[j * BS : (j + 1) * BS, :], NT, live_of(blk, j)))


def w_slot(got, j):
    return jnp.concatenate([got[q, 4 * j : 4 * j + 4, :] for q in range(NP)], axis=0)


def h2_terms_kernel(blk, w_got, values, w_slots, out):
    terms = []
    for j in range(CAP):
        w_slots[j] = w_slot(w_got, j)
        terms.append(grams(w_slots[j], values[j * BS : (j + 1) * BS, :], NN, live_of(blk, j)))
    send_grams(out, *zip(*terms))


def h_collect_kernel(table, got, out):
    out[...] = jnp.zeros(out.shape, out.dtype)
    lane = lax.broadcasted_iota(jnp.int32, (8, CAP * RANK), 1)
    for q in range(NH):
        gram = got[q, :, CAP * BS :]
        for j in range(CAP):
            b = table[q * CAP + j]
            out[b, :, :BS] = out[b, :, :BS] + got[q, :, BS * j : BS * (j + 1)]
            out[b, :, BS:] = out[b, :, BS:] + jnp.where(lane // RANK == j, gram, 0.0)


def h2_update_kernel(table, h_all, mine, theirs, final, out, new):
    half = lax.axis_index(HALF)
    first = lax.axis_index("z4") == 0
    for b in range(NB):
        rows = h_updated(h_all, mine, theirs, b, half)
        new[b] = rows
        for high in range(2):
            pair = rows[4 * high : 4 * high + 4]
            final[2 * high : 2 * high + 2, b * BS : (b + 1) * BS] = jnp.where(first, pair[0:2], pair[2:4])
    for q in range(NH):
        for j in range(CAP):
            out[q, 8 * j : 8 * (j + 1), :] = new[table[q * CAP + j]]


def collect_kernel(table, got, out):
    rows = out.shape[1]
    out[...] = jnp.zeros(out.shape, out.dtype)
    for q in range(got.shape[0]):
        for j in range(CAP):
            b = table[q * CAP + j]
            out[b] = out[b] + got[q, rows * j : rows * (j + 1), :]


def updated(own, mine, theirs):
    rows = own.shape[1]
    upper = mine[:, :rows, :] + theirs[:, :rows, :]
    lower = mine[:, rows:, :] + theirs[:, rows:, :]
    return own[...] * upper / lower


def update_kernel(table, own, mine, theirs, new, out):
    rows = own.shape[1]
    new[...] = updated(own, mine, theirs)
    for q in range(out.shape[0]):
        for j in range(CAP):
            out[q, rows * j : rows * (j + 1), :] = new[table[q * CAP + j]]


def last_w_kernel(own, mine, theirs, final, new):
    new[...] = updated(own, mine, theirs)
    first = lax.axis_index("zh") == 0
    for b in range(NB):
        final[:, b * BS : (b + 1) * BS] = jnp.where(first, new[b, 0:2, :], new[b, 2:4, :])


def call(body, scalars, arrays, outs, tables=(), scratch=()):
    smem = pl.BlockSpec(memory_space=pltpu.SMEM)
    vmem = pl.BlockSpec(memory_space=pltpu.VMEM)
    return pl.pallas_call(
        body,
        in_specs=[smem] * len(scalars) + [vmem] * len(arrays),
        out_specs=[vmem] * len(outs) + [smem] * len(tables),
        out_shape=[pltpu.VMEM(s, jnp.float32) for s in outs] + [pltpu.SMEM(s, jnp.int32) for s in tables],
        scratch_shapes=[pltpu.VMEM(s, jnp.float32) for s in scratch],
    )(
        *(pltpu.with_memory_space_constraint(a, pltpu.SMEM) for a in scalars),
        *(pltpu.with_memory_space_constraint(a, pltpu.VMEM) for a in arrays),
    )


def per_device(blocks, observed, w_factor, h_factor):
    blk = blocks[0, 0]
    values = observed[0, 0]
    wide = NB * BS + TAB

    w_other = swap(w_factor, "zh")
    (h_pack,) = call(h_pack_kernel, (blk,), (h_factor,), [(NQ, 4, wide)], scratch=[(4, wide)])
    h_quad = exchange(h_pack, QUAD)
    h_half = lax.all_gather(h_quad, "core", axis=0)
    h_other = swap(h_half, "z4")
    (w_pair,) = call(w_pair_kernel, (blk,), (w_factor, w_other), [(NP, 4, wide)], scratch=[(4, wide)])
    w_got = exchange(w_pair, PLANE)

    grams_out = (NH, 8, CAP * (BS + RANK))
    w_slots, w_own, sent, rows, cols = call(
        h1_terms_kernel,
        (blk,),
        (w_got, h_half, values),
        [(CAP, RANK, BS), (NB, 4, BS), grams_out],
        tables=[(NP * CAP,), (NH * CAP,)],
    )
    got = exchange(sent, HALF)
    (mine,) = call(h_collect_kernel, (cols,), (got,), [(NB, 8, BS + CAP * RANK)])
    theirs = swap(mine, "z4")
    (h_all,) = call(h_arrange_kernel, (), (h_half, h_other), [(NB, RANK, BS)])
    (out,) = call(h1_update_kernel, (), (h_all, mine, theirs), [(NQ, NB, 8, BS)])
    h_got = lax.all_gather(exchange(out, QUAD), "core", axis=0)

    h_all, sent = call(w1_terms_kernel, (blk,), (h_got, w_slots, values), [(NB, RANK, BS), (NP, 16, BS)])
    got = exchange(sent, PLANE)
    (mine,) = call(collect_kernel, (rows,), (got,), [(NB, 8, BS)])
    theirs = swap(mine, "zh")
    w_own, out = call(update_kernel, (rows,), (w_own, mine, theirs), [(NB, 4, BS), (NP, 8, BS)])
    w_got = exchange(out, PLANE)

    w_slots, sent = call(h2_terms_kernel, (blk,), (w_got, values), [(CAP, RANK, BS), grams_out])
    got = exchange(sent, HALF)
    (mine,) = call(h_collect_kernel, (cols,), (got,), [(NB, 8, BS + CAP * RANK)])
    theirs = swap(mine, "z4")
    h_final, out = call(
        h2_update_kernel, (cols,), (h_all, mine, theirs), [(4, NB * BS), (NH, 16, BS)], scratch=[(NB, 8, BS)]
    )
    h_got = exchange(out, HALF)

    (sent,) = call(w2_terms_kernel, (blk,), (h_got, w_slots, values), [(NP, 16, BS)])
    got = exchange(sent, PLANE)
    (mine,) = call(collect_kernel, (rows,), (got,), [(NB, 8, BS)])
    theirs = swap(mine, "zh")
    (w_final,) = call(last_w_kernel, (), (w_own, mine, theirs), [(2, NB * BS)], scratch=[(NB, 4, BS)])
    return w_final, h_final


def solution(mesh):
    fine = Mesh(mesh.devices.reshape(2, 2, 2, 2, 2, 4, 4), FINE)
    tex = ("z4",) + HALF
    smp = ("zh",) + PLANE
    in_specs = (P(tex, smp, None, None), P(tex, smp, None, None), P(smp, tex), P(tex, smp))
    out_specs = (P(smp, tex), P(tex, smp))
    return jax.shard_map(per_device, mesh=fine, in_specs=in_specs, out_specs=out_specs, check_vma=False)
```

time: 179 us -> 187 us (1.045)
  the two profiles are of different devices: /device:TPU:32 before, /device:TPU:2 now
where the time goes in v5:
time: 187 us; the launch traced here: 186 us
  starting transfers between devices  80 us (43%)
  blocking collectives  67.1 us (36%)
  waiting for transfers between devices  27.2 us (15%)
  Pallas kernels  9 us (5%)
  local copies, waits for them, and re-layouts  1.93 us (1%)
    all_to_all x6, blocking collectives, exchange(): return lax.all_to_all(x, axes, split_axis=0, concat_axis=0, tiled=True)  63.2 us
    ppermute x6, starting transfers between devices, swap(): return lax.ppermute(x, axis, [(0, 1), (1, 0)])  61.5 us
    ppermute x6, waiting for transfers between devices, swap(): return lax.ppermute(x, axis, [(0, 1), (1, 0)])  21.6 us
    all_to_all x3, starting transfers between devices, exchange(): return lax.all_to_all(x, axes, split_axis=0, concat_axis=0, tiled=True)  18.5 us
    pallas_call x15, Pallas kernels, call(): pl.pallas_call(body, in_specs=[smem] * len(scalars) + [vmem] * len(arrays...  9 us
    all_to_all x3, waiting for transfers between devices, exchange(): return lax.all_to_all(x, axes, split_axis=0, concat_axis=0, tiled=True)  5.61 us
  transfers between devices with their start and end apart: 9, of which 7 were waited for; matrix products, arithmetic and copies ran while one was open for 0% of the time, Pallas kernels for 1%

profile of v5, /device:TPU:2, one launch (start us, length us, event | category | flops | bytes accessed | tf_op | source)
XLA Modules:
  0.0 186.0 jit_solution(3566543555832165478)
XLA Ops:
  2.7 6.0 %all-to-all-start.1 = ((f32[4,4,1152]{2,1,0:T(4,128)}), f32[4,4,1152]{2,1,0:T(4,128)S(1)}, u32[]{:S(2)}, u32[]{:S(2)}) async-start(f32[4,4,1152]{2,1,0:T(4,128)} %shard_map.60), calls=%async_computation.1 | async-start | bytes 147456 | tf_op jit(solution)/shard_map/all_to_all | solution.py:28
  8.7 13.3 %collective-permute-start = (f32[2,1024]{1,0:T(2,128)S(1)}, f32[2,1024]{1,0:T(2,128)S(1)}, u32[]{:S(2)}, u32[]{:S(2)}) collective-permute-start(f32[2,1024]{1,0:T(2,128)S(1)} %copy-done.2), channel_id=1, source_target_pairs={{0,16},{16,0},{1,17},{17,1},{2,18},{18,2},{3,19},{19,3},{4,20},{20... | collective-permute-start | bytes 24584 | tf_op jit(solution)/shard_map/ppermute | solution.py:32
  22.0 1.6 collective-permute-done.theirs
  25.0 7.5 %all-to-all-start = ((f32[16,4,1152]{2,1,0:T(4,128)}), f32[16,4,1152]{2,1,0:T(4,128)S(1)}, u32[]{:S(2)}, u32[]{:S(2)}) async-start(f32[16,4,1152]{2,1,0:T(4,128)} %shard_map.59), calls=%async_computation | async-start | bytes 589824 | tf_op jit(solution)/shard_map/all_to_all | solution.py:28
  32.5 1.9 %all-gather = f32[8,4,1152]{2,1,0:T(4,128)S(1)} all-gather(f32[4,4,1152]{2,1,0:T(4,128)S(1)} %all-to-all-done.1), channel_id=2, replica_groups=mesh['z4'=2,'z2'=2,'z1'=2,'core'=2,'zh'=2,'y'=4,'x'=4] {'core'}, dimensions={0}, use_global_device_ids=true | all-gather | bytes 221184 | tf_op jit(solution)/shard_map/all_gather | solution.py:263
  34.4 5.6 %all-to-all-done.w0 = f32[16,4,1152]{2,1,0:T(4,128)S(1)} async-done(((f32[16,4,1152]{2,1,0:T(4,128)}), f32[16,4,1152]{2,1,0:T(4,128)S(1)}, u32[]{:S(2)}, u32[]{:S(2)}) %all-to-all-start) | async-done | bytes 294944 | tf_op jit(solution)/shard_map/all_to_all | solution.py:28
  40.0 1.7 shard_map.61
  41.8 5.0 %all-to-all-start.2 = ((f32[8,8,640]{2,1,0:T(8,128)}), f32[8,8,640]{2,1,0:T(8,128)S(1)}, u32[]{:S(2)}, u32[]{:S(2)}) async-start(f32[8,8,640]{2,1,0:T(8,128)} %get-tuple-element.18), calls=%async_computation.2 | async-start | bytes 327680 | tf_op jit(solution)/shard_map/all_to_all | solution.py:28
  46.8 8.6 %collective-permute-start.1 = (f32[2,4,4,1152]{3,2,1,0:T(4,128)S(1)}, f32[2,4,4,1152]{3,2,1,0:T(4,128)S(1)}, u32[]{:S(2)}, u32[]{:S(2)}) collective-permute-start(f32[2,4,4,1152]{3,2,1,0:T(4,128)S(1)} %bitcast.9), channel_id=1, source_target_pairs={{0,256},{256,0},{1,257},{257,1},{2,258},{258,2},{3,259},{259,3},{4... | collective-permute-start | bytes 442376 | tf_op jit(solution)/shard_map/ppermute | solution.py:32
  55.5 11.3 %collective-permute-start.2 = (f32[4,8,384]{2,1,0:T(8,128)S(1)}, f32[4,8,384]{2,1,0:T(8,128)S(1)}, u32[]{:S(2)}, u32[]{:S(2)}) collective-permute-start(f32[4,8,384]{2,1,0:T(8,128)S(1)} %shard_map.63.mine), channel_id=1, source_target_pairs={{0,256},{256,0},{1,257},{257,1},{2,258},{258,2},{3,259},{259,3},{4... | collective-permute-start | bytes 147464 | tf_op jit(solution)/shard_map/ppermute | solution.py:32
  66.8 6.0 %collective-permute-done.1.theirs = f32[2,4,4,1152]{3,2,1,0:T(4,128)S(1)} collective-permute-done((f32[2,4,4,1152]{3,2,1,0:T(4,128)S(1)}, f32[2,4,4,1152]{3,2,1,0:T(4,128)S(1)}, u32[]{:S(2)}, u32[]{:S(2)}) %collective-permute-start.1) | collective-permute-done | bytes 147488 | tf_op jit(solution)/shard_map/ppermute | solution.py:32
  73.8 9.7 %all_to_all.45 = f32[4,4,8,256]{3,2,1,0:T(8,128)S(1)} all-to-all(f32[4,4,8,256]{3,2,1,0:T(8,128)S(1)} %shard_map.64), channel_id=1, replica_groups=mesh['z4'=2,'z2'=2,'z1'=2,'core'=2,'zh'=2,'y'=4,'x'=4] {'z2','z1'}, dimensions={0} | all-to-all | bytes 262144 | tf_op jit(solution)/shard_map/all_to_all | solution.py:28
  83.5 2.0 %all-gather.1 = f32[8,4,8,256]{3,2,1,0:T(8,128)S(1)} all-gather(f32[4,4,8,256]{3,2,1,0:T(8,128)S(1)} %all_to_all.45), channel_id=3, replica_groups=mesh['z4'=2,'z2'=2,'z1'=2,'core'=2,'zh'=2,'y'=4,'x'=4] {'core'}, dimensions={0}, use_global_device_ids=true | all-gather | bytes 393216 | tf_op jit(solution)/shard_map/all_gather | solution.py:281
  86.8 11.9 %all_to_all.46.got = f32[16,16,256]{2,1,0:T(8,128)S(1)} all-to-all(f32[16,16,256]{2,1,0:T(8,128)S(1)} %get-tuple-element.20), channel_id=1, replica_groups=mesh['z4'=2,'z2'=2,'z1'=2,'core'=2,'zh'=2,'y'=4,'x'=4] {'y','x'}, dimensions={0} | all-to-all | bytes 524288 | tf_op jit(solution)/shard_map/all_to_all | solution.py:28
  98.8 10.3 %collective-permute-start.3 = (f32[4,8,256]{2,1,0:T(8,128)S(1)}, f32[4,8,256]{2,1,0:T(8,128)S(1)}, u32[]{:S(2)}, u32[]{:S(2)}) collective-permute-start(f32[4,8,256]{2,1,0:T(8,128)S(1)} %shard_map.66.mine), channel_id=1, source_target_pairs={{0,16},{16,0},{1,17},{17,1},{2,18},{18,2},{3,19},{19,3},{4,20},{20... | collective-permute-start | bytes 98312 | tf_op jit(solution)/shard_map/ppermute | solution.py:32
  109.1 4.2 %collective-permute-done.3.theirs = f32[4,8,256]{2,1,0:T(8,128)S(1)} collective-permute-done((f32[4,8,256]{2,1,0:T(8,128)S(1)}, f32[4,8,256]{2,1,0:T(8,128)S(1)}, u32[]{:S(2)}, u32[]{:S(2)}) %collective-permute-start.3) | collective-permute-done | bytes 32800 | tf_op jit(solution)/shard_map/ppermute | solution.py:32
  113.3 10.9 %all_to_all.47.w_got = f32[16,8,256]{2,1,0:T(8,128)S(1)} all-to-all(f32[16,8,256]{2,1,0:T(8,128)S(1)} %get-tuple-element.23), channel_id=1, replica_groups=mesh['z4'=2,'z2'=2,'z1'=2,'core'=2,'zh'=2,'y'=4,'x'=4] {'y','x'}, dimensions={0} | all-to-all | bytes 262144 | tf_op jit(solution)/shard_map/all_to_all | solution.py:28
  125.3 9.9 %all_to_all.48.got = f32[8,8,640]{2,1,0:T(8,128)S(1)} all-to-all(f32[8,8,640]{2,1,0:T(8,128)S(1)} %get-tuple-element.24), channel_id=1, replica_groups=mesh['z4'=2,'z2'=2,'z1'=2,'core'=2,'zh'=2,'y'=4,'x'=4] {'z2','z1','core'}, dimensions={0} | all-to-all | bytes 327680 | tf_op jit(solution)/shard_map/all_to_all | solution.py:28
  135.3 8.8 %collective-permute-start.4 = (f32[4,8,384]{2,1,0:T(8,128)S(1)}, f32[4,8,384]{2,1,0:T(8,128)S(1)}, u32[]{:S(2)}, u32[]{:S(2)}) collective-permute-start(f32[4,8,384]{2,1,0:T(8,128)S(1)} %shard_map.69.mine), channel_id=1, source_target_pairs={{0,256},{256,0},{1,257},{257,1},{2,258},{258,2},{3,259},{259,3},{4... | collective-permute-start | bytes 147464 | tf_op jit(solution)/shard_map/ppermute | solution.py:32
  144.1 4.3 %collective-permute-done.4.theirs = f32[4,8,384]{2,1,0:T(8,128)S(1)} collective-permute-done((f32[4,8,384]{2,1,0:T(8,128)S(1)}, f32[4,8,384]{2,1,0:T(8,128)S(1)}, u32[]{:S(2)}, u32[]{:S(2)}) %collective-permute-start.4) | collective-permute-done | bytes 49184 | tf_op jit(solution)/shard_map/ppermute | solution.py:32
  148.6 9.1 %all_to_all.49.h_got = f32[8,16,256]{2,1,0:T(8,128)S(1)} all-to-all(f32[8,16,256]{2,1,0:T(8,128)S(1)} %get-tuple-element.25), channel_id=1, replica_groups=mesh['z4'=2,'z2'=2,'z1'=2,'core'=2,'zh'=2,'y'=4,'x'=4] {'z2','z1','core'}, dimensions={0} | all-to-all | bytes 262144 | tf_op jit(solution)/shard_map/all_to_all | solution.py:28
  159.0 11.8 %all_to_all.50.got = f32[16,16,256]{2,1,0:T(8,128)S(1)} all-to-all(f32[16,16,256]{2,1,0:T(8,128)S(1)} %shard_map.71), channel_id=1, replica_groups=mesh['z4'=2,'z2'=2,'z1'=2,'core'=2,'zh'=2,'y'=4,'x'=4] {'y','x'}, dimensions={0} | all-to-all | bytes 524288 | tf_op jit(solution)/shard_map/all_to_all | solution.py:28
  170.9 9.2 %collective-permute-start.5 = (f32[4,8,256]{2,1,0:T(8,128)S(1)}, f32[4,8,256]{2,1,0:T(8,128)S(1)}, u32[]{:S(2)}, u32[]{:S(2)}) collective-permute-start(f32[4,8,256]{2,1,0:T(8,128)S(1)} %shard_map.72.mine), channel_id=1, source_target_pairs={{0,16},{16,0},{1,17},{17,1},{2,18},{18,2},{3,19},{19,3},{4,20},{20... | collective-permute-start | bytes 98312 | tf_op jit(solution)/shard_map/ppermute | solution.py:32
  180.7 4.7 %collective-permute-done.5.theirs = f32[4,8,256]{2,1,0:T(8,128)S(1)} collective-permute-done((f32[4,8,256]{2,1,0:T(8,128)S(1)}, f32[4,8,256]{2,1,0:T(8,128)S(1)}, u32[]{:S(2)}, u32[]{:S(2)}) %collective-permute-start.5) | collective-permute-done | bytes 32800 | tf_op jit(solution)/shard_map/ppermute | solution.py:32
  (25 shorter events, 10.0 us)
Async XLA Ops:
  0.6 0.7 copy-start.1
  2.7 6.0 %copy-start.2 = (f32[2,1024]{1,0:T(2,128)S(1)}, f32[2,1024]{1,0:T(2,128)}, u32[]{:S(2)}) copy-start(f32[2,1024]{1,0:T(2,128)} %mine.1) | copy-start | bytes 24580
  2.7 22.4 %all-to-all-start.1 = ((f32[4,4,1152]{2,1,0:T(4,128)}), f32[4,4,1152]{2,1,0:T(4,128)S(1)}, u32[]{:S(2)}, u32[]{:S(2)}) async-start(f32[4,4,1152]{2,1,0:T(4,128)} %shard_map.60), calls=%async_computation.1 | async-start | bytes 147456 | tf_op jit(solution)/shard_map/all_to_all | solution.py:28
  8.7 31.3 %copy-start = (f32[1,1,512,256]{3,2,1,0:T(8,128)S(1)}, f32[1,1,512,256]{3,2,1,0:T(8,128)}, u32[]{:S(2)}) copy-start(f32[1,1,512,256]{3,2,1,0:T(8,128)} %param.5) | copy-start | bytes 1572868
  8.7 14.9 %collective-permute-start = (f32[2,1024]{1,0:T(2,128)S(1)}, f32[2,1024]{1,0:T(2,128)S(1)}, u32[]{:S(2)}, u32[]{:S(2)}) collective-permute-start(f32[2,1024]{1,0:T(2,128)S(1)} %copy-done.2), channel_id=1, source_target_pairs={{0,16},{16,0},{1,17},{17,1},{2,18},{18,2},{3,19},{19,3},{4,20},{20... | collective-permute-start | bytes 24584 | tf_op jit(solution)/shard_map/ppermute | solution.py:32
  25.0 15.0 %all-to-all-start = ((f32[16,4,1152]{2,1,0:T(4,128)}), f32[16,4,1152]{2,1,0:T(4,128)S(1)}, u32[]{:S(2)}, u32[]{:S(2)}) async-start(f32[16,4,1152]{2,1,0:T(4,128)} %shard_map.59), calls=%async_computation | async-start | bytes 589824 | tf_op jit(solution)/shard_map/all_to_all | solution.py:28
  41.8 13.7 %all-to-all-start.2 = ((f32[8,8,640]{2,1,0:T(8,128)}), f32[8,8,640]{2,1,0:T(8,128)S(1)}, u32[]{:S(2)}, u32[]{:S(2)}) async-start(f32[8,8,640]{2,1,0:T(8,128)} %get-tuple-element.18), calls=%async_computation.2 | async-start | bytes 327680 | tf_op jit(solution)/shard_map/all_to_all | solution.py:28
  46.8 26.0 %collective-permute-start.1 = (f32[2,4,4,1152]{3,2,1,0:T(4,128)S(1)}, f32[2,4,4,1152]{3,2,1,0:T(4,128)S(1)}, u32[]{:S(2)}, u32[]{:S(2)}) collective-permute-start(f32[2,4,4,1152]{3,2,1,0:T(4,128)S(1)} %bitcast.9), channel_id=1, source_target_pairs={{0,256},{256,0},{1,257},{257,1},{2,258},{258,2},{3,259},{259,3},{4... | collective-permute-start | bytes 442376 | tf_op jit(solution)/shard_map/ppermute | solution.py:32
  55.5 18.1 %collective-permute-start.2 = (f32[4,8,384]{2,1,0:T(8,128)S(1)}, f32[4,8,384]{2,1,0:T(8,128)S(1)}, u32[]{:S(2)}, u32[]{:S(2)}) collective-permute-start(f32[4,8,384]{2,1,0:T(8,128)S(1)} %shard_map.63.mine), channel_id=1, source_target_pairs={{0,256},{256,0},{1,257},{257,1},{2,258},{258,2},{3,259},{259,3},{4... | collective-permute-start | bytes 147464 | tf_op jit(solution)/shard_map/ppermute | solution.py:32
  98.8 14.5 %collective-permute-start.3 = (f32[4,8,256]{2,1,0:T(8,128)S(1)}, f32[4,8,256]{2,1,0:T(8,128)S(1)}, u32[]{:S(2)}, u32[]{:S(2)}) collective-permute-start(f32[4,8,256]{2,1,0:T(8,128)S(1)} %shard_map.66.mine), channel_id=1, source_target_pairs={{0,16},{16,0},{1,17},{17,1},{2,18},{18,2},{3,19},{19,3},{4,20},{20... | collective-permute-start | bytes 98312 | tf_op jit(solution)/shard_map/ppermute | solution.py:32
  135.3 13.2 %collective-permute-start.4 = (f32[4,8,384]{2,1,0:T(8,128)S(1)}, f32[4,8,384]{2,1,0:T(8,128)S(1)}, u32[]{:S(2)}, u32[]{:S(2)}) collective-permute-start(f32[4,8,384]{2,1,0:T(8,128)S(1)} %shard_map.69.mine), channel_id=1, source_target_pairs={{0,256},{256,0},{1,257},{257,1},{2,258},{258,2},{3,259},{259,3},{4... | collective-permute-start | bytes 147464 | tf_op jit(solution)/shard_map/ppermute | solution.py:32
  170.9 14.5 %collective-permute-start.5 = (f32[4,8,256]{2,1,0:T(8,128)S(1)}, f32[4,8,256]{2,1,0:T(8,128)S(1)}, u32[]{:S(2)}, u32[]{:S(2)}) collective-permute-start(f32[4,8,256]{2,1,0:T(8,128)S(1)} %shard_map.72.mine), channel_id=1, source_target_pairs={{0,16},{16,0},{1,17},{17,1},{2,18},{18,2},{3,19},{19,3},{4,20},{20... | collective-permute-start | bytes 98312 | tf_op jit(solution)/shard_map/ppermute | solution.py:32

commit v6 on v4

--- a/solution.py
+++ b/solution.py
@@ -5,6 +5,7 @@
 from jax.experimental.pallas import tpu as pltpu
 from jax.sharding import Mesh, PartitionSpec as P
 
+
 RANK = 64
 BS = 256
 CAP = 2
@@ -13,8 +14,10 @@
 
 FINE = ("z4", "z2", "z1", "core", "zh", "y", "x")
 HALF = ("z2", "z1", "core")
+QUAD = ("z2", "z1")
 PLANE = ("y", "x")
 NH = 8
+NQ = 4
 COLS = NB * BS // NH
 NP = 16
 
@@ -36,20 +39,32 @@
     return hi, lo
 
 
-def product(a, b, dims):
+def product(a, b, dims=NN):
     dot = lambda x, y: lax.dot_general(x, y, dims, preferred_element_type=jnp.float32)
     return dot(a[0], b[0]) + (dot(a[0], b[1]) + dot(a[1], b[0]))
 
 
-def grams(left, values, dims, live):
+def grams(left, values, live):
     whole = halves(left)
     left = halves(left * live)
-    return product(left, halves(values), dims), product(left, whole, NT)
-
-
-def sums(left, right, values, dims, live):
-    upper, gram = grams(left, values, dims, live)
-    return upper, product(halves(gram), halves(right), NN)
+    return product(left, values), product(left, whole, NT)
+
+
+def sums(left, right, values, live):
+    upper, gram = grams(left, values, live)
+    return upper, product(halves(gram), halves(right))
+
+
+def prepare_kernel(values, w, parts, turned, w_mine):
+    w_mine[...] = w[...]
+    for j in range(CAP):
+        block = values[j * BS : (j + 1) * BS, :]
+        parts[j, 0], parts[j, 1] = halves(block)
+        turned[j, 0], turned[j, 1] = halves(block.T)
+
+
+def both_of(parts, j):
+    return parts[j, 0], parts[j, 1]
 
 
 def live_of(blk, j):
@@ -86,7 +101,7 @@
         at = pl.multiple_of(block_of(blk, 0, j) * BS, BS)
         for q in range(NP):
             w_slots[j, 4 * q : 4 * q + 4, :] = w0[q, :, pl.ds(at, BS)]
-        upper, gram = grams(w_slots[j], values[j * BS : (j + 1) * BS, :], NN, live_of(blk, j))
+        upper, gram = grams(w_slots[j], both_of(values, j), live_of(blk, j))
         gram = jnp.concatenate([gram[:32], gram[32:]], axis=1)
         for side in range(2):
             q = 2 * block_of(blk, 1, j) + side
@@ -124,13 +139,13 @@
     for k in range(16):
         pairs += [low[2 * k : 2 * k + 2], high[2 * k : 2 * k + 2]]
     old = jnp.concatenate(pairs, axis=0)
-    new = old * total[:64] / product(halves(gram), halves(old), NN)
-    for q in range(NH):
+    new = old * total[:64] / product(halves(gram), halves(old))
+    for q in range(NQ):
         out[q] = new
 
 
 def whole_block(h_all, b):
-    return jnp.concatenate([h_all[2 * b], h_all[2 * b + 1]], axis=1)
+    return jnp.concatenate([h_all[0, b], h_all[1, b]], axis=1)
 
 
 def send_w(out, j, upper, lower):
@@ -142,13 +157,13 @@
 def w1_terms_kernel(blk, h_all, w_slots, values, out):
     for j in range(CAP):
         h_slot = whole_block(h_all, block_of(blk, 1, j))
-        send_w(out, j, *sums(h_slot, w_slots[j], values[j * BS : (j + 1) * BS, :], NT, live_of(blk, j)))
+        send_w(out, j, *sums(h_slot, w_slots[j], both_of(values, j), live_of(blk, j)))
 
 
 def w2_terms_kernel(blk, h_got, w_slots, values, out):
     for j in range(CAP):
         h_slot = h_got[:, 8 * j : 8 * j + 8, :].reshape(RANK, BS)
-        send_w(out, j, *sums(h_slot, w_slots[j], values[j * BS : (j + 1) * BS, :], NT, live_of(blk, j)))
+        send_w(out, j, *sums(h_slot, w_slots[j], both_of(values, j), live_of(blk, j)))
 
 
 def w_slot(got, j):
@@ -159,7 +174,7 @@
     both = []
     for j in range(CAP):
         w_slots[j] = w_slot(w_got, j)
-        upper, gram = grams(w_slots[j], values[j * BS : (j + 1) * BS, :], NN, live_of(blk, j))
+        upper, gram = grams(w_slots[j], both_of(values, j), live_of(blk, j))
         both.append(gram)
         for q in range(NH):
             out[q, :, BS * j : BS * (j + 1)] = upper[8 * q : 8 * q + 8, :]
@@ -193,7 +208,7 @@
         rest = lax.dot_general(gram, block[1], NN, preferred_element_type=jnp.float32)
         lower = most[:8] + (most[8:] + rest[:8])
         at = pl.multiple_of(8 * half, 8)
-        own = jnp.concatenate([h_all[2 * b, pl.ds(at, 8), :], h_all[2 * b + 1, pl.ds(at, 8), :]], axis=1)
+        own = jnp.concatenate([h_all[0, b, pl.ds(at, 8), :], h_all[1, b, pl.ds(at, 8), :]], axis=1)
         rows = own * total[:, :BS] / lower
         new[b] = rows
         for high in range(2):
@@ -235,16 +250,16 @@
         final[:, b * BS : (b + 1) * BS] = jnp.where(first, new[b, 0:2, :], new[b, 2:4, :])
 
 
-def call(body, scalars, arrays, outs, tables=(), scratch=(), name=None):
+def call(body, scalars, arrays, outs, tables=(), scratch=(), last=False, dtypes=None):
     smem = pl.BlockSpec(memory_space=pltpu.SMEM)
     vmem = pl.BlockSpec(memory_space=pltpu.VMEM)
+    kind = jax.ShapeDtypeStruct if last else pltpu.VMEM
     return pl.pallas_call(
         body,
         in_specs=[smem] * len(scalars) + [vmem] * len(arrays),
         out_specs=[vmem] * len(outs) + [smem] * len(tables),
-        out_shape=[pltpu.VMEM(s, jnp.float32) for s in outs] + [pltpu.SMEM(s, jnp.int32) for s in tables],
+        out_shape=[kind(*s) for s in zip(outs, dtypes or [jnp.float32] * len(outs))] + [pltpu.SMEM(s, jnp.int32) for s in tables],
         scratch_shapes=[pltpu.VMEM(s, jnp.float32) for s in scratch],
-        name=name,
     )(
         *(pltpu.with_memory_space_constraint(a, pltpu.SMEM) for a in scalars),
         *(pltpu.with_memory_space_constraint(a, pltpu.VMEM) for a in arrays),
@@ -253,11 +268,17 @@
 
 def per_device(blocks, observed, w_factor, h_factor):
     blk = blocks[0, 0]
-    values = observed[0, 0]
     wide = NB * BS + TAB
 
     w_other = swap(w_factor, "zh")
-    (w_pair,) = call(w_pair_kernel, (blk,), (w_factor, w_other), [(NP, 4, wide)], scratch=[(4, wide)], name="w_pair")
+    values, turned, w_mine = call(
+        prepare_kernel,
+        (),
+        (observed[0, 0], w_factor),
+        [(CAP, 2, BS, BS), (CAP, 2, BS, BS), w_factor.shape],
+        dtypes=[jnp.bfloat16, jnp.bfloat16, jnp.float32],
+    )
+    (w_pair,) = call(w_pair_kernel, (blk,), (w_mine, w_other), [(NP, 4, wide)], scratch=[(4, wide)])
     w_got = exchange(w_pair, PLANE)
 
     w_slots, w_own, sent, rows = call(
@@ -266,46 +287,34 @@
         (w_got, h_factor, values),
         [(CAP, RANK, BS), (NB, 4, BS), (NH, 104, COLS)],
         tables=[(NP * CAP,)],
-        name="h1_terms",
     )
     got = exchange(sent, HALF)
-    mine, cols = call(h1_collect_kernel, (), (got,), [(128, COLS)], tables=[(NH * CAP,)], name="h1_collect")
+    mine, cols = call(h1_collect_kernel, (), (got,), [(128, COLS)], tables=[(NH * CAP,)])
     theirs = swap(mine, "z4")
-    (out,) = call(h1_update_kernel, (), (mine, theirs), [(NH, RANK, COLS)], name="h1_update")
-    h_all = exchange(out, HALF)
-
-    (sent,) = call(w1_terms_kernel, (blk,), (h_all, w_slots, values), [(NP, 16, BS)], name="w1_terms")
+    (out,) = call(h1_update_kernel, (), (mine, theirs), [(NQ, RANK, COLS)])
+    h_all = lax.all_gather(exchange(out, QUAD), "core", axis=0)
+
+    (sent,) = call(w1_terms_kernel, (blk,), (h_all, w_slots, turned), [(NP, 16, BS)])
     got = exchange(sent, PLANE)
-    (mine,) = call(collect_kernel, (rows,), (got,), [(NB, 8, BS)], name="w1_collect")
+    (mine,) = call(collect_kernel, (rows,), (got,), [(NB, 8, BS)])
     theirs = swap(mine, "zh")
-    w_own, out = call(
-        update_kernel, (rows,), (w_own, mine, theirs), [(NB, 4, BS), (NP, 8, BS)], name="w1_update"
-    )
+    w_own, out = call(update_kernel, (rows,), (w_own, mine, theirs), [(NB, 4, BS), (NP, 8, BS)])
     w_got = exchange(out, PLANE)
 
-    w_slots, sent = call(
-        h2_terms_kernel, (blk,), (w_got, values), [(CAP, RANK, BS), (NH, 8, CAP * (BS + RANK))], name="h2_terms"
-    )
+    w_slots, sent = call(h2_terms_kernel, (blk,), (w_got, values), [(CAP, RANK, BS), (NH, 8, CAP * (BS + RANK))])
     got = exchange(sent, HALF)
-    (mine,) = call(h2_collect_kernel, (cols,), (got,), [(NB, 8, BS + CAP * RANK)], name="h2_collect")
+    (mine,) = call(h2_collect_kernel, (cols,), (got,), [(NB, 8, BS + CAP * RANK)])
     theirs = swap(mine, "z4")
     h_final, out = call(
-        h2_update_kernel,
-        (cols,),
-        (h_all, mine, theirs),
-        [(4, NB * BS), (NH, 16, BS)],
-        scratch=[(NB, 8, BS)],
-        name="h2_update",
+        h2_update_kernel, (cols,), (h_all, mine, theirs), [(4, NB * BS), (NH, 16, BS)], scratch=[(NB, 8, BS)]
     )
     h_got = exchange(out, HALF)
 
-    (sent,) = call(w2_terms_kernel, (blk,), (h_got, w_slots, values), [(NP, 16, BS)], name="w2_terms")
+    (sent,) = call(w2_terms_kernel, (blk,), (h_got, w_slots, turned), [(NP, 16, BS)])
     got = exchange(sent, PLANE)
-    (mine,) = call(collect_kernel, (rows,), (got,), [(NB, 8, BS)], name="w2_collect")
+    (mine,) = call(collect_kernel, (rows,), (got,), [(NB, 8, BS)])
     theirs = swap(mine, "zh")
-    (w_final,) = call(
-        last_w_kernel, (), (w_own, mine, theirs), [(2, NB * BS)], scratch=[(NB, 4, BS)], name="w2_update"
-    )
+    (w_final,) = call(last_w_kernel, (), (w_own, mine, theirs), [(2, NB * BS)], scratch=[(NB, 4, BS)], last=True)
     return w_final, h_final
 
 

time: 179 us -> 176 us (0.983)
  the two profiles are of different devices: /device:TPU:32 before, /device:TPU:2 now
where the time goes in v6:
time: 176 us
  blocking collectives  95.3 us (54%)
  starting transfers between devices  55.3 us (31%)
  waiting for transfers between devices  14.8 us (8%)
  Pallas kernels  7.11 us (4%)
  local copies, waits for them, and re-layouts  2.35 us (1%)
    all_to_all x8, blocking collectives, exchange(): return lax.all_to_all(x, axes, split_axis=0, concat_axis=0, tiled=True)  93.3 us
    ppermute x5, starting transfers between devices, swap(): return lax.ppermute(x, axis, [(0, 1), (1, 0)])  55.3 us
    ppermute x5, waiting for transfers between devices, swap(): return lax.ppermute(x, axis, [(0, 1), (1, 0)])  14.8 us
    pallas_call x14, Pallas kernels, call(): pl.pallas_call(body, in_specs=[smem] * len(scalars) + [vmem] * len(arrays...  7.11 us
  transfers between devices with their start and end apart: 5, of which 4 were waited for; matrix products, arithmetic and copies ran while one was open for 0% of the time, Pallas kernels for 0%

profile of v6, /device:TPU:2, one launch (start us, length us, event | category | flops | bytes accessed | tf_op | source)
XLA Modules:
  0.0 175.6 jit_solution(7626954688631334427)
XLA Ops:
  0.6 15.7 %collective-permute-start = (f32[2,1024]{1,0:T(2,128)}, f32[2,1024]{1,0:T(2,128)S(1)}, u32[]{:S(2)}, u32[]{:S(2)}) collective-permute-start(f32[2,1024]{1,0:T(2,128)} %w.1), channel_id=1, source_target_pairs={{0,16},{16,0},{1,17},{17,1},{2,18},{18,2},{3,19},{19,3},{4,20},{20... | collective-permute-start | bytes 24584 | tf_op jit(solution)/shard_map/ppermute | solution.py:33
  16.4 1.0 copy-done
  18.3 0.7 shard_map.60
  19.1 14.8 %all_to_all.40.w0 = f32[16,4,1152]{2,1,0:T(4,128)S(1)} all-to-all(f32[16,4,1152]{2,1,0:T(4,128)S(1)} %shard_map.60), channel_id=1, replica_groups=mesh['z4'=2,'z2'=2,'z1'=2,'core'=2,'zh'=2,'y'=4,'x'=4] {'y','x'}, dimensions={0} | all-to-all | bytes 589824 | tf_op jit(solution)/shard_map/all_to_all | solution.py:29
  33.8 1.1 shard_map.61
  34.9 16.2 %all_to_all.41.got = f32[8,104,128]{2,1,0:T(8,128)S(1)} all-to-all(f32[8,104,128]{2,1,0:T(8,128)S(1)} %get-tuple-element.21), channel_id=1, replica_groups=mesh['z4'=2,'z2'=2,'z1'=2,'core'=2,'zh'=2,'y'=4,'x'=4] {'z2','z1','core'}, dimensions={0} | all-to-all | bytes 851968 | tf_op jit(solution)/shard_map/all_to_all | solution.py:29
  51.3 8.6 %collective-permute-start.1 = (f32[128,128]{1,0:T(8,128)S(1)}, f32[128,128]{1,0:T(8,128)S(1)}, u32[]{:S(2)}, u32[]{:S(2)}) collective-permute-start(f32[128,128]{1,0:T(8,128)S(1)} %get-tuple-element.22.mine), channel_id=1, source_target_pairs={{0,256},{256,0},{1,257},{257,1},{2,258},{258,2},{3,259},{259,3},{4... | collective-permute-start | bytes 196616 | tf_op jit(solution)/shard_map/ppermute | solution.py:33
  59.9 5.5 %collective-permute-done.1.theirs = f32[128,128]{1,0:T(8,128)S(1)} collective-permute-done((f32[128,128]{1,0:T(8,128)S(1)}, f32[128,128]{1,0:T(8,128)S(1)}, u32[]{:S(2)}, u32[]{:S(2)}) %collective-permute-start.1) | collective-permute-done | bytes 65568 | tf_op jit(solution)/shard_map/ppermute | solution.py:33
  65.6 8.8 %all_to_all.42 = f32[4,64,128]{2,1,0:T(8,128)S(1)} all-to-all(f32[4,64,128]{2,1,0:T(8,128)S(1)} %shard_map.63), channel_id=1, replica_groups=mesh['z4'=2,'z2'=2,'z1'=2,'core'=2,'zh'=2,'y'=4,'x'=4] {'z2','z1'}, dimensions={0} | all-to-all | bytes 262144 | tf_op jit(solution)/shard_map/all_to_all | solution.py:29
  74.3 2.0 %all-gather = f32[8,64,128]{2,1,0:T(8,128)S(1)} all-gather(f32[4,64,128]{2,1,0:T(8,128)S(1)} %all_to_all.42), channel_id=2, replica_groups=mesh['z4'=2,'z2'=2,'z1'=2,'core'=2,'zh'=2,'y'=4,'x'=4] {'core'}, dimensions={0}, use_global_device_ids=true | all-gather | bytes 393216 | tf_op jit(solution)/shard_map/all_gather | solution.py:295
  76.3 1.3 shard_map.64
  77.6 11.9 %all_to_all.43.got = f32[16,16,256]{2,1,0:T(8,128)S(1)} all-to-all(f32[16,16,256]{2,1,0:T(8,128)S(1)} %shard_map.64), channel_id=1, replica_groups=mesh['z4'=2,'z2'=2,'z1'=2,'core'=2,'zh'=2,'y'=4,'x'=4] {'y','x'}, dimensions={0} | all-to-all | bytes 524288 | tf_op jit(solution)/shard_map/all_to_all | solution.py:29
  89.6 11.5 %collective-permute-start.2 = (f32[4,8,256]{2,1,0:T(8,128)S(1)}, f32[4,8,256]{2,1,0:T(8,128)S(1)}, u32[]{:S(2)}, u32[]{:S(2)}) collective-permute-start(f32[4,8,256]{2,1,0:T(8,128)S(1)} %shard_map.65.mine), channel_id=1, source_target_pairs={{0,16},{16,0},{1,17},{17,1},{2,18},{18,2},{3,19},{19,3},{4,20},{20... | collective-permute-start | bytes 98312 | tf_op jit(solution)/shard_map/ppermute | solution.py:33
  101.0 3.1 %collective-permute-done.2.theirs = f32[4,8,256]{2,1,0:T(8,128)S(1)} collective-permute-done((f32[4,8,256]{2,1,0:T(8,128)S(1)}, f32[4,8,256]{2,1,0:T(8,128)S(1)}, u32[]{:S(2)}, u32[]{:S(2)}) %collective-permute-start.2) | collective-permute-done | bytes 32800 | tf_op jit(solution)/shard_map/ppermute | solution.py:33
  104.1 10.9 %all_to_all.44.w_got = f32[16,8,256]{2,1,0:T(8,128)S(1)} all-to-all(f32[16,8,256]{2,1,0:T(8,128)S(1)} %get-tuple-element.27), channel_id=1, replica_groups=mesh['z4'=2,'z2'=2,'z1'=2,'core'=2,'zh'=2,'y'=4,'x'=4] {'y','x'}, dimensions={0} | all-to-all | bytes 262144 | tf_op jit(solution)/shard_map/all_to_all | solution.py:29
  115.0 1.0 shard_map.67
  116.1 9.9 %all_to_all.45.got = f32[8,8,640]{2,1,0:T(8,128)S(1)} all-to-all(f32[8,8,640]{2,1,0:T(8,128)S(1)} %get-tuple-element.28), channel_id=1, replica_groups=mesh['z4'=2,'z2'=2,'z1'=2,'core'=2,'zh'=2,'y'=4,'x'=4] {'z2','z1','core'}, dimensions={0} | all-to-all | bytes 327680 | tf_op jit(solution)/shard_map/all_to_all | solution.py:29
  126.0 7.5 %collective-permute-start.3 = (f32[4,8,384]{2,1,0:T(8,128)S(1)}, f32[4,8,384]{2,1,0:T(8,128)S(1)}, u32[]{:S(2)}, u32[]{:S(2)}) collective-permute-start(f32[4,8,384]{2,1,0:T(8,128)S(1)} %shard_map.68.mine), channel_id=1, source_target_pairs={{0,256},{256,0},{1,257},{257,1},{2,258},{258,2},{3,259},{259,3},{4... | collective-permute-start | bytes 147464 | tf_op jit(solution)/shard_map/ppermute | solution.py:33
  133.5 4.4 %collective-permute-done.3.theirs = f32[4,8,384]{2,1,0:T(8,128)S(1)} collective-permute-done((f32[4,8,384]{2,1,0:T(8,128)S(1)}, f32[4,8,384]{2,1,0:T(8,128)S(1)}, u32[]{:S(2)}, u32[]{:S(2)}) %collective-permute-start.3) | collective-permute-done | bytes 49184 | tf_op jit(solution)/shard_map/ppermute | solution.py:33
  138.1 9.1 %all_to_all.46.h_got = f32[8,16,256]{2,1,0:T(8,128)S(1)} all-to-all(f32[8,16,256]{2,1,0:T(8,128)S(1)} %get-tuple-element.29), channel_id=1, replica_groups=mesh['z4'=2,'z2'=2,'z1'=2,'core'=2,'zh'=2,'y'=4,'x'=4] {'z2','z1','core'}, dimensions={0} | all-to-all | bytes 262144 | tf_op jit(solution)/shard_map/all_to_all | solution.py:29
  147.3 1.2 shard_map.70
  148.5 11.8 %all_to_all.47.got = f32[16,16,256]{2,1,0:T(8,128)S(1)} all-to-all(f32[16,16,256]{2,1,0:T(8,128)S(1)} %shard_map.70), channel_id=1, replica_groups=mesh['z4'=2,'z2'=2,'z1'=2,'core'=2,'zh'=2,'y'=4,'x'=4] {'y','x'}, dimensions={0} | all-to-all | bytes 524288 | tf_op jit(solution)/shard_map/all_to_all | solution.py:29
  160.4 12.0 %collective-permute-start.4 = (f32[4,8,256]{2,1,0:T(8,128)S(1)}, f32[4,8,256]{2,1,0:T(8,128)S(1)}, u32[]{:S(2)}, u32[]{:S(2)}) collective-permute-start(f32[4,8,256]{2,1,0:T(8,128)S(1)} %shard_map.71.mine), channel_id=1, source_target_pairs={{0,16},{16,0},{1,17},{17,1},{2,18},{18,2},{3,19},{19,3},{4,20},{20... | collective-permute-start | bytes 98312 | tf_op jit(solution)/shard_map/ppermute | solution.py:33
  173.1 1.9 %collective-permute-done.4.theirs = f32[4,8,256]{2,1,0:T(8,128)S(1)} collective-permute-done((f32[4,8,256]{2,1,0:T(8,128)S(1)}, f32[4,8,256]{2,1,0:T(8,128)S(1)}, u32[]{:S(2)}, u32[]{:S(2)}) %collective-permute-start.4) | collective-permute-done | bytes 32800 | tf_op jit(solution)/shard_map/ppermute | solution.py:33
  (16 shorter events, 3.1 us)
Async XLA Ops:
  0.6 17.7 %collective-permute-start = (f32[2,1024]{1,0:T(2,128)}, f32[2,1024]{1,0:T(2,128)S(1)}, u32[]{:S(2)}, u32[]{:S(2)}) collective-permute-start(f32[2,1024]{1,0:T(2,128)} %w.1), channel_id=1, source_target_pairs={{0,16},{16,0},{1,17},{17,1},{2,18},{18,2},{3,19},{19,3},{4,20},{20... | collective-permute-start | bytes 24584 | tf_op jit(solution)/shard_map/ppermute | solution.py:33
  16.4 1.0 copy-start
  17.4 0.7 copy-start.2
  19.1 14.8 %copy-start.1 = (f32[4,1024]{1,0:T(4,128)S(1)}, f32[4,1024]{1,0:T(4,128)}, u32[]{:S(2)}) copy-start(f32[4,1024]{1,0:T(4,128)} %h.1) | copy-start | bytes 49156
  51.3 14.0 %collective-permute-start.1 = (f32[128,128]{1,0:T(8,128)S(1)}, f32[128,128]{1,0:T(8,128)S(1)}, u32[]{:S(2)}, u32[]{:S(2)}) collective-permute-start(f32[128,128]{1,0:T(8,128)S(1)} %get-tuple-element.22.mine), channel_id=1, source_target_pairs={{0,256},{256,0},{1,257},{257,1},{2,258},{258,2},{3,259},{259,3},{4... | collective-permute-start | bytes 196616 | tf_op jit(solution)/shard_map/ppermute | solution.py:33
  89.6 14.5 %collective-permute-start.2 = (f32[4,8,256]{2,1,0:T(8,128)S(1)}, f32[4,8,256]{2,1,0:T(8,128)S(1)}, u32[]{:S(2)}, u32[]{:S(2)}) collective-permute-start(f32[4,8,256]{2,1,0:T(8,128)S(1)} %shard_map.65.mine), channel_id=1, source_target_pairs={{0,16},{16,0},{1,17},{17,1},{2,18},{18,2},{3,19},{19,3},{4,20},{20... | collective-permute-start | bytes 98312 | tf_op jit(solution)/shard_map/ppermute | solution.py:33
  126.0 11.9 %collective-permute-start.3 = (f32[4,8,384]{2,1,0:T(8,128)S(1)}, f32[4,8,384]{2,1,0:T(8,128)S(1)}, u32[]{:S(2)}, u32[]{:S(2)}) collective-permute-start(f32[4,8,384]{2,1,0:T(8,128)S(1)} %shard_map.68.mine), channel_id=1, source_target_pairs={{0,256},{256,0},{1,257},{257,1},{2,258},{258,2},{3,259},{259,3},{4... | collective-permute-start | bytes 147464 | tf_op jit(solution)/shard_map/ppermute | solution.py:33
  160.4 14.5 %collective-permute-start.4 = (f32[4,8,256]{2,1,0:T(8,128)S(1)}, f32[4,8,256]{2,1,0:T(8,128)S(1)}, u32[]{:S(2)}, u32[]{:S(2)}) collective-permute-start(f32[4,8,256]{2,1,0:T(8,128)S(1)} %shard_map.71.mine), channel_id=1, source_target_pairs={{0,16},{16,0},{1,17},{17,1},{2,18},{18,2},{3,19},{19,3},{4,20},{20... | collective-permute-start | bytes 98312 | tf_op jit(solution)/shard_map/ppermute | solution.py:33

commit v7 on v6

--- a/solution.py
+++ b/solution.py
@@ -55,7 +55,10 @@
     return upper, product(halves(gram), halves(right))
 
 
-def prepare_kernel(values, w, parts, turned, w_mine):
+def prepare_kernel(blk, values, w, parts, turned, w_mine, listed):
+    for d in range(2):
+        for j in range(CAP):
+            listed[CAP * d + j] = blk[d, j]
     w_mine[...] = w[...]
     for j in range(CAP):
         block = values[j * BS : (j + 1) * BS, :]
@@ -68,17 +71,17 @@
 
 
 def live_of(blk, j):
-    return jnp.where(blk[0, j] >= 0, 1.0, 0.0).astype(jnp.float32)
+    return jnp.where(blk[j] >= 0, 1.0, 0.0).astype(jnp.float32)
 
 
 def block_of(blk, d, j):
-    return jnp.maximum(blk[d, j], 0)
+    return jnp.maximum(blk[CAP * d + j], 0)
 
 
 def with_list(rows, blk, d, lists):
     lane = lax.broadcasted_iota(jnp.int32, (rows.shape[0], TAB), 1)
     lists[:, : NB * BS] = rows
-    lists[:, NB * BS :] = jnp.where(lane == 0, blk[d, 0], blk[d, 1]).astype(jnp.float32)
+    lists[:, NB * BS :] = jnp.where(lane == 0, blk[CAP * d], blk[CAP * d + 1]).astype(jnp.float32)
 
 
 def w_pair_kernel(blk, mine, theirs, out, message):
@@ -108,7 +111,7 @@
             out[q, :64, :] = out[q, :64, :] + upper[:, COLS * side : COLS * (side + 1)]
             out[q, 64:96, :] = out[q, 64:96, :] + gram
     lane = lax.broadcasted_iota(jnp.int32, (4, COLS), 1)
-    listed = jnp.where(lane == 0, blk[1, 0], blk[1, 1]).astype(jnp.float32)
+    listed = jnp.where(lane == 0, blk[CAP], blk[CAP + 1]).astype(jnp.float32)
     for q in range(NH):
         out[q, 96:100, :] = h[:, COLS * q : COLS * (q + 1)]
         out[q, 100:104, :] = listed
@@ -267,16 +270,16 @@
 
 
 def per_device(blocks, observed, w_factor, h_factor):
-    blk = blocks[0, 0]
     wide = NB * BS + TAB
 
     w_other = swap(w_factor, "zh")
-    values, turned, w_mine = call(
+    values, turned, w_mine, blk = call(
         prepare_kernel,
-        (),
+        (blocks[0, 0],),
         (observed[0, 0], w_factor),
         [(CAP, 2, BS, BS), (CAP, 2, BS, BS), w_factor.shape],
         dtypes=[jnp.bfloat16, jnp.bfloat16, jnp.float32],
+        tables=[(2 * CAP,)],
     )
     (w_pair,) = call(w_pair_kernel, (blk,), (w_mine, w_other), [(NP, 4, wide)], scratch=[(4, wide)])
     w_got = exchange(w_pair, PLANE)

time: 176 us -> 173 us (0.983)
  Pallas kernels: 7.11 us -> 4.37 us
    pallas_call x14, Pallas kernels: 7.11 us -> 4.37 us  [call(): pl.pallas_call(body, in_specs=[smem] * len(scalars) + [vmem] * len(arrays...]
  transfers between devices with their start and end apart: 5 -> 5, of which waited for: 4 -> 4; matrix products, arithmetic and copies ran while one was open for 0% -> 0% of each run, Pallas kernels for 0% -> 1%
where the time goes in v7:
time: 173 us; the launch traced here: 172 us
  blocking collectives  95.3 us (55%)
  starting transfers between devices  54.6 us (32%)
  waiting for transfers between devices  14.8 us (9%)
  Pallas kernels  4.37 us (3%)
  local copies, waits for them, and re-layouts  2.35 us (1%)
    all_to_all x8, blocking collectives, exchange(): return lax.all_to_all(x, axes, split_axis=0, concat_axis=0, tiled=True)  93.3 us
    ppermute x5, starting transfers between devices, swap(): return lax.ppermute(x, axis, [(0, 1), (1, 0)])  54.6 us
    ppermute x5, waiting for transfers between devices, swap(): return lax.ppermute(x, axis, [(0, 1), (1, 0)])  14.8 us
    pallas_call x14, Pallas kernels, call(): pl.pallas_call(body, in_specs=[smem] * len(scalars) + [vmem] * len(arrays...  4.37 us
  transfers between devices with their start and end apart: 5, of which 4 were waited for; matrix products, arithmetic and copies ran while one was open for 0% of the time, Pallas kernels for 1%

profile of v7, /device:TPU:2, one launch (start us, length us, event | category | flops | bytes accessed | tf_op | source)
XLA Modules:
  0.0 172.1 jit_solution(9997981622873761761)
XLA Ops:
  0.6 15.7 %collective-permute-start = (f32[2,1024]{1,0:T(2,128)}, f32[2,1024]{1,0:T(2,128)S(1)}, u32[]{:S(2)}, u32[]{:S(2)}) collective-permute-start(f32[2,1024]{1,0:T(2,128)} %w.1), channel_id=1, source_target_pairs={{0,16},{16,0},{1,17},{17,1},{2,18},{18,2},{3,19},{19,3},{4,20},{20... | collective-permute-start | bytes 24584 | tf_op jit(solution)/shard_map/ppermute | solution.py:33
  16.4 1.0 copy-done
  17.4 0.7 copy-done.2
  18.1 0.9 shard_map.59
  19.1 14.8 %all_to_all.40.w0 = f32[16,4,1152]{2,1,0:T(4,128)S(1)} all-to-all(f32[16,4,1152]{2,1,0:T(4,128)S(1)} %shard_map.60), channel_id=1, replica_groups=mesh['z4'=2,'z2'=2,'z1'=2,'core'=2,'zh'=2,'y'=4,'x'=4] {'y','x'}, dimensions={0} | all-to-all | bytes 589824 | tf_op jit(solution)/shard_map/all_to_all | solution.py:29
  34.2 16.2 %all_to_all.41.got = f32[8,104,128]{2,1,0:T(8,128)S(1)} all-to-all(f32[8,104,128]{2,1,0:T(8,128)S(1)} %get-tuple-element.23), channel_id=1, replica_groups=mesh['z4'=2,'z2'=2,'z1'=2,'core'=2,'zh'=2,'y'=4,'x'=4] {'z2','z1','core'}, dimensions={0} | all-to-all | bytes 851968 | tf_op jit(solution)/shard_map/all_to_all | solution.py:29
  50.6 7.9 %collective-permute-start.1 = (f32[128,128]{1,0:T(8,128)S(1)}, f32[128,128]{1,0:T(8,128)S(1)}, u32[]{:S(2)}, u32[]{:S(2)}) collective-permute-start(f32[128,128]{1,0:T(8,128)S(1)} %get-tuple-element.24.mine), channel_id=1, source_target_pairs={{0,256},{256,0},{1,257},{257,1},{2,258},{258,2},{3,259},{259,3},{4... | collective-permute-start | bytes 196616 | tf_op jit(solution)/shard_map/ppermute | solution.py:33
  58.5 5.5 %collective-permute-done.1.theirs = f32[128,128]{1,0:T(8,128)S(1)} collective-permute-done((f32[128,128]{1,0:T(8,128)S(1)}, f32[128,128]{1,0:T(8,128)S(1)}, u32[]{:S(2)}, u32[]{:S(2)}) %collective-permute-start.1) | collective-permute-done | bytes 65568 | tf_op jit(solution)/shard_map/ppermute | solution.py:33
  64.2 8.8 %all_to_all.42 = f32[4,64,128]{2,1,0:T(8,128)S(1)} all-to-all(f32[4,64,128]{2,1,0:T(8,128)S(1)} %shard_map.63), channel_id=1, replica_groups=mesh['z4'=2,'z2'=2,'z1'=2,'core'=2,'zh'=2,'y'=4,'x'=4] {'z2','z1'}, dimensions={0} | all-to-all | bytes 262144 | tf_op jit(solution)/shard_map/all_to_all | solution.py:29
  72.9 2.0 %all-gather = f32[8,64,128]{2,1,0:T(8,128)S(1)} all-gather(f32[4,64,128]{2,1,0:T(8,128)S(1)} %all_to_all.42), channel_id=2, replica_groups=mesh['z4'=2,'z2'=2,'z1'=2,'core'=2,'zh'=2,'y'=4,'x'=4] {'core'}, dimensions={0}, use_global_device_ids=true | all-gather | bytes 393216 | tf_op jit(solution)/shard_map/all_gather | solution.py:298
  74.9 0.6 shard_map.64
  75.5 11.9 %all_to_all.43.got = f32[16,16,256]{2,1,0:T(8,128)S(1)} all-to-all(f32[16,16,256]{2,1,0:T(8,128)S(1)} %shard_map.64), channel_id=1, replica_groups=mesh['z4'=2,'z2'=2,'z1'=2,'core'=2,'zh'=2,'y'=4,'x'=4] {'y','x'}, dimensions={0} | all-to-all | bytes 524288 | tf_op jit(solution)/shard_map/all_to_all | solution.py:29
  87.5 11.5 %collective-permute-start.2 = (f32[4,8,256]{2,1,0:T(8,128)S(1)}, f32[4,8,256]{2,1,0:T(8,128)S(1)}, u32[]{:S(2)}, u32[]{:S(2)}) collective-permute-start(f32[4,8,256]{2,1,0:T(8,128)S(1)} %shard_map.65.mine), channel_id=1, source_target_pairs={{0,16},{16,0},{1,17},{17,1},{2,18},{18,2},{3,19},{19,3},{4,20},{20... | collective-permute-start | bytes 98312 | tf_op jit(solution)/shard_map/ppermute | solution.py:33
  99.0 3.0 %collective-permute-done.2.theirs = f32[4,8,256]{2,1,0:T(8,128)S(1)} collective-permute-done((f32[4,8,256]{2,1,0:T(8,128)S(1)}, f32[4,8,256]{2,1,0:T(8,128)S(1)}, u32[]{:S(2)}, u32[]{:S(2)}) %collective-permute-start.2) | collective-permute-done | bytes 32800 | tf_op jit(solution)/shard_map/ppermute | solution.py:33
  102.1 10.9 %all_to_all.44.w_got = f32[16,8,256]{2,1,0:T(8,128)S(1)} all-to-all(f32[16,8,256]{2,1,0:T(8,128)S(1)} %get-tuple-element.29), channel_id=1, replica_groups=mesh['z4'=2,'z2'=2,'z1'=2,'core'=2,'zh'=2,'y'=4,'x'=4] {'y','x'}, dimensions={0} | all-to-all | bytes 262144 | tf_op jit(solution)/shard_map/all_to_all | solution.py:29
  113.3 9.9 %all_to_all.45.got = f32[8,8,640]{2,1,0:T(8,128)S(1)} all-to-all(f32[8,8,640]{2,1,0:T(8,128)S(1)} %get-tuple-element.30), channel_id=1, replica_groups=mesh['z4'=2,'z2'=2,'z1'=2,'core'=2,'zh'=2,'y'=4,'x'=4] {'z2','z1','core'}, dimensions={0} | all-to-all | bytes 327680 | tf_op jit(solution)/shard_map/all_to_all | solution.py:29
  123.3 7.5 %collective-permute-start.3 = (f32[4,8,384]{2,1,0:T(8,128)S(1)}, f32[4,8,384]{2,1,0:T(8,128)S(1)}, u32[]{:S(2)}, u32[]{:S(2)}) collective-permute-start(f32[4,8,384]{2,1,0:T(8,128)S(1)} %shard_map.68.mine), channel_id=1, source_target_pairs={{0,256},{256,0},{1,257},{257,1},{2,258},{258,2},{3,259},{259,3},{4... | collective-permute-start | bytes 147464 | tf_op jit(solution)/shard_map/ppermute | solution.py:33
  130.8 4.4 %collective-permute-done.3.theirs = f32[4,8,384]{2,1,0:T(8,128)S(1)} collective-permute-done((f32[4,8,384]{2,1,0:T(8,128)S(1)}, f32[4,8,384]{2,1,0:T(8,128)S(1)}, u32[]{:S(2)}, u32[]{:S(2)}) %collective-permute-start.3) | collective-permute-done | bytes 49184 | tf_op jit(solution)/shard_map/ppermute | solution.py:33
  135.4 9.1 %all_to_all.46.h_got = f32[8,16,256]{2,1,0:T(8,128)S(1)} all-to-all(f32[8,16,256]{2,1,0:T(8,128)S(1)} %get-tuple-element.31), channel_id=1, replica_groups=mesh['z4'=2,'z2'=2,'z1'=2,'core'=2,'zh'=2,'y'=4,'x'=4] {'z2','z1','core'}, dimensions={0} | all-to-all | bytes 262144 | tf_op jit(solution)/shard_map/all_to_all | solution.py:29
  145.1 11.8 %all_to_all.47.got = f32[16,16,256]{2,1,0:T(8,128)S(1)} all-to-all(f32[16,16,256]{2,1,0:T(8,128)S(1)} %shard_map.70), channel_id=1, replica_groups=mesh['z4'=2,'z2'=2,'z1'=2,'core'=2,'zh'=2,'y'=4,'x'=4] {'y','x'}, dimensions={0} | all-to-all | bytes 524288 | tf_op jit(solution)/shard_map/all_to_all | solution.py:29
  157.0 12.0 %collective-permute-start.4 = (f32[4,8,256]{2,1,0:T(8,128)S(1)}, f32[4,8,256]{2,1,0:T(8,128)S(1)}, u32[]{:S(2)}, u32[]{:S(2)}) collective-permute-start(f32[4,8,256]{2,1,0:T(8,128)S(1)} %shard_map.71.mine), channel_id=1, source_target_pairs={{0,16},{16,0},{1,17},{17,1},{2,18},{18,2},{3,19},{19,3},{4,20},{20... | collective-permute-start | bytes 98312 | tf_op jit(solution)/shard_map/ppermute | solution.py:33
  169.1 0.6 copy.6
  169.7 1.9 %collective-permute-done.4.theirs = f32[4,8,256]{2,1,0:T(8,128)S(1)} collective-permute-done((f32[4,8,256]{2,1,0:T(8,128)S(1)}, f32[4,8,256]{2,1,0:T(8,128)S(1)}, u32[]{:S(2)}, u32[]{:S(2)}) %collective-permute-start.4) | collective-permute-done | bytes 32800 | tf_op jit(solution)/shard_map/ppermute | solution.py:33
  171.5 0.6 shard_map.72
  (16 shorter events, 2.3 us)
Async XLA Ops:
  0.6 18.4 %collective-permute-start = (f32[2,1024]{1,0:T(2,128)}, f32[2,1024]{1,0:T(2,128)S(1)}, u32[]{:S(2)}, u32[]{:S(2)}) collective-permute-start(f32[2,1024]{1,0:T(2,128)} %w.1), channel_id=1, source_target_pairs={{0,16},{16,0},{1,17},{17,1},{2,18},{18,2},{3,19},{19,3},{4,20},{20... | collective-permute-start | bytes 24584 | tf_op jit(solution)/shard_map/ppermute | solution.py:33
  16.4 1.0 copy-start
  17.4 0.7 copy-start.2
  19.1 14.8 %copy-start.1 = (f32[4,1024]{1,0:T(4,128)S(1)}, f32[4,1024]{1,0:T(4,128)}, u32[]{:S(2)}) copy-start(f32[4,1024]{1,0:T(4,128)} %h.1) | copy-start | bytes 49156
  50.6 13.4 %collective-permute-start.1 = (f32[128,128]{1,0:T(8,128)S(1)}, f32[128,128]{1,0:T(8,128)S(1)}, u32[]{:S(2)}, u32[]{:S(2)}) collective-permute-start(f32[128,128]{1,0:T(8,128)S(1)} %get-tuple-element.24.mine), channel_id=1, source_target_pairs={{0,256},{256,0},{1,257},{257,1},{2,258},{258,2},{3,259},{259,3},{4... | collective-permute-start | bytes 196616 | tf_op jit(solution)/shard_map/ppermute | solution.py:33
  87.5 14.5 %collective-permute-start.2 = (f32[4,8,256]{2,1,0:T(8,128)S(1)}, f32[4,8,256]{2,1,0:T(8,128)S(1)}, u32[]{:S(2)}, u32[]{:S(2)}) collective-permute-start(f32[4,8,256]{2,1,0:T(8,128)S(1)} %shard_map.65.mine), channel_id=1, source_target_pairs={{0,16},{16,0},{1,17},{17,1},{2,18},{18,2},{3,19},{19,3},{4,20},{20... | collective-permute-start | bytes 98312 | tf_op jit(solution)/shard_map/ppermute | solution.py:33
  123.3 11.9 %collective-permute-start.3 = (f32[4,8,384]{2,1,0:T(8,128)S(1)}, f32[4,8,384]{2,1,0:T(8,128)S(1)}, u32[]{:S(2)}, u32[]{:S(2)}) collective-permute-start(f32[4,8,384]{2,1,0:T(8,128)S(1)} %shard_map.68.mine), channel_id=1, source_target_pairs={{0,256},{256,0},{1,257},{257,1},{2,258},{258,2},{3,259},{259,3},{4... | collective-permute-start | bytes 147464 | tf_op jit(solution)/shard_map/ppermute | solution.py:33
  157.0 14.5 %collective-permute-start.4 = (f32[4,8,256]{2,1,0:T(8,128)S(1)}, f32[4,8,256]{2,1,0:T(8,128)S(1)}, u32[]{:S(2)}, u32[]{:S(2)}) collective-permute-start(f32[4,8,256]{2,1,0:T(8,128)S(1)} %shard_map.71.mine), channel_id=1, source_target_pairs={{0,16},{16,0},{1,17},{17,1},{2,18},{18,2},{3,19},{19,3},{4,20},{20... | collective-permute-start | bytes 98312 | tf_op jit(solution)/shard_map/ppermute | solution.py:33

commit v8 on v7

--- a/solution.py
+++ b/solution.py
@@ -98,7 +98,7 @@
         table[q * CAP + j] = jnp.maximum(listed[:, j : j + 1].astype(jnp.int32)[0, 0], 0)
 
 
-def h1_terms_kernel(blk, w0, h, values, w_slots, w_own, out, rows):
+def h1_terms_kernel(blk, w0, h, values, w_own, out, rows, w_slots):
     out[:, :96, :] = jnp.zeros((NH, 96, COLS), jnp.float32)
     for j in range(CAP):
         at = pl.multiple_of(block_of(blk, 0, j) * BS, BS)
@@ -157,10 +157,21 @@
         out[q, 8 * j + 4 : 8 * j + 8, :] = lower[4 * q : 4 * q + 4, :]
 
 
-def w1_terms_kernel(blk, h_all, w_slots, values, out):
+def send_grams(out, terms):
+    rows = out.shape[1]
+    both = jnp.concatenate([gram for _, gram in terms], axis=1)
+    for q in range(out.shape[0]):
+        for j in range(CAP):
+            out[q, :, BS * j : BS * (j + 1)] = terms[j][0][rows * q : rows * (q + 1), :]
+        out[q, :, CAP * BS :] = both[rows * q : rows * (q + 1), :]
+
+
+def w1_terms_kernel(blk, h_all, values, out):
+    terms = []
     for j in range(CAP):
         h_slot = whole_block(h_all, block_of(blk, 1, j))
-        send_w(out, j, *sums(h_slot, w_slots[j], both_of(values, j), live_of(blk, j)))
+        terms.append(grams(h_slot, both_of(values, j), live_of(blk, j)))
+    send_grams(out, terms)
 
 
 def w2_terms_kernel(blk, h_got, w_slots, values, out):
@@ -174,45 +185,60 @@
 
 
 def h2_terms_kernel(blk, w_got, values, w_slots, out):
-    both = []
+    terms = []
     for j in range(CAP):
         w_slots[j] = w_slot(w_got, j)
-        upper, gram = grams(w_slots[j], both_of(values, j), live_of(blk, j))
-        both.append(gram)
-        for q in range(NH):
-            out[q, :, BS * j : BS * (j + 1)] = upper[8 * q : 8 * q + 8, :]
-    both = jnp.concatenate(both, axis=1)
-    for q in range(NH):
-        out[q, :, CAP * BS :] = both[8 * q : 8 * q + 8, :]
-
-
-def h2_collect_kernel(table, got, out):
+        terms.append(grams(w_slots[j], both_of(values, j), live_of(blk, j)))
+    send_grams(out, terms)
+
+
+def gram_collect_kernel(table, got, out):
+    rows = out.shape[1]
     out[...] = jnp.zeros(out.shape, out.dtype)
-    lane = lax.broadcasted_iota(jnp.int32, (8, CAP * RANK), 1)
-    for q in range(NH):
-        gram = got[q, :, CAP * BS :]
+    half = lax.broadcasted_iota(jnp.int32, (rows, CAP * RANK), 1) // RANK
+    for q in range(got.shape[0]):
+        grams = got[q, :, CAP * BS :]
+        turned = jnp.concatenate([grams[:, RANK:], grams[:, :RANK]], axis=1)
         for j in range(CAP):
             b = table[q * CAP + j]
-            out[b, :, :BS] = out[b, :, :BS] + got[q, :, BS * j : BS * (j + 1)]
-            out[b, :, BS:] = out[b, :, BS:] + jnp.where(lane // RANK == j, gram, 0.0)
+            out[b] = out[b] + got[q, :, BS * j : BS * (j + 1)]
+            side = b % 2
+            at = pl.ds(pl.multiple_of(b // 2 * CAP * RANK, CAP * RANK), CAP * RANK)
+            mine = jnp.where(side == j, grams, turned)
+            out[NB, :, at] = out[NB, :, at] + jnp.where(half == side, mine, 0.0)
+
+
+def owned(own, whole, mine, theirs, b):
+    rows = own.shape[0]
+    gram = mine[NB, :, RANK * b : RANK * (b + 1)] + theirs[NB, :, RANK * b : RANK * (b + 1)]
+    high = gram.astype(jnp.bfloat16).astype(jnp.float32)
+    gram = jnp.concatenate([high, gram - high], axis=0).astype(jnp.bfloat16)
+    whole = halves(whole)
+    most = lax.dot_general(gram, whole[0], NN, preferred_element_type=jnp.float32)
+    rest = lax.dot_general(gram, whole[1], NN, preferred_element_type=jnp.float32)
+    return own * (mine[b] + theirs[b]) / (most[:rows] + (most[rows:] + rest[:rows]))
+
+
+def w_arrange_kernel(w0, w_all):
+    for b in range(NB):
+        for q in range(NP):
+            w_all[b, 4 * q : 4 * q + 4, :] = w0[q, :, b * BS : (b + 1) * BS]
+
+
+def w1_update_kernel(table, own, w_all, mine, theirs, new, out):
+    for b in range(NB):
+        new[b] = owned(own[b], w_all[b], mine, theirs, b)
+    for q in range(NP):
+        for j in range(CAP):
+            out[q, 4 * j : 4 * (j + 1), :] = new[table[q * CAP + j]]
 
 
 def h2_update_kernel(table, h_all, mine, theirs, final, out, new):
-    half = lax.axis_index(HALF)
     first = lax.axis_index("z4") == 0
-    for b in range(NB):
-        total = mine[b] + theirs[b]
-        gram = total[:, BS:]
-        high = gram.astype(jnp.bfloat16).astype(jnp.float32)
-        gram = jnp.concatenate([high, gram - high], axis=0).astype(jnp.bfloat16)
-        block = whole_block(h_all, b)
-        block = halves(jnp.concatenate([block, block], axis=0))
-        most = lax.dot_general(gram, block[0], NN, preferred_element_type=jnp.float32)
-        rest = lax.dot_general(gram, block[1], NN, preferred_element_type=jnp.float32)
-        lower = most[:8] + (most[8:] + rest[:8])
-        at = pl.multiple_of(8 * half, 8)
-        own = jnp.concatenate([h_all[0, b, pl.ds(at, 8), :], h_all[1, b, pl.ds(at, 8), :]], axis=1)
-        rows = own * total[:, :BS] / lower
+    at = pl.ds(pl.multiple_of(8 * lax.axis_index(HALF), 8), 8)
+    for b in range(NB):
+        own = jnp.concatenate([h_all[0, b, at, :], h_all[1, b, at, :]], axis=1)
+        rows = owned(own, whole_block(h_all, b), mine, theirs, b)
         new[b] = rows
         for high in range(2):
             pair = rows[4 * high : 4 * high + 4]
@@ -222,35 +248,26 @@
             out[q, 8 * j : 8 * (j + 1), :] = new[table[q * CAP + j]]
 
 
-def collect_kernel(table, got, out):
-    rows = out.shape[1]
-    out[...] = jnp.zeros(out.shape, out.dtype)
-    for q in range(got.shape[0]):
+def w2_collect_kernel(table, got, mine, out, total):
+    total[...] = jnp.zeros(total.shape, total.dtype)
+    for q in range(NP):
         for j in range(CAP):
             b = table[q * CAP + j]
-            out[b] = out[b] + got[q, rows * j : rows * (j + 1), :]
-
-
-def updated(own, mine, theirs):
-    rows = own.shape[1]
-    upper = mine[:, :rows, :] + theirs[:, :rows, :]
-    lower = mine[:, rows:, :] + theirs[:, rows:, :]
-    return own[...] * upper / lower
-
-
-def update_kernel(table, own, mine, theirs, new, out):
-    rows = own.shape[1]
-    new[...] = updated(own, mine, theirs)
-    for q in range(out.shape[0]):
-        for j in range(CAP):
-            out[q, rows * j : rows * (j + 1), :] = new[table[q * CAP + j]]
-
-
-def last_w_kernel(own, mine, theirs, final, new):
-    new[...] = updated(own, mine, theirs)
+            total[b] = total[b] + got[q, 8 * j : 8 * (j + 1), :]
     first = lax.axis_index("zh") == 0
     for b in range(NB):
-        final[:, b * BS : (b + 1) * BS] = jnp.where(first, new[b, 0:2, :], new[b, 2:4, :])
+        low = jnp.concatenate([total[b, 0:2, :], total[b, 4:6, :]], axis=0)
+        high = jnp.concatenate([total[b, 2:4, :], total[b, 6:8, :]], axis=0)
+        mine[b] = jnp.where(first, low, high)
+        out[b] = jnp.where(first, high, low)
+
+
+def last_w_kernel(own, mine, theirs, final):
+    first = lax.axis_index("zh") == 0
+    for b in range(NB):
+        total = mine[b] + theirs[b]
+        rows = jnp.where(first, own[b, 0:2, :], own[b, 2:4, :])
+        final[:, b * BS : (b + 1) * BS] = rows * total[0:2] / total[2:4]
 
 
 def call(body, scalars, arrays, outs, tables=(), scratch=(), last=False, dtypes=None):
@@ -284,29 +301,32 @@
     (w_pair,) = call(w_pair_kernel, (blk,), (w_mine, w_other), [(NP, 4, wide)], scratch=[(4, wide)])
     w_got = exchange(w_pair, PLANE)
 
-    w_slots, w_own, sent, rows = call(
+    w_own, sent, rows = call(
         h1_terms_kernel,
         (blk,),
         (w_got, h_factor, values),
-        [(CAP, RANK, BS), (NB, 4, BS), (NH, 104, COLS)],
+        [(NB, 4, BS), (NH, 104, COLS)],
         tables=[(NP * CAP,)],
+        scratch=[(CAP, RANK, BS)],
     )
     got = exchange(sent, HALF)
     mine, cols = call(h1_collect_kernel, (), (got,), [(128, COLS)], tables=[(NH * CAP,)])
     theirs = swap(mine, "z4")
+    (w_all,) = call(w_arrange_kernel, (), (w_got,), [(NB, RANK, BS)])
     (out,) = call(h1_update_kernel, (), (mine, theirs), [(NQ, RANK, COLS)])
     h_all = lax.all_gather(exchange(out, QUAD), "core", axis=0)
 
-    (sent,) = call(w1_terms_kernel, (blk,), (h_all, w_slots, turned), [(NP, 16, BS)])
+    wide = CAP * (BS + RANK)
+    (sent,) = call(w1_terms_kernel, (blk,), (h_all, turned), [(NP, 4, wide)])
     got = exchange(sent, PLANE)
-    (mine,) = call(collect_kernel, (rows,), (got,), [(NB, 8, BS)])
+    (mine,) = call(gram_collect_kernel, (rows,), (got,), [(NB + 1, 4, BS)])
     theirs = swap(mine, "zh")
-    w_own, out = call(update_kernel, (rows,), (w_own, mine, theirs), [(NB, 4, BS), (NP, 8, BS)])
+    w_own, out = call(w1_update_kernel, (rows,), (w_own, w_all, mine, theirs), [(NB, 4, BS), (NP, 8, BS)])
     w_got = exchange(out, PLANE)
 
-    w_slots, sent = call(h2_terms_kernel, (blk,), (w_got, values), [(CAP, RANK, BS), (NH, 8, CAP * (BS + RANK))])
+    w_slots, sent = call(h2_terms_kernel, (blk,), (w_got, values), [(CAP, RANK, BS), (NH, 8, wide)])
     got = exchange(sent, HALF)
-    (mine,) = call(h2_collect_kernel, (cols,), (got,), [(NB, 8, BS + CAP * RANK)])
+    (mine,) = call(gram_collect_kernel, (cols,), (got,), [(NB + 1, 8, BS)])
     theirs = swap(mine, "z4")
     h_final, out = call(
         h2_update_kernel, (cols,), (h_all, mine, theirs), [(4, NB * BS), (NH, 16, BS)], scratch=[(NB, 8, BS)]
@@ -315,9 +335,9 @@
 
     (sent,) = call(w2_terms_kernel, (blk,), (h_got, w_slots, turned), [(NP, 16, BS)])
     got = exchange(sent, PLANE)
-    (mine,) = call(collect_kernel, (rows,), (got,), [(NB, 8, BS)])
-    theirs = swap(mine, "zh")
-    (w_final,) = call(last_w_kernel, (), (w_own, mine, theirs), [(2, NB * BS)], scratch=[(NB, 4, BS)], last=True)
+    mine, out = call(w2_collect_kernel, (rows,), (got,), [(NB, 4, BS), (NB, 4, BS)], scratch=[(NB, 8, BS)])
+    theirs = swap(out, "zh")
+    (w_final,) = call(last_w_kernel, (), (w_own, mine, theirs), [(2, NB * BS)], last=True)
     return w_final, h_final
 
 

time: 173 us -> 172 us (level)
    pallas_call x14 -> x15, Pallas kernels: 4.37 us -> 4.76 us  [call(): pl.pallas_call(body, in_specs=[smem] * len(scalars) + [vmem] * len(arrays...]
where the time goes in v8:
time: 172 us; the launch traced here: 171 us
  blocking collectives  94.6 us (55%)
  starting transfers between devices  54.3 us (32%)
  waiting for transfers between devices  14.1 us (8%)
  Pallas kernels  4.76 us (3%)
  local copies, waits for them, and re-layouts  2.35 us (1%)
    all_to_all x8, blocking collectives, exchange(): return lax.all_to_all(x, axes, split_axis=0, concat_axis=0, tiled=True)  92.6 us
    ppermute x5, starting transfers between devices, swap(): return lax.ppermute(x, axis, [(0, 1), (1, 0)])  54.3 us
    ppermute x5, waiting for transfers between devices, swap(): return lax.ppermute(x, axis, [(0, 1), (1, 0)])  14.1 us
    pallas_call x15, Pallas kernels, call(): pl.pallas_call(body, in_specs=[smem] * len(scalars) + [vmem] * len(arrays...  4.76 us
  transfers between devices with their start and end apart: 5, of which 4 were waited for; matrix products, arithmetic and copies ran while one was open for 0% of the time, Pallas kernels for 1%

profile of v8, /device:TPU:2, one launch (start us, length us, event | category | flops | bytes accessed | tf_op | source)
XLA Modules:
  0.0 170.9 jit_solution(14083934155933191865)
XLA Ops:
  0.6 15.7 %collective-permute-start = (f32[2,1024]{1,0:T(2,128)}, f32[2,1024]{1,0:T(2,128)S(1)}, u32[]{:S(2)}, u32[]{:S(2)}) collective-permute-start(f32[2,1024]{1,0:T(2,128)} %w.1), channel_id=1, source_target_pairs={{0,16},{16,0},{1,17},{17,1},{2,18},{18,2},{3,19},{19,3},{4,20},{20... | collective-permute-start | bytes 24584 | tf_op jit(solution)/shard_map/ppermute | solution.py:33
  16.4 1.0 copy-done
  17.4 0.7 copy-done.2
  18.1 0.9 shard_map.59
  19.1 14.8 %all_to_all.40.w0 = f32[16,4,1152]{2,1,0:T(4,128)S(1)} all-to-all(f32[16,4,1152]{2,1,0:T(4,128)S(1)} %shard_map.60), channel_id=1, replica_groups=mesh['z4'=2,'z2'=2,'z1'=2,'core'=2,'zh'=2,'y'=4,'x'=4] {'y','x'}, dimensions={0} | all-to-all | bytes 589824 | tf_op jit(solution)/shard_map/all_to_all | solution.py:29
  34.2 16.2 %all_to_all.41.got = f32[8,104,128]{2,1,0:T(8,128)S(1)} all-to-all(f32[8,104,128]{2,1,0:T(8,128)S(1)} %get-tuple-element.24), channel_id=1, replica_groups=mesh['z4'=2,'z2'=2,'z1'=2,'core'=2,'zh'=2,'y'=4,'x'=4] {'z2','z1','core'}, dimensions={0} | all-to-all | bytes 851968 | tf_op jit(solution)/shard_map/all_to_all | solution.py:29
  50.6 7.9 %collective-permute-start.1 = (f32[128,128]{1,0:T(8,128)S(1)}, f32[128,128]{1,0:T(8,128)S(1)}, u32[]{:S(2)}, u32[]{:S(2)}) collective-permute-start(f32[128,128]{1,0:T(8,128)S(1)} %get-tuple-element.25.mine), channel_id=1, source_target_pairs={{0,256},{256,0},{1,257},{257,1},{2,258},{258,2},{3,259},{259,3},{4... | collective-permute-start | bytes 196616 | tf_op jit(solution)/shard_map/ppermute | solution.py:33
  58.5 5.5 %collective-permute-done.1.theirs = f32[128,128]{1,0:T(8,128)S(1)} collective-permute-done((f32[128,128]{1,0:T(8,128)S(1)}, f32[128,128]{1,0:T(8,128)S(1)}, u32[]{:S(2)}, u32[]{:S(2)}) %collective-permute-start.1) | collective-permute-done | bytes 65568 | tf_op jit(solution)/shard_map/ppermute | solution.py:33
  64.2 8.8 %all_to_all.42 = f32[4,64,128]{2,1,0:T(8,128)S(1)} all-to-all(f32[4,64,128]{2,1,0:T(8,128)S(1)} %shard_map.64), channel_id=1, replica_groups=mesh['z4'=2,'z2'=2,'z1'=2,'core'=2,'zh'=2,'y'=4,'x'=4] {'z2','z1'}, dimensions={0} | all-to-all | bytes 262144 | tf_op jit(solution)/shard_map/all_to_all | solution.py:29
  72.9 2.0 %all-gather = f32[8,64,128]{2,1,0:T(8,128)S(1)} all-gather(f32[4,64,128]{2,1,0:T(8,128)S(1)} %all_to_all.42), channel_id=2, replica_groups=mesh['z4'=2,'z2'=2,'z1'=2,'core'=2,'zh'=2,'y'=4,'x'=4] {'core'}, dimensions={0}, use_global_device_ids=true | all-gather | bytes 393216 | tf_op jit(solution)/shard_map/all_gather | solution.py:317
  75.3 11.0 %all_to_all.43.got = f32[16,4,640]{2,1,0:T(4,128)S(1)} all-to-all(f32[16,4,640]{2,1,0:T(4,128)S(1)} %shard_map.65), channel_id=1, replica_groups=mesh['z4'=2,'z2'=2,'z1'=2,'core'=2,'zh'=2,'y'=4,'x'=4] {'y','x'}, dimensions={0} | all-to-all | bytes 327680 | tf_op jit(solution)/shard_map/all_to_all | solution.py:29
  86.7 11.5 %collective-permute-start.2 = (f32[5,4,256]{2,1,0:T(4,128)S(1)}, f32[5,4,256]{2,1,0:T(4,128)S(1)}, u32[]{:S(2)}, u32[]{:S(2)}) collective-permute-start(f32[5,4,256]{2,1,0:T(4,128)S(1)} %shard_map.66.mine), channel_id=1, source_target_pairs={{0,16},{16,0},{1,17},{17,1},{2,18},{18,2},{3,19},{19,3},{4,20},{20... | collective-permute-start | bytes 61448 | tf_op jit(solution)/shard_map/ppermute | solution.py:33
  98.2 2.9 %collective-permute-done.2.theirs = f32[5,4,256]{2,1,0:T(4,128)S(1)} collective-permute-done((f32[5,4,256]{2,1,0:T(4,128)S(1)}, f32[5,4,256]{2,1,0:T(4,128)S(1)}, u32[]{:S(2)}, u32[]{:S(2)}) %collective-permute-start.2) | collective-permute-done | bytes 20512 | tf_op jit(solution)/shard_map/ppermute | solution.py:33
  101.3 11.0 %all_to_all.44.w_got = f32[16,8,256]{2,1,0:T(8,128)S(1)} all-to-all(f32[16,8,256]{2,1,0:T(8,128)S(1)} %get-tuple-element.29), channel_id=1, replica_groups=mesh['z4'=2,'z2'=2,'z1'=2,'core'=2,'zh'=2,'y'=4,'x'=4] {'y','x'}, dimensions={0} | all-to-all | bytes 262144 | tf_op jit(solution)/shard_map/all_to_all | solution.py:29
  112.7 9.9 %all_to_all.45.got = f32[8,8,640]{2,1,0:T(8,128)S(1)} all-to-all(f32[8,8,640]{2,1,0:T(8,128)S(1)} %get-tuple-element.30), channel_id=1, replica_groups=mesh['z4'=2,'z2'=2,'z1'=2,'core'=2,'zh'=2,'y'=4,'x'=4] {'z2','z1','core'}, dimensions={0} | all-to-all | bytes 327680 | tf_op jit(solution)/shard_map/all_to_all | solution.py:29
  122.8 7.5 %collective-permute-start.3 = (f32[5,8,256]{2,1,0:T(8,128)S(1)}, f32[5,8,256]{2,1,0:T(8,128)S(1)}, u32[]{:S(2)}, u32[]{:S(2)}) collective-permute-start(f32[5,8,256]{2,1,0:T(8,128)S(1)} %shard_map.69.mine), channel_id=1, source_target_pairs={{0,256},{256,0},{1,257},{257,1},{2,258},{258,2},{3,259},{259,3},{4... | collective-permute-start | bytes 122888 | tf_op jit(solution)/shard_map/ppermute | solution.py:33
  130.3 3.8 %collective-permute-done.3.theirs = f32[5,8,256]{2,1,0:T(8,128)S(1)} collective-permute-done((f32[5,8,256]{2,1,0:T(8,128)S(1)}, f32[5,8,256]{2,1,0:T(8,128)S(1)}, u32[]{:S(2)}, u32[]{:S(2)}) %collective-permute-start.3) | collective-permute-done | bytes 40992 | tf_op jit(solution)/shard_map/ppermute | solution.py:33
  134.3 9.1 %all_to_all.46.h_got = f32[8,16,256]{2,1,0:T(8,128)S(1)} all-to-all(f32[8,16,256]{2,1,0:T(8,128)S(1)} %get-tuple-element.31), channel_id=1, replica_groups=mesh['z4'=2,'z2'=2,'z1'=2,'core'=2,'zh'=2,'y'=4,'x'=4] {'z2','z1','core'}, dimensions={0} | all-to-all | bytes 262144 | tf_op jit(solution)/shard_map/all_to_all | solution.py:29
  143.4 0.6 shard_map.71
  144.0 11.8 %all_to_all.47.got = f32[16,16,256]{2,1,0:T(8,128)S(1)} all-to-all(f32[16,16,256]{2,1,0:T(8,128)S(1)} %shard_map.71), channel_id=1, replica_groups=mesh['z4'=2,'z2'=2,'z1'=2,'core'=2,'zh'=2,'y'=4,'x'=4] {'y','x'}, dimensions={0} | all-to-all | bytes 524288 | tf_op jit(solution)/shard_map/all_to_all | solution.py:29
  155.9 11.7 %collective-permute-start.4 = (f32[4,4,256]{2,1,0:T(4,128)S(1)}, f32[4,4,256]{2,1,0:T(4,128)S(1)}, u32[]{:S(2)}, u32[]{:S(2)}) collective-permute-start(f32[4,4,256]{2,1,0:T(4,128)S(1)} %get-tuple-element.34), channel_id=1, source_target_pairs={{0,16},{16,0},{1,17},{17,1},{2,18},{18,2},{3,19},{19,3},{4,20},{20... | collective-permute-start | bytes 49160 | tf_op jit(solution)/shard_map/ppermute | solution.py:33
  167.6 0.6 copy.6
  168.3 2.0 %collective-permute-done.4.theirs = f32[4,4,256]{2,1,0:T(4,128)S(1)} collective-permute-done((f32[4,4,256]{2,1,0:T(4,128)S(1)}, f32[4,4,256]{2,1,0:T(4,128)S(1)}, u32[]{:S(2)}, u32[]{:S(2)}) %collective-permute-start.4) | collective-permute-done | bytes 16416 | tf_op jit(solution)/shard_map/ppermute | solution.py:33
  170.3 0.6 shard_map.73
  (17 shorter events, 2.7 us)
Async XLA Ops:
  0.6 18.4 %collective-permute-start = (f32[2,1024]{1,0:T(2,128)}, f32[2,1024]{1,0:T(2,128)S(1)}, u32[]{:S(2)}, u32[]{:S(2)}) collective-permute-start(f32[2,1024]{1,0:T(2,128)} %w.1), channel_id=1, source_target_pairs={{0,16},{16,0},{1,17},{17,1},{2,18},{18,2},{3,19},{19,3},{4,20},{20... | collective-permute-start | bytes 24584 | tf_op jit(solution)/shard_map/ppermute | solution.py:33
  16.4 1.0 copy-start
  17.4 0.7 copy-start.2
  19.1 14.8 %copy-start.1 = (f32[4,1024]{1,0:T(4,128)S(1)}, f32[4,1024]{1,0:T(4,128)}, u32[]{:S(2)}) copy-start(f32[4,1024]{1,0:T(4,128)} %h.1) | copy-start | bytes 49156
  50.6 13.4 %collective-permute-start.1 = (f32[128,128]{1,0:T(8,128)S(1)}, f32[128,128]{1,0:T(8,128)S(1)}, u32[]{:S(2)}, u32[]{:S(2)}) collective-permute-start(f32[128,128]{1,0:T(8,128)S(1)} %get-tuple-element.25.mine), channel_id=1, source_target_pairs={{0,256},{256,0},{1,257},{257,1},{2,258},{258,2},{3,259},{259,3},{4... | collective-permute-start | bytes 196616 | tf_op jit(solution)/shard_map/ppermute | solution.py:33
  86.7 14.4 %collective-permute-start.2 = (f32[5,4,256]{2,1,0:T(4,128)S(1)}, f32[5,4,256]{2,1,0:T(4,128)S(1)}, u32[]{:S(2)}, u32[]{:S(2)}) collective-permute-start(f32[5,4,256]{2,1,0:T(4,128)S(1)} %shard_map.66.mine), channel_id=1, source_target_pairs={{0,16},{16,0},{1,17},{17,1},{2,18},{18,2},{3,19},{19,3},{4,20},{20... | collective-permute-start | bytes 61448 | tf_op jit(solution)/shard_map/ppermute | solution.py:33
  122.8 11.3 %collective-permute-start.3 = (f32[5,8,256]{2,1,0:T(8,128)S(1)}, f32[5,8,256]{2,1,0:T(8,128)S(1)}, u32[]{:S(2)}, u32[]{:S(2)}) collective-permute-start(f32[5,8,256]{2,1,0:T(8,128)S(1)} %shard_map.69.mine), channel_id=1, source_target_pairs={{0,256},{256,0},{1,257},{257,1},{2,258},{258,2},{3,259},{259,3},{4... | collective-permute-start | bytes 122888 | tf_op jit(solution)/shard_map/ppermute | solution.py:33
  155.9 14.3 %collective-permute-start.4 = (f32[4,4,256]{2,1,0:T(4,128)S(1)}, f32[4,4,256]{2,1,0:T(4,128)S(1)}, u32[]{:S(2)}, u32[]{:S(2)}) collective-permute-start(f32[4,4,256]{2,1,0:T(4,128)S(1)} %get-tuple-element.34), channel_id=1, source_target_pairs={{0,16},{16,0},{1,17},{17,1},{2,18},{18,2},{3,19},{19,3},{4,20},{20... | collective-permute-start | bytes 49160 | tf_op jit(solution)/shard_map/ppermute | solution.py:33

commit v9 on v8

--- a/solution.py
+++ b/solution.py
@@ -50,11 +50,6 @@
     return product(left, values), product(left, whole, NT)
 
 
-def sums(left, right, values, live):
-    upper, gram = grams(left, values, live)
-    return upper, product(halves(gram), halves(right))
-
-
 def prepare_kernel(blk, values, w, parts, turned, w_mine, listed):
     for d in range(2):
         for j in range(CAP):
@@ -98,23 +93,25 @@
         table[q * CAP + j] = jnp.maximum(listed[:, j : j + 1].astype(jnp.int32)[0, 0], 0)
 
 
+def w_slot(w_got, j, blk, w_slots):
+    at = pl.multiple_of(block_of(blk, 0, j) * BS, BS)
+    for q in range(NP):
+        w_slots[j, 4 * q : 4 * q + 4, :] = w_got[q, :, pl.ds(at, BS)]
+    return w_slots[j]
+
+
 def h1_terms_kernel(blk, w0, h, values, w_own, out, rows, w_slots):
-    out[:, :96, :] = jnp.zeros((NH, 96, COLS), jnp.float32)
-    for j in range(CAP):
-        at = pl.multiple_of(block_of(blk, 0, j) * BS, BS)
-        for q in range(NP):
-            w_slots[j, 4 * q : 4 * q + 4, :] = w0[q, :, pl.ds(at, BS)]
-        upper, gram = grams(w_slots[j], both_of(values, j), live_of(blk, j))
-        gram = jnp.concatenate([gram[:32], gram[32:]], axis=1)
+    for j in range(CAP):
+        upper, gram = grams(w_slot(w0, j, blk, w_slots), both_of(values, j), live_of(blk, j))
         for side in range(2):
-            q = 2 * block_of(blk, 1, j) + side
-            out[q, :64, :] = out[q, :64, :] + upper[:, COLS * side : COLS * (side + 1)]
-            out[q, 64:96, :] = out[q, 64:96, :] + gram
-    lane = lax.broadcasted_iota(jnp.int32, (4, COLS), 1)
-    listed = jnp.where(lane == 0, blk[CAP], blk[CAP + 1]).astype(jnp.float32)
+            at = 128 * j + RANK * side
+            out[at : at + RANK, :] = upper[:, COLS * side : COLS * (side + 1)]
+        out[256 + 32 * j : 288 + 32 * j, :] = jnp.concatenate([gram[:32], gram[32:]], axis=1)
     for q in range(NH):
-        out[q, 96:100, :] = h[:, COLS * q : COLS * (q + 1)]
-        out[q, 100:104, :] = listed
+        at = 320 + 16 * (q % 2) + 4 * (q // 2)
+        out[at : at + 4, :] = h[:, COLS * q : COLS * (q + 1)]
+    lane = lax.broadcasted_iota(jnp.int32, (8, COLS), 1)
+    out[352:360, :] = jnp.where(lane == 0, blk[CAP], blk[CAP + 1]).astype(jnp.float32)
     plane = lax.axis_index(PLANE)
     for b in range(NB):
         w_own[b] = w0[plane, :, b * BS : (b + 1) * BS]
@@ -122,14 +119,31 @@
         read_list(rows, q, w0[q, 0:1, NB * BS :])
 
 
+def h1_build_kernel(pair, out, lists):
+    core = lax.axis_index("core")
+    out[:, :96, :] = jnp.zeros((NQ, 96, COLS), jnp.float32)
+    for i in range(2):
+        read_list(lists, i, pair[i, 352:353, :])
+        for j in range(CAP):
+            q = lists[CAP * i + j]
+            at = pl.multiple_of(128 * j + RANK * core, 8)
+            out[q, :64, :] = out[q, :64, :] + pair[i, pl.ds(at, RANK), :]
+            out[q, 64:96, :] = out[q, 64:96, :] + pair[i, 256 + 32 * j : 288 + 32 * j, :]
+        side = pair[i, pl.ds(pl.multiple_of(320 + 16 * core, 8), 16), :]
+        for q in range(NQ):
+            out[q, 96 + 4 * i : 100 + 4 * i, :] = side[4 * q : 4 * q + 4]
+            out[q, 104 + 4 * i : 108 + 4 * i, :] = pair[i, 352:356, :]
+
+
 def h1_collect_kernel(got, out, cols):
     total = got[0, :96, :]
-    for q in range(1, NH):
+    for q in range(1, NQ):
         total = total + got[q, :96, :]
     out[:96, :] = total
-    for q in range(NH):
-        out[96 + 4 * q : 100 + 4 * q, :] = got[q, 96:100, :]
-        read_list(cols, q, got[q, 100:101, :])
+    for q in range(NQ):
+        out[96 + 8 * q : 104 + 8 * q, :] = got[q, 96:104, :]
+        for i in range(2):
+            read_list(cols, 2 * q + i, got[q, 104 + 4 * i : 105 + 4 * i, :])
 
 
 def h1_update_kernel(mine, theirs, out):
@@ -151,12 +165,6 @@
     return jnp.concatenate([h_all[0, b], h_all[1, b]], axis=1)
 
 
-def send_w(out, j, upper, lower):
-    for q in range(NP):
-        out[q, 8 * j : 8 * j + 4, :] = upper[4 * q : 4 * q + 4, :]
-        out[q, 8 * j + 4 : 8 * j + 8, :] = lower[4 * q : 4 * q + 4, :]
-
-
 def send_grams(out, terms):
     rows = out.shape[1]
     both = jnp.concatenate([gram for _, gram in terms], axis=1)
@@ -174,21 +182,18 @@
     send_grams(out, terms)
 
 
-def w2_terms_kernel(blk, h_got, w_slots, values, out):
+def w2_terms_kernel(blk, h_got, values, out):
+    terms = []
     for j in range(CAP):
         h_slot = h_got[:, 8 * j : 8 * j + 8, :].reshape(RANK, BS)
-        send_w(out, j, *sums(h_slot, w_slots[j], both_of(values, j), live_of(blk, j)))
-
-
-def w_slot(got, j):
-    return jnp.concatenate([got[q, 4 * j : 4 * j + 4, :] for q in range(NP)], axis=0)
-
-
-def h2_terms_kernel(blk, w_got, values, w_slots, out):
+        terms.append(grams(h_slot, both_of(values, j), live_of(blk, j)))
+    send_grams(out, terms)
+
+
+def h2_terms_kernel(blk, w_got, values, out, w_slots):
     terms = []
     for j in range(CAP):
-        w_slots[j] = w_slot(w_got, j)
-        terms.append(grams(w_slots[j], both_of(values, j), live_of(blk, j)))
+        terms.append(grams(w_slot(w_got, j, blk, w_slots), both_of(values, j), live_of(blk, j)))
     send_grams(out, terms)
 
 
@@ -225,12 +230,12 @@
             w_all[b, 4 * q : 4 * q + 4, :] = w0[q, :, b * BS : (b + 1) * BS]
 
 
-def w1_update_kernel(table, own, w_all, mine, theirs, new, out):
-    for b in range(NB):
-        new[b] = owned(own[b], w_all[b], mine, theirs, b)
-    for q in range(NP):
-        for j in range(CAP):
-            out[q, 4 * j : 4 * (j + 1), :] = new[table[q * CAP + j]]
+def w1_update_kernel(own, w_all, mine, theirs, new, out):
+    for b in range(NB):
+        rows = owned(own[b], w_all[b], mine, theirs, b)
+        new[b] = rows
+        for q in range(NP):
+            out[q, :, b * BS : (b + 1) * BS] = rows
 
 
 def h2_update_kernel(table, h_all, mine, theirs, final, out, new):
@@ -249,28 +254,21 @@
 
 
 def w2_collect_kernel(table, got, mine, out, total):
-    total[...] = jnp.zeros(total.shape, total.dtype)
-    for q in range(NP):
-        for j in range(CAP):
-            b = table[q * CAP + j]
-            total[b] = total[b] + got[q, 8 * j : 8 * (j + 1), :]
+    gram_collect_kernel(table, got, total)
     first = lax.axis_index("zh") == 0
-    for b in range(NB):
-        low = jnp.concatenate([total[b, 0:2, :], total[b, 4:6, :]], axis=0)
-        high = jnp.concatenate([total[b, 2:4, :], total[b, 6:8, :]], axis=0)
-        mine[b] = jnp.where(first, low, high)
-        out[b] = jnp.where(first, high, low)
-
-
-def last_w_kernel(own, mine, theirs, final):
+    low, high = total[:, 0:2, :], total[:, 2:4, :]
+    mine[...] = jnp.where(first, low, high)
+    out[...] = jnp.where(first, high, low)
+
+
+def last_w_kernel(own, w_all, mine, theirs, final):
     first = lax.axis_index("zh") == 0
     for b in range(NB):
-        total = mine[b] + theirs[b]
         rows = jnp.where(first, own[b, 0:2, :], own[b, 2:4, :])
-        final[:, b * BS : (b + 1) * BS] = rows * total[0:2] / total[2:4]
-
-
-def call(body, scalars, arrays, outs, tables=(), scratch=(), last=False, dtypes=None):
+        final[:, b * BS : (b + 1) * BS] = owned(rows, w_all[b], mine, theirs, b)
+
+
+def call(body, scalars, arrays, outs, tables=(), scratch=(), counts=(), last=False, dtypes=None):
     smem = pl.BlockSpec(memory_space=pltpu.SMEM)
     vmem = pl.BlockSpec(memory_space=pltpu.VMEM)
     kind = jax.ShapeDtypeStruct if last else pltpu.VMEM
@@ -279,7 +277,7 @@
         in_specs=[smem] * len(scalars) + [vmem] * len(arrays),
         out_specs=[vmem] * len(outs) + [smem] * len(tables),
         out_shape=[kind(*s) for s in zip(outs, dtypes or [jnp.float32] * len(outs))] + [pltpu.SMEM(s, jnp.int32) for s in tables],
-        scratch_shapes=[pltpu.VMEM(s, jnp.float32) for s in scratch],
+        scratch_shapes=[pltpu.VMEM(s, jnp.float32) for s in scratch] + [pltpu.SMEM((n,), jnp.int32) for n in counts],
     )(
         *(pltpu.with_memory_space_constraint(a, pltpu.SMEM) for a in scalars),
         *(pltpu.with_memory_space_constraint(a, pltpu.VMEM) for a in arrays),
@@ -305,11 +303,13 @@
         h1_terms_kernel,
         (blk,),
         (w_got, h_factor, values),
-        [(NB, 4, BS), (NH, 104, COLS)],
+        [(NB, 4, BS), (360, COLS)],
         tables=[(NP * CAP,)],
         scratch=[(CAP, RANK, BS)],
     )
-    got = exchange(sent, HALF)
+    pair = lax.all_gather(sent, "core", axis=0)
+    (sent,) = call(h1_build_kernel, (), (pair,), [(NQ, 112, COLS)], counts=(2 * CAP,))
+    got = exchange(sent, QUAD)
     mine, cols = call(h1_collect_kernel, (), (got,), [(128, COLS)], tables=[(NH * CAP,)])
     theirs = swap(mine, "z4")
     (w_all,) = call(w_arrange_kernel, (), (w_got,), [(NB, RANK, BS)])
@@ -321,23 +321,24 @@
     got = exchange(sent, PLANE)
     (mine,) = call(gram_collect_kernel, (rows,), (got,), [(NB + 1, 4, BS)])
     theirs = swap(mine, "zh")
-    w_own, out = call(w1_update_kernel, (rows,), (w_own, w_all, mine, theirs), [(NB, 4, BS), (NP, 8, BS)])
+    w_own, out = call(w1_update_kernel, (), (w_own, w_all, mine, theirs), [(NB, 4, BS), (NP, 4, NB * BS)])
     w_got = exchange(out, PLANE)
 
-    w_slots, sent = call(h2_terms_kernel, (blk,), (w_got, values), [(CAP, RANK, BS), (NH, 8, wide)])
+    (sent,) = call(h2_terms_kernel, (blk,), (w_got, values), [(NH, 8, wide)], scratch=[(CAP, RANK, BS)])
     got = exchange(sent, HALF)
     (mine,) = call(gram_collect_kernel, (cols,), (got,), [(NB + 1, 8, BS)])
     theirs = swap(mine, "z4")
+    (w_all,) = call(w_arrange_kernel, (), (w_got,), [(NB, RANK, BS)])
     h_final, out = call(
         h2_update_kernel, (cols,), (h_all, mine, theirs), [(4, NB * BS), (NH, 16, BS)], scratch=[(NB, 8, BS)]
     )
     h_got = exchange(out, HALF)
 
-    (sent,) = call(w2_terms_kernel, (blk,), (h_got, w_slots, turned), [(NP, 16, BS)])
+    (sent,) = call(w2_terms_kernel, (blk,), (h_got, turned), [(NP, 4, wide)])
     got = exchange(sent, PLANE)
-    mine, out = call(w2_collect_kernel, (rows,), (got,), [(NB, 4, BS), (NB, 4, BS)], scratch=[(NB, 8, BS)])
+    mine, out = call(w2_collect_kernel, (rows,), (got,), [(NB + 1, 2, BS), (NB + 1, 2, BS)], scratch=[(NB + 1, 4, BS)])
     theirs = swap(out, "zh")
-    (w_final,) = call(last_w_kernel, (), (w_own, mine, theirs), [(2, NB * BS)], last=True)
+    (w_final,) = call(last_w_kernel, (), (w_own, w_all, mine, theirs), [(2, NB * BS)], last=True)
     return w_final, h_final
 
 

time: 172 us -> 169 us (0.983)
  the two profiles are of different devices: /device:TPU:2 before, /device:TPU:128 now
where the time goes in v9:
time: 169 us; the launch traced here: 168 us
  blocking collectives  100 us (59%)
  starting transfers between devices  31.6 us (19%)
  waiting for transfers between devices  28.1 us (17%)
  Pallas kernels  5.16 us (3%)
  local copies, waits for them, and re-layouts  2.35 us (1%)
    all_to_all x8, blocking collectives, exchange(): return lax.all_to_all(x, axes, split_axis=0, concat_axis=0, tiled=True)  96.2 us
    ppermute x5, starting transfers between devices, swap(): return lax.ppermute(x, axis, [(0, 1), (1, 0)])  31.6 us
    ppermute x5, waiting for transfers between devices, swap(): return lax.ppermute(x, axis, [(0, 1), (1, 0)])  28.1 us
    pallas_call x17, Pallas kernels, call(): pl.pallas_call(body, in_specs=[smem] * len(scalars) + [vmem] * len(arrays...  5.16 us
  transfers between devices with their start and end apart: 5, of which 5 were waited for; matrix products, arithmetic and copies ran while one was open for 0% of the time, Pallas kernels for 1%

profile of v9, /device:TPU:128, one launch (start us, length us, event | category | flops | bytes accessed | tf_op | source)
XLA Modules:
  0.0 168.2 jit_solution(12444037314004258980)
XLA Ops:
  0.6 10.9 %collective-permute-start = (f32[2,1024]{1,0:T(2,128)}, f32[2,1024]{1,0:T(2,128)S(1)}, u32[]{:S(2)}, u32[]{:S(2)}) collective-permute-start(f32[2,1024]{1,0:T(2,128)} %w.1), channel_id=1, source_target_pairs={{0,16},{16,0},{1,17},{17,1},{2,18},{18,2},{3,19},{19,3},{4,20},{20... | collective-permute-start | bytes 24584 | tf_op jit(solution)/shard_map/ppermute | solution.py:33
  11.6 1.0 copy-done
  12.6 0.7 copy-done.2
  13.3 0.9 shard_map.59
  14.2 0.9 collective-permute-done.theirs
  15.2 15.7 %all_to_all.40.w0 = f32[16,4,1152]{2,1,0:T(4,128)S(1)} all-to-all(f32[16,4,1152]{2,1,0:T(4,128)S(1)} %shard_map.60), channel_id=1, replica_groups=mesh['z4'=2,'z2'=2,'z1'=2,'core'=2,'zh'=2,'y'=4,'x'=4] {'y','x'}, dimensions={0} | all-to-all | bytes 589824 | tf_op jit(solution)/shard_map/all_to_all | solution.py:29
  31.2 2.1 %all-gather = f32[720,128]{1,0:T(8,128)S(1)} all-gather(f32[360,128]{1,0:T(8,128)S(1)} %get-tuple-element.22), channel_id=2, replica_groups=mesh['z4'=2,'z2'=2,'z1'=2,'core'=2,'zh'=2,'y'=4,'x'=4] {'core'}, dimensions={0}, use_global_device_ids=true | all-gather | bytes 552960 | tf_op jit(solution)/shard_map/all_gather | solution.py:310
  33.4 14.2 %all_to_all.41.got = f32[4,112,128]{2,1,0:T(8,128)S(1)} all-to-all(f32[4,112,128]{2,1,0:T(8,128)S(1)} %shard_map.63), channel_id=1, replica_groups=mesh['z4'=2,'z2'=2,'z1'=2,'core'=2,'zh'=2,'y'=4,'x'=4] {'z2','z1'}, dimensions={0} | all-to-all | bytes 458752 | tf_op jit(solution)/shard_map/all_to_all | solution.py:29
  47.7 1.9 %collective-permute-start.1 = (f32[128,128]{1,0:T(8,128)S(1)}, f32[128,128]{1,0:T(8,128)S(1)}, u32[]{:S(2)}, u32[]{:S(2)}) collective-permute-start(f32[128,128]{1,0:T(8,128)S(1)} %get-tuple-element.23.mine), channel_id=1, source_target_pairs={{0,256},{256,0},{1,257},{257,1},{2,258},{258,2},{3,259},{259,3},{4... | collective-permute-start | bytes 196616 | tf_op jit(solution)/shard_map/ppermute | solution.py:33
  49.7 8.1 %collective-permute-done.1.theirs = f32[128,128]{1,0:T(8,128)S(1)} collective-permute-done((f32[128,128]{1,0:T(8,128)S(1)}, f32[128,128]{1,0:T(8,128)S(1)}, u32[]{:S(2)}, u32[]{:S(2)}) %collective-permute-start.1) | collective-permute-done | bytes 65568 | tf_op jit(solution)/shard_map/ppermute | solution.py:33
  58.0 11.4 %all_to_all.42 = f32[4,64,128]{2,1,0:T(8,128)S(1)} all-to-all(f32[4,64,128]{2,1,0:T(8,128)S(1)} %shard_map.65), channel_id=1, replica_groups=mesh['z4'=2,'z2'=2,'z1'=2,'core'=2,'zh'=2,'y'=4,'x'=4] {'z2','z1'}, dimensions={0} | all-to-all | bytes 262144 | tf_op jit(solution)/shard_map/all_to_all | solution.py:29
  69.5 2.0 %all-gather.1 = f32[8,64,128]{2,1,0:T(8,128)S(1)} all-gather(f32[4,64,128]{2,1,0:T(8,128)S(1)} %all_to_all.42), channel_id=3, replica_groups=mesh['z4'=2,'z2'=2,'z1'=2,'core'=2,'zh'=2,'y'=4,'x'=4] {'core'}, dimensions={0}, use_global_device_ids=true | all-gather | bytes 393216 | tf_op jit(solution)/shard_map/all_gather | solution.py:317
  71.8 11.0 %all_to_all.43.got = f32[16,4,640]{2,1,0:T(4,128)S(1)} all-to-all(f32[16,4,640]{2,1,0:T(4,128)S(1)} %shard_map.66), channel_id=1, replica_groups=mesh['z4'=2,'z2'=2,'z1'=2,'core'=2,'zh'=2,'y'=4,'x'=4] {'y','x'}, dimensions={0} | all-to-all | bytes 327680 | tf_op jit(solution)/shard_map/all_to_all | solution.py:29
  83.2 8.2 %collective-permute-start.2 = (f32[5,4,256]{2,1,0:T(4,128)S(1)}, f32[5,4,256]{2,1,0:T(4,128)S(1)}, u32[]{:S(2)}, u32[]{:S(2)}) collective-permute-start(f32[5,4,256]{2,1,0:T(4,128)S(1)} %shard_map.67.mine), channel_id=1, source_target_pairs={{0,16},{16,0},{1,17},{17,1},{2,18},{18,2},{3,19},{19,3},{4,20},{20... | collective-permute-start | bytes 61448 | tf_op jit(solution)/shard_map/ppermute | solution.py:33
  91.5 6.1 %collective-permute-done.2.theirs = f32[5,4,256]{2,1,0:T(4,128)S(1)} collective-permute-done((f32[5,4,256]{2,1,0:T(4,128)S(1)}, f32[5,4,256]{2,1,0:T(4,128)S(1)}, u32[]{:S(2)}, u32[]{:S(2)}) %collective-permute-start.2) | collective-permute-done | bytes 20512 | tf_op jit(solution)/shard_map/ppermute | solution.py:33
  97.8 11.7 %all_to_all.44.w0.w_got = f32[16,4,1024]{2,1,0:T(4,128)S(1)} all-to-all(f32[16,4,1024]{2,1,0:T(4,128)S(1)} %get-tuple-element.26), channel_id=1, replica_groups=mesh['z4'=2,'z2'=2,'z1'=2,'core'=2,'zh'=2,'y'=4,'x'=4] {'y','x'}, dimensions={0} | all-to-all | bytes 524288 | tf_op jit(solution)/shard_map/all_to_all | solution.py:29
  110.0 9.9 %all_to_all.45.got = f32[8,8,640]{2,1,0:T(8,128)S(1)} all-to-all(f32[8,8,640]{2,1,0:T(8,128)S(1)} %shard_map.70), channel_id=1, replica_groups=mesh['z4'=2,'z2'=2,'z1'=2,'core'=2,'zh'=2,'y'=4,'x'=4] {'z2','z1','core'}, dimensions={0} | all-to-all | bytes 327680 | tf_op jit(solution)/shard_map/all_to_all | solution.py:29
  120.0 1.9 %collective-permute-start.3 = (f32[5,8,256]{2,1,0:T(8,128)S(1)}, f32[5,8,256]{2,1,0:T(8,128)S(1)}, u32[]{:S(2)}, u32[]{:S(2)}) collective-permute-start(f32[5,8,256]{2,1,0:T(8,128)S(1)} %shard_map.71.mine), channel_id=1, source_target_pairs={{0,256},{256,0},{1,257},{257,1},{2,258},{258,2},{3,259},{259,3},{4... | collective-permute-start | bytes 122888 | tf_op jit(solution)/shard_map/ppermute | solution.py:33
  122.0 7.9 %collective-permute-done.3.theirs = f32[5,8,256]{2,1,0:T(8,128)S(1)} collective-permute-done((f32[5,8,256]{2,1,0:T(8,128)S(1)}, f32[5,8,256]{2,1,0:T(8,128)S(1)}, u32[]{:S(2)}, u32[]{:S(2)}) %collective-permute-start.3) | collective-permute-done | bytes 40992 | tf_op jit(solution)/shard_map/ppermute | solution.py:33
  130.1 11.2 %all_to_all.46.h_got = f32[8,16,256]{2,1,0:T(8,128)S(1)} all-to-all(f32[8,16,256]{2,1,0:T(8,128)S(1)} %get-tuple-element.28), channel_id=1, replica_groups=mesh['z4'=2,'z2'=2,'z1'=2,'core'=2,'zh'=2,'y'=4,'x'=4] {'z2','z1','core'}, dimensions={0} | all-to-all | bytes 262144 | tf_op jit(solution)/shard_map/all_to_all | solution.py:29
  141.7 11.1 %all_to_all.47.got = f32[16,4,640]{2,1,0:T(4,128)S(1)} all-to-all(f32[16,4,640]{2,1,0:T(4,128)S(1)} %shard_map.73), channel_id=1, replica_groups=mesh['z4'=2,'z2'=2,'z1'=2,'core'=2,'zh'=2,'y'=4,'x'=4] {'y','x'}, dimensions={0} | all-to-all | bytes 327680 | tf_op jit(solution)/shard_map/all_to_all | solution.py:29
  153.1 8.6 %collective-permute-start.4 = (f32[5,2,256]{2,1,0:T(2,128)S(1)}, f32[5,2,256]{2,1,0:T(2,128)S(1)}, u32[]{:S(2)}, u32[]{:S(2)}) collective-permute-start(f32[5,2,256]{2,1,0:T(2,128)S(1)} %get-tuple-element.30), channel_id=1, source_target_pairs={{0,16},{16,0},{1,17},{17,1},{2,18},{18,2},{3,19},{19,3},{4,20},{20... | collective-permute-start | bytes 30728 | tf_op jit(solution)/shard_map/ppermute | solution.py:33
  162.3 5.0 %collective-permute-done.4.theirs = f32[5,2,256]{2,1,0:T(2,128)S(1)} collective-permute-done((f32[5,2,256]{2,1,0:T(2,128)S(1)}, f32[5,2,256]{2,1,0:T(2,128)S(1)}, u32[]{:S(2)}, u32[]{:S(2)}) %collective-permute-start.4) | collective-permute-done | bytes 10272 | tf_op jit(solution)/shard_map/ppermute | solution.py:33
  167.4 0.8 shard_map.75
  (20 shorter events, 4.1 us)
Async XLA Ops:
  0.6 14.5 %collective-permute-start = (f32[2,1024]{1,0:T(2,128)}, f32[2,1024]{1,0:T(2,128)S(1)}, u32[]{:S(2)}, u32[]{:S(2)}) collective-permute-start(f32[2,1024]{1,0:T(2,128)} %w.1), channel_id=1, source_target_pairs={{0,16},{16,0},{1,17},{17,1},{2,18},{18,2},{3,19},{19,3},{4,20},{20... | collective-permute-start | bytes 24584 | tf_op jit(solution)/shard_map/ppermute | solution.py:33
  11.6 1.0 copy-start
  12.6 0.7 copy-start.2
  15.1 15.7 %copy-start.1 = (f32[4,1024]{1,0:T(4,128)S(1)}, f32[4,1024]{1,0:T(4,128)}, u32[]{:S(2)}) copy-start(f32[4,1024]{1,0:T(4,128)} %h.1) | copy-start | bytes 49156
  47.7 10.1 %collective-permute-start.1 = (f32[128,128]{1,0:T(8,128)S(1)}, f32[128,128]{1,0:T(8,128)S(1)}, u32[]{:S(2)}, u32[]{:S(2)}) collective-permute-start(f32[128,128]{1,0:T(8,128)S(1)} %get-tuple-element.23.mine), channel_id=1, source_target_pairs={{0,256},{256,0},{1,257},{257,1},{2,258},{258,2},{3,259},{259,3},{4... | collective-permute-start | bytes 196616 | tf_op jit(solution)/shard_map/ppermute | solution.py:33
  83.2 14.4 %collective-permute-start.2 = (f32[5,4,256]{2,1,0:T(4,128)S(1)}, f32[5,4,256]{2,1,0:T(4,128)S(1)}, u32[]{:S(2)}, u32[]{:S(2)}) collective-permute-start(f32[5,4,256]{2,1,0:T(4,128)S(1)} %shard_map.67.mine), channel_id=1, source_target_pairs={{0,16},{16,0},{1,17},{17,1},{2,18},{18,2},{3,19},{19,3},{4,20},{20... | collective-permute-start | bytes 61448 | tf_op jit(solution)/shard_map/ppermute | solution.py:33
  120.0 9.8 %collective-permute-start.3 = (f32[5,8,256]{2,1,0:T(8,128)S(1)}, f32[5,8,256]{2,1,0:T(8,128)S(1)}, u32[]{:S(2)}, u32[]{:S(2)}) collective-permute-start(f32[5,8,256]{2,1,0:T(8,128)S(1)} %shard_map.71.mine), channel_id=1, source_target_pairs={{0,256},{256,0},{1,257},{257,1},{2,258},{258,2},{3,259},{259,3},{4... | collective-permute-start | bytes 122888 | tf_op jit(solution)/shard_map/ppermute | solution.py:33
  153.1 14.3 %collective-permute-start.4 = (f32[5,2,256]{2,1,0:T(2,128)S(1)}, f32[5,2,256]{2,1,0:T(2,128)S(1)}, u32[]{:S(2)}, u32[]{:S(2)}) collective-permute-start(f32[5,2,256]{2,1,0:T(2,128)S(1)} %get-tuple-element.30), channel_id=1, source_target_pairs={{0,16},{16,0},{1,17},{17,1},{2,18},{18,2},{3,19},{19,3},{4,20},{20... | collective-permute-start | bytes 30728 | tf_op jit(solution)/shard_map/ppermute | solution.py:33

commit v10 on v9

--- a/solution.py
+++ b/solution.py
@@ -100,18 +100,22 @@
     return w_slots[j]
 
 
-def h1_terms_kernel(blk, w0, h, values, w_own, out, rows, w_slots):
+def h1_terms_kernel(blk, w0, h, h_other, values, w_own, out, rows, w_slots):
     for j in range(CAP):
         upper, gram = grams(w_slot(w0, j, blk, w_slots), both_of(values, j), live_of(blk, j))
         for side in range(2):
             at = 128 * j + RANK * side
             out[at : at + RANK, :] = upper[:, COLS * side : COLS * (side + 1)]
         out[256 + 32 * j : 288 + 32 * j, :] = jnp.concatenate([gram[:32], gram[32:]], axis=1)
+    first = lax.axis_index("z4") == 0
+    low = jnp.where(first, h[...], h_other[...])
+    high = jnp.where(first, h_other[...], h[...])
+    old = jnp.concatenate([low[0:2], high[0:2], low[2:4], high[2:4]], axis=0)
     for q in range(NH):
-        at = 320 + 16 * (q % 2) + 4 * (q // 2)
-        out[at : at + 4, :] = h[:, COLS * q : COLS * (q + 1)]
+        at = 320 + 32 * (q % 2) + 8 * (q // 2)
+        out[at : at + 8, :] = old[:, COLS * q : COLS * (q + 1)]
     lane = lax.broadcasted_iota(jnp.int32, (8, COLS), 1)
-    out[352:360, :] = jnp.where(lane == 0, blk[CAP], blk[CAP + 1]).astype(jnp.float32)
+    out[384:392, :] = jnp.where(lane == 0, blk[CAP], blk[CAP + 1]).astype(jnp.float32)
     plane = lax.axis_index(PLANE)
     for b in range(NB):
         w_own[b] = w0[plane, :, b * BS : (b + 1) * BS]
@@ -123,40 +127,33 @@
     core = lax.axis_index("core")
     out[:, :96, :] = jnp.zeros((NQ, 96, COLS), jnp.float32)
     for i in range(2):
-        read_list(lists, i, pair[i, 352:353, :])
+        read_list(lists, i, pair[i, 384:385, :])
         for j in range(CAP):
             q = lists[CAP * i + j]
             at = pl.multiple_of(128 * j + RANK * core, 8)
             out[q, :64, :] = out[q, :64, :] + pair[i, pl.ds(at, RANK), :]
             out[q, 64:96, :] = out[q, 64:96, :] + pair[i, 256 + 32 * j : 288 + 32 * j, :]
-        side = pair[i, pl.ds(pl.multiple_of(320 + 16 * core, 8), 16), :]
+        side = pair[i, pl.ds(pl.multiple_of(320 + 32 * core, 8), 32), :]
         for q in range(NQ):
-            out[q, 96 + 4 * i : 100 + 4 * i, :] = side[4 * q : 4 * q + 4]
-            out[q, 104 + 4 * i : 108 + 4 * i, :] = pair[i, 352:356, :]
-
-
-def h1_collect_kernel(got, out, cols):
+            out[q, 96 + 8 * i : 104 + 8 * i, :] = side[8 * q : 8 * q + 8]
+            out[q, 112 + 4 * i : 116 + 4 * i, :] = pair[i, 384:388, :]
+
+
+def h1_collect_kernel(got, out, old, cols):
     total = got[0, :96, :]
     for q in range(1, NQ):
         total = total + got[q, :96, :]
-    out[:96, :] = total
+    out[...] = total
     for q in range(NQ):
-        out[96 + 8 * q : 104 + 8 * q, :] = got[q, 96:104, :]
+        old[16 * q : 16 * q + 16, :] = got[q, 96:112, :]
         for i in range(2):
-            read_list(cols, 2 * q + i, got[q, 104 + 4 * i : 105 + 4 * i, :])
-
-
-def h1_update_kernel(mine, theirs, out):
-    total = mine[:96, :] + theirs[:96, :]
+            read_list(cols, 2 * q + i, got[q, 112 + 4 * i : 113 + 4 * i, :])
+
+
+def h1_update_kernel(mine, theirs, old, out):
+    total = mine[...] + theirs[...]
     gram = jnp.concatenate([total[64:, :64], total[64:, 64:]], axis=0)
-    first = lax.axis_index("z4") == 0
-    low = jnp.where(first, mine[96:, :], theirs[96:, :])
-    high = jnp.where(first, theirs[96:, :], mine[96:, :])
-    pairs = []
-    for k in range(16):
-        pairs += [low[2 * k : 2 * k + 2], high[2 * k : 2 * k + 2]]
-    old = jnp.concatenate(pairs, axis=0)
-    new = old * total[:64] / product(halves(gram), halves(old))
+    new = old[...] * total[:64] / product(halves(gram), halves(old[...]))
     for q in range(NQ):
         out[q] = new
 
@@ -288,6 +285,7 @@
     wide = NB * BS + TAB
 
     w_other = swap(w_factor, "zh")
+    h_other = swap(h_factor, "z4")
     values, turned, w_mine, blk = call(
         prepare_kernel,
         (blocks[0, 0],),
@@ -297,23 +295,24 @@
         tables=[(2 * CAP,)],
     )
     (w_pair,) = call(w_pair_kernel, (blk,), (w_mine, w_other), [(NP, 4, wide)], scratch=[(4, wide)])
+    w_pair, h_other = lax.optimization_barrier((w_pair, h_other))
     w_got = exchange(w_pair, PLANE)
 
     w_own, sent, rows = call(
         h1_terms_kernel,
         (blk,),
-        (w_got, h_factor, values),
-        [(NB, 4, BS), (360, COLS)],
+        (w_got, h_factor, h_other, values),
+        [(NB, 4, BS), (392, COLS)],
         tables=[(NP * CAP,)],
         scratch=[(CAP, RANK, BS)],
     )
     pair = lax.all_gather(sent, "core", axis=0)
-    (sent,) = call(h1_build_kernel, (), (pair,), [(NQ, 112, COLS)], counts=(2 * CAP,))
+    (sent,) = call(h1_build_kernel, (), (pair,), [(NQ, 120, COLS)], counts=(2 * CAP,))
     got = exchange(sent, QUAD)
-    mine, cols = call(h1_collect_kernel, (), (got,), [(128, COLS)], tables=[(NH * CAP,)])
+    mine, old, cols = call(h1_collect_kernel, (), (got,), [(96, COLS), (RANK, COLS)], tables=[(NH * CAP,)])
     theirs = swap(mine, "z4")
     (w_all,) = call(w_arrange_kernel, (), (w_got,), [(NB, RANK, BS)])
-    (out,) = call(h1_update_kernel, (), (mine, theirs), [(NQ, RANK, COLS)])
+    (out,) = call(h1_update_kernel, (), (mine, theirs, old), [(NQ, RANK, COLS)])
     h_all = lax.all_gather(exchange(out, QUAD), "core", axis=0)
 
     wide = CAP * (BS + RANK)

time: 169 us -> 175 us (1.036)
  the two profiles are of different devices: /device:TPU:128 before, /device:TPU:2 now
where the time goes in v10:
time: 175 us; the launch traced here: 174 us
  blocking collectives  94.6 us (54%)
  starting transfers between devices  40.9 us (23%)
  waiting for transfers between devices  30.6 us (17%)
  Pallas kernels  5.16 us (3%)
  local copies, waits for them, and re-layouts  2.35 us (1%)
    all_to_all x8, blocking collectives, exchange(): return lax.all_to_all(x, axes, split_axis=0, concat_axis=0, tiled=True)  90.5 us
    ppermute x6, starting transfers between devices, swap(): return lax.ppermute(x, axis, [(0, 1), (1, 0)])  40.9 us
    ppermute x6, waiting for transfers between devices, swap(): return lax.ppermute(x, axis, [(0, 1), (1, 0)])  30.6 us
    pallas_call x17, Pallas kernels, call(): pl.pallas_call(body, in_specs=[smem] * len(scalars) + [vmem] * len(arrays...  5.16 us
  transfers between devices with their start and end apart: 6, of which 5 were waited for; matrix products, arithmetic and copies ran while one was open for 0% of the time, Pallas kernels for 1%

profile of v10, /device:TPU:2, one launch (start us, length us, event | category | flops | bytes accessed | tf_op | source)
XLA Modules:
  0.0 174.4 jit_solution(12488082924784696290)
XLA Ops:
  0.6 9.1 %collective-permute-start.1 = (f32[4,1024]{1,0:T(4,128)}, f32[4,1024]{1,0:T(4,128)S(1)}, u32[]{:S(2)}, u32[]{:S(2)}) collective-permute-start(f32[4,1024]{1,0:T(4,128)} %h.1), channel_id=1, source_target_pairs={{0,256},{256,0},{1,257},{257,1},{2,258},{258,2},{3,259},{259,3},{4... | collective-permute-start | bytes 49160 | tf_op jit(solution)/shard_map/ppermute | solution.py:33
  9.7 10.9 %collective-permute-start = (f32[2,1024]{1,0:T(2,128)}, f32[2,1024]{1,0:T(2,128)S(1)}, u32[]{:S(2)}, u32[]{:S(2)}) collective-permute-start(f32[2,1024]{1,0:T(2,128)} %w.1), channel_id=1, source_target_pairs={{0,16},{16,0},{1,17},{17,1},{2,18},{18,2},{3,19},{19,3},{4,20},{20... | collective-permute-start | bytes 24584 | tf_op jit(solution)/shard_map/ppermute | solution.py:33
  20.7 1.0 copy-done
  22.4 0.9 shard_map.59
  23.3 0.9 collective-permute-done.theirs
  24.3 14.8 %all_to_all.40.w0 = f32[16,4,1152]{2,1,0:T(4,128)S(1)} all-to-all(f32[16,4,1152]{2,1,0:T(4,128)S(1)} %shard_map.60), channel_id=1, replica_groups=mesh['z4'=2,'z2'=2,'z1'=2,'core'=2,'zh'=2,'y'=4,'x'=4] {'y','x'}, dimensions={0} | all-to-all | bytes 589824 | tf_op jit(solution)/shard_map/all_to_all | solution.py:29
  39.4 2.1 %all-gather = f32[784,128]{1,0:T(8,128)S(1)} all-gather(f32[392,128]{1,0:T(8,128)S(1)} %get-tuple-element.27), channel_id=2, replica_groups=mesh['z4'=2,'z2'=2,'z1'=2,'core'=2,'zh'=2,'y'=4,'x'=4] {'core'}, dimensions={0}, use_global_device_ids=true | all-gather | bytes 602112 | tf_op jit(solution)/shard_map/all_gather | solution.py:309
  41.7 14.5 %all_to_all.41.got = f32[4,120,128]{2,1,0:T(8,128)S(1)} all-to-all(f32[4,120,128]{2,1,0:T(8,128)S(1)} %shard_map.63), channel_id=1, replica_groups=mesh['z4'=2,'z2'=2,'z1'=2,'core'=2,'zh'=2,'y'=4,'x'=4] {'z2','z1'}, dimensions={0} | all-to-all | bytes 491520 | tf_op jit(solution)/shard_map/all_to_all | solution.py:29
  56.3 1.9 %collective-permute-start.2 = (f32[96,128]{1,0:T(8,128)S(1)}, f32[96,128]{1,0:T(8,128)S(1)}, u32[]{:S(2)}, u32[]{:S(2)}) collective-permute-start(f32[96,128]{1,0:T(8,128)S(1)} %get-tuple-element.28.mine), channel_id=1, source_target_pairs={{0,256},{256,0},{1,257},{257,1},{2,258},{258,2},{3,259},{259,3},{4... | collective-permute-start | bytes 147464 | tf_op jit(solution)/shard_map/ppermute | solution.py:33
  58.2 9.4 %collective-permute-done.2.theirs = f32[96,128]{1,0:T(8,128)S(1)} collective-permute-done((f32[96,128]{1,0:T(8,128)S(1)}, f32[96,128]{1,0:T(8,128)S(1)}, u32[]{:S(2)}, u32[]{:S(2)}) %collective-permute-start.2) | collective-permute-done | bytes 49184 | tf_op jit(solution)/shard_map/ppermute | solution.py:33
  67.9 8.3 %all_to_all.42 = f32[4,64,128]{2,1,0:T(8,128)S(1)} all-to-all(f32[4,64,128]{2,1,0:T(8,128)S(1)} %shard_map.65), channel_id=1, replica_groups=mesh['z4'=2,'z2'=2,'z1'=2,'core'=2,'zh'=2,'y'=4,'x'=4] {'z2','z1'}, dimensions={0} | all-to-all | bytes 262144 | tf_op jit(solution)/shard_map/all_to_all | solution.py:29
  76.2 2.0 %all-gather.1 = f32[8,64,128]{2,1,0:T(8,128)S(1)} all-gather(f32[4,64,128]{2,1,0:T(8,128)S(1)} %all_to_all.42), channel_id=3, replica_groups=mesh['z4'=2,'z2'=2,'z1'=2,'core'=2,'zh'=2,'y'=4,'x'=4] {'core'}, dimensions={0}, use_global_device_ids=true | all-gather | bytes 393216 | tf_op jit(solution)/shard_map/all_gather | solution.py:316
  78.5 11.0 %all_to_all.43.got = f32[16,4,640]{2,1,0:T(4,128)S(1)} all-to-all(f32[16,4,640]{2,1,0:T(4,128)S(1)} %shard_map.66), channel_id=1, replica_groups=mesh['z4'=2,'z2'=2,'z1'=2,'core'=2,'zh'=2,'y'=4,'x'=4] {'y','x'}, dimensions={0} | all-to-all | bytes 327680 | tf_op jit(solution)/shard_map/all_to_all | solution.py:29
  89.9 8.2 %collective-permute-start.3 = (f32[5,4,256]{2,1,0:T(4,128)S(1)}, f32[5,4,256]{2,1,0:T(4,128)S(1)}, u32[]{:S(2)}, u32[]{:S(2)}) collective-permute-start(f32[5,4,256]{2,1,0:T(4,128)S(1)} %shard_map.67.mine), channel_id=1, source_target_pairs={{0,16},{16,0},{1,17},{17,1},{2,18},{18,2},{3,19},{19,3},{4,20},{20... | collective-permute-start | bytes 61448 | tf_op jit(solution)/shard_map/ppermute | solution.py:33
  98.2 6.1 %collective-permute-done.3.theirs = f32[5,4,256]{2,1,0:T(4,128)S(1)} collective-permute-done((f32[5,4,256]{2,1,0:T(4,128)S(1)}, f32[5,4,256]{2,1,0:T(4,128)S(1)}, u32[]{:S(2)}, u32[]{:S(2)}) %collective-permute-start.3) | collective-permute-done | bytes 20512 | tf_op jit(solution)/shard_map/ppermute | solution.py:33
  104.5 11.7 %all_to_all.44.w0.w_got = f32[16,4,1024]{2,1,0:T(4,128)S(1)} all-to-all(f32[16,4,1024]{2,1,0:T(4,128)S(1)} %get-tuple-element.32), channel_id=1, replica_groups=mesh['z4'=2,'z2'=2,'z1'=2,'core'=2,'zh'=2,'y'=4,'x'=4] {'y','x'}, dimensions={0} | all-to-all | bytes 524288 | tf_op jit(solution)/shard_map/all_to_all | solution.py:29
  116.6 10.0 %all_to_all.45.got = f32[8,8,640]{2,1,0:T(8,128)S(1)} all-to-all(f32[8,8,640]{2,1,0:T(8,128)S(1)} %shard_map.70), channel_id=1, replica_groups=mesh['z4'=2,'z2'=2,'z1'=2,'core'=2,'zh'=2,'y'=4,'x'=4] {'z2','z1','core'}, dimensions={0} | all-to-all | bytes 327680 | tf_op jit(solution)/shard_map/all_to_all | solution.py:29
  126.8 2.8 %collective-permute-start.4 = (f32[5,8,256]{2,1,0:T(8,128)S(1)}, f32[5,8,256]{2,1,0:T(8,128)S(1)}, u32[]{:S(2)}, u32[]{:S(2)}) collective-permute-start(f32[5,8,256]{2,1,0:T(8,128)S(1)} %shard_map.71.mine), channel_id=1, source_target_pairs={{0,256},{256,0},{1,257},{257,1},{2,258},{258,2},{3,259},{259,3},{4... | collective-permute-start | bytes 122888 | tf_op jit(solution)/shard_map/ppermute | solution.py:33
  129.6 8.5 %collective-permute-done.4.theirs = f32[5,8,256]{2,1,0:T(8,128)S(1)} collective-permute-done((f32[5,8,256]{2,1,0:T(8,128)S(1)}, f32[5,8,256]{2,1,0:T(8,128)S(1)}, u32[]{:S(2)}, u32[]{:S(2)}) %collective-permute-start.4) | collective-permute-done | bytes 40992 | tf_op jit(solution)/shard_map/ppermute | solution.py:33
  138.3 9.1 %all_to_all.46.h_got = f32[8,16,256]{2,1,0:T(8,128)S(1)} all-to-all(f32[8,16,256]{2,1,0:T(8,128)S(1)} %get-tuple-element.34), channel_id=1, replica_groups=mesh['z4'=2,'z2'=2,'z1'=2,'core'=2,'zh'=2,'y'=4,'x'=4] {'z2','z1','core'}, dimensions={0} | all-to-all | bytes 262144 | tf_op jit(solution)/shard_map/all_to_all | solution.py:29
  147.8 11.1 %all_to_all.47.got = f32[16,4,640]{2,1,0:T(4,128)S(1)} all-to-all(f32[16,4,640]{2,1,0:T(4,128)S(1)} %shard_map.73), channel_id=1, replica_groups=mesh['z4'=2,'z2'=2,'z1'=2,'core'=2,'zh'=2,'y'=4,'x'=4] {'y','x'}, dimensions={0} | all-to-all | bytes 327680 | tf_op jit(solution)/shard_map/all_to_all | solution.py:29
  159.3 8.0 %collective-permute-start.5 = (f32[5,2,256]{2,1,0:T(2,128)S(1)}, f32[5,2,256]{2,1,0:T(2,128)S(1)}, u32[]{:S(2)}, u32[]{:S(2)}) collective-permute-start(f32[5,2,256]{2,1,0:T(2,128)S(1)} %get-tuple-element.36), channel_id=1, source_target_pairs={{0,16},{16,0},{1,17},{17,1},{2,18},{18,2},{3,19},{19,3},{4,20},{20... | collective-permute-start | bytes 30728 | tf_op jit(solution)/shard_map/ppermute | solution.py:33
  167.9 5.6 %collective-permute-done.5.theirs = f32[5,2,256]{2,1,0:T(2,128)S(1)} collective-permute-done((f32[5,2,256]{2,1,0:T(2,128)S(1)}, f32[5,2,256]{2,1,0:T(2,128)S(1)}, u32[]{:S(2)}, u32[]{:S(2)}) %collective-permute-start.5) | collective-permute-done | bytes 10272 | tf_op jit(solution)/shard_map/ppermute | solution.py:33
  173.6 0.8 shard_map.75
  (22 shorter events, 4.8 us)
Async XLA Ops:
  0.6 23.6 %collective-permute-start.1 = (f32[4,1024]{1,0:T(4,128)}, f32[4,1024]{1,0:T(4,128)S(1)}, u32[]{:S(2)}, u32[]{:S(2)}) collective-permute-start(f32[4,1024]{1,0:T(4,128)} %h.1), channel_id=1, source_target_pairs={{0,256},{256,0},{1,257},{257,1},{2,258},{258,2},{3,259},{259,3},{4... | collective-permute-start | bytes 49160 | tf_op jit(solution)/shard_map/ppermute | solution.py:33
  9.7 14.5 %collective-permute-start = (f32[2,1024]{1,0:T(2,128)}, f32[2,1024]{1,0:T(2,128)S(1)}, u32[]{:S(2)}, u32[]{:S(2)}) collective-permute-start(f32[2,1024]{1,0:T(2,128)} %w.1), channel_id=1, source_target_pairs={{0,16},{16,0},{1,17},{17,1},{2,18},{18,2},{3,19},{19,3},{4,20},{20... | collective-permute-start | bytes 24584 | tf_op jit(solution)/shard_map/ppermute | solution.py:33
  20.7 1.0 copy-start
  21.7 0.7 copy-start.2
  24.2 14.8 %copy-start.1 = (f32[4,1024]{1,0:T(4,128)S(1)}, f32[4,1024]{1,0:T(4,128)}, u32[]{:S(2)}) copy-start(f32[4,1024]{1,0:T(4,128)} %h.1) | copy-start | bytes 49156
  56.3 11.3 %collective-permute-start.2 = (f32[96,128]{1,0:T(8,128)S(1)}, f32[96,128]{1,0:T(8,128)S(1)}, u32[]{:S(2)}, u32[]{:S(2)}) collective-permute-start(f32[96,128]{1,0:T(8,128)S(1)} %get-tuple-element.28.mine), channel_id=1, source_target_pairs={{0,256},{256,0},{1,257},{257,1},{2,258},{258,2},{3,259},{259,3},{4... | collective-permute-start | bytes 147464 | tf_op jit(solution)/shard_map/ppermute | solution.py:33
  89.9 14.4 %collective-permute-start.3 = (f32[5,4,256]{2,1,0:T(4,128)S(1)}, f32[5,4,256]{2,1,0:T(4,128)S(1)}, u32[]{:S(2)}, u32[]{:S(2)}) collective-permute-start(f32[5,4,256]{2,1,0:T(4,128)S(1)} %shard_map.67.mine), channel_id=1, source_target_pairs={{0,16},{16,0},{1,17},{17,1},{2,18},{18,2},{3,19},{19,3},{4,20},{20... | collective-permute-start | bytes 61448 | tf_op jit(solution)/shard_map/ppermute | solution.py:33
  126.8 11.3 %collective-permute-start.4 = (f32[5,8,256]{2,1,0:T(8,128)S(1)}, f32[5,8,256]{2,1,0:T(8,128)S(1)}, u32[]{:S(2)}, u32[]{:S(2)}) collective-permute-start(f32[5,8,256]{2,1,0:T(8,128)S(1)} %shard_map.71.mine), channel_id=1, source_target_pairs={{0,256},{256,0},{1,257},{257,1},{2,258},{258,2},{3,259},{259,3},{4... | collective-permute-start | bytes 122888 | tf_op jit(solution)/shard_map/ppermute | solution.py:33
  159.3 14.3 %collective-permute-start.5 = (f32[5,2,256]{2,1,0:T(2,128)S(1)}, f32[5,2,256]{2,1,0:T(2,128)S(1)}, u32[]{:S(2)}, u32[]{:S(2)}) collective-permute-start(f32[5,2,256]{2,1,0:T(2,128)S(1)} %get-tuple-element.36), channel_id=1, source_target_pairs={{0,16},{16,0},{1,17},{17,1},{2,18},{18,2},{3,19},{19,3},{4,20},{20... | collective-permute-start | bytes 30728 | tf_op jit(solution)/shard_map/ppermute | solution.py:33

commit v11 on v9

--- a/solution.py
+++ b/solution.py
@@ -73,19 +73,13 @@
     return jnp.maximum(blk[CAP * d + j], 0)
 
 
-def with_list(rows, blk, d, lists):
-    lane = lax.broadcasted_iota(jnp.int32, (rows.shape[0], TAB), 1)
-    lists[:, : NB * BS] = rows
-    lists[:, NB * BS :] = jnp.where(lane == 0, blk[CAP * d], blk[CAP * d + 1]).astype(jnp.float32)
-
-
-def w_pair_kernel(blk, mine, theirs, out, message):
+def w_pair_kernel(mine, theirs, out):
     first = lax.axis_index("zh") == 0
     low = jnp.where(first, mine[...], theirs[...])
     high = jnp.where(first, theirs[...], mine[...])
-    with_list(jnp.concatenate([low, high], axis=0), blk, 0, message)
+    both = jnp.concatenate([low, high], axis=0)
     for q in range(NP):
-        out[q] = message[...]
+        out[q] = both
 
 
 def read_list(table, q, listed):
@@ -100,7 +94,7 @@
     return w_slots[j]
 
 
-def h1_terms_kernel(blk, w0, h, values, w_own, out, rows, w_slots):
+def h1_terms_kernel(blk, w0, h, values, w_own, out, w_slots):
     for j in range(CAP):
         upper, gram = grams(w_slot(w0, j, blk, w_slots), both_of(values, j), live_of(blk, j))
         for side in range(2):
@@ -115,8 +109,6 @@
     plane = lax.axis_index(PLANE)
     for b in range(NB):
         w_own[b] = w0[plane, :, b * BS : (b + 1) * BS]
-    for q in range(NP):
-        read_list(rows, q, w0[q, 0:1, NB * BS :])
 
 
 def h1_build_kernel(pair, out, lists):
@@ -171,7 +163,7 @@
     for q in range(out.shape[0]):
         for j in range(CAP):
             out[q, :, BS * j : BS * (j + 1)] = terms[j][0][rows * q : rows * (q + 1), :]
-        out[q, :, CAP * BS :] = both[rows * q : rows * (q + 1), :]
+        out[q, :, CAP * BS : CAP * (BS + RANK)] = both[rows * q : rows * (q + 1), :]
 
 
 def w1_terms_kernel(blk, h_all, values, out):
@@ -180,6 +172,10 @@
         h_slot = whole_block(h_all, block_of(blk, 1, j))
         terms.append(grams(h_slot, both_of(values, j), live_of(blk, j)))
     send_grams(out, terms)
+    lane = lax.broadcasted_iota(jnp.int32, (4, TAB), 1)
+    listed = jnp.where(lane == 0, blk[0], blk[1]).astype(jnp.float32)
+    for q in range(NP):
+        out[q, :, CAP * (BS + RANK) :] = listed
 
 
 def w2_terms_kernel(blk, h_got, values, out):
@@ -202,7 +198,7 @@
     out[...] = jnp.zeros(out.shape, out.dtype)
     half = lax.broadcasted_iota(jnp.int32, (rows, CAP * RANK), 1) // RANK
     for q in range(got.shape[0]):
-        grams = got[q, :, CAP * BS :]
+        grams = got[q, :, CAP * BS : CAP * (BS + RANK)]
         turned = jnp.concatenate([grams[:, RANK:], grams[:, :RANK]], axis=1)
         for j in range(CAP):
             b = table[q * CAP + j]
@@ -211,6 +207,12 @@
             at = pl.ds(pl.multiple_of(b // 2 * CAP * RANK, CAP * RANK), CAP * RANK)
             mine = jnp.where(side == j, grams, turned)
             out[NB, :, at] = out[NB, :, at] + jnp.where(half == side, mine, 0.0)
+
+
+def w1_collect_kernel(got, out, rows):
+    for q in range(NP):
+        read_list(rows, q, got[q, 0:1, CAP * (BS + RANK) :])
+    gram_collect_kernel(rows, got, out)
 
 
 def owned(own, whole, mine, theirs, b):
@@ -285,8 +287,6 @@
 
 
 def per_device(blocks, observed, w_factor, h_factor):
-    wide = NB * BS + TAB
-
     w_other = swap(w_factor, "zh")
     values, turned, w_mine, blk = call(
         prepare_kernel,
@@ -296,16 +296,11 @@
         dtypes=[jnp.bfloat16, jnp.bfloat16, jnp.float32],
         tables=[(2 * CAP,)],
     )
-    (w_pair,) = call(w_pair_kernel, (blk,), (w_mine, w_other), [(NP, 4, wide)], scratch=[(4, wide)])
+    (w_pair,) = call(w_pair_kernel, (), (w_mine, w_other), [(NP, 4, NB * BS)])
     w_got = exchange(w_pair, PLANE)
 
-    w_own, sent, rows = call(
-        h1_terms_kernel,
-        (blk,),
-        (w_got, h_factor, values),
-        [(NB, 4, BS), (360, COLS)],
-        tables=[(NP * CAP,)],
-        scratch=[(CAP, RANK, BS)],
+    w_own, sent = call(
+        h1_terms_kernel, (blk,), (w_got, h_factor, values), [(NB, 4, BS), (360, COLS)], scratch=[(CAP, RANK, BS)]
     )
     pair = lax.all_gather(sent, "core", axis=0)
     (sent,) = call(h1_build_kernel, (), (pair,), [(NQ, 112, COLS)], counts=(2 * CAP,))
@@ -317,9 +312,9 @@
     h_all = lax.all_gather(exchange(out, QUAD), "core", axis=0)
 
     wide = CAP * (BS + RANK)
-    (sent,) = call(w1_terms_kernel, (blk,), (h_all, turned), [(NP, 4, wide)])
+    (sent,) = call(w1_terms_kernel, (blk,), (h_all, turned), [(NP, 4, wide + TAB)])
     got = exchange(sent, PLANE)
-    (mine,) = call(gram_collect_kernel, (rows,), (got,), [(NB + 1, 4, BS)])
+    mine, rows = call(w1_collect_kernel, (), (got,), [(NB + 1, 4, BS)], tables=[(NP * CAP,)])
     theirs = swap(mine, "zh")
     w_own, out = call(w1_update_kernel, (), (w_own, w_all, mine, theirs), [(NB, 4, BS), (NP, 4, NB * BS)])
     w_got = exchange(out, PLANE)

time: 169 us -> 169 us (level)
  no operation moved by 1% of the time
where the time goes in v11:
time: 169 us; the launch traced here: 168 us
  blocking collectives  100 us (59%)
  starting transfers between devices  31.6 us (19%)
  waiting for transfers between devices  28.1 us (17%)
  Pallas kernels  5.24 us (3%)
  local copies, waits for them, and re-layouts  2.35 us (1%)
    all_to_all x8, blocking collectives, exchange(): return lax.all_to_all(x, axes, split_axis=0, concat_axis=0, tiled=True)  96.2 us
    ppermute x5, starting transfers between devices, swap(): return lax.ppermute(x, axis, [(0, 1), (1, 0)])  31.6 us
    ppermute x5, waiting for transfers between devices, swap(): return lax.ppermute(x, axis, [(0, 1), (1, 0)])  28.1 us
    pallas_call x17, Pallas kernels, call(): pl.pallas_call(body, in_specs=[smem] * len(scalars) + [vmem] * len(arrays...  5.24 us
  transfers between devices with their start and end apart: 5, of which 5 were waited for; matrix products, arithmetic and copies ran while one was open for 0% of the time, Pallas kernels for 1%

profile of v11, /device:TPU:128, one launch (start us, length us, event | category | flops | bytes accessed | tf_op | source)
XLA Modules:
  0.0 168.3 jit_solution(899617359295668328)
XLA Ops:
  0.6 10.9 %collective-permute-start = (f32[2,1024]{1,0:T(2,128)}, f32[2,1024]{1,0:T(2,128)S(1)}, u32[]{:S(2)}, u32[]{:S(2)}) collective-permute-start(f32[2,1024]{1,0:T(2,128)} %w.1), channel_id=1, source_target_pairs={{0,16},{16,0},{1,17},{17,1},{2,18},{18,2},{3,19},{19,3},{4,20},{20... | collective-permute-start | bytes 24584 | tf_op jit(solution)/shard_map/ppermute | solution.py:33
  11.6 1.0 copy-done
  12.6 0.7 copy-done.2
  13.3 0.9 shard_map.59
  14.2 0.9 collective-permute-done.theirs
  15.1 15.5 %all_to_all.40.w0 = f32[16,4,1024]{2,1,0:T(4,128)S(1)} all-to-all(f32[16,4,1024]{2,1,0:T(4,128)S(1)} %shard_map.60), channel_id=1, replica_groups=mesh['z4'=2,'z2'=2,'z1'=2,'core'=2,'zh'=2,'y'=4,'x'=4] {'y','x'}, dimensions={0} | all-to-all | bytes 524288 | tf_op jit(solution)/shard_map/all_to_all | solution.py:29
  31.1 2.1 %all-gather = f32[720,128]{1,0:T(8,128)S(1)} all-gather(f32[360,128]{1,0:T(8,128)S(1)} %get-tuple-element.22), channel_id=2, replica_groups=mesh['z4'=2,'z2'=2,'z1'=2,'core'=2,'zh'=2,'y'=4,'x'=4] {'core'}, dimensions={0}, use_global_device_ids=true | all-gather | bytes 552960 | tf_op jit(solution)/shard_map/all_gather | solution.py:305
  33.3 14.2 %all_to_all.41.got = f32[4,112,128]{2,1,0:T(8,128)S(1)} all-to-all(f32[4,112,128]{2,1,0:T(8,128)S(1)} %shard_map.63), channel_id=1, replica_groups=mesh['z4'=2,'z2'=2,'z1'=2,'core'=2,'zh'=2,'y'=4,'x'=4] {'z2','z1'}, dimensions={0} | all-to-all | bytes 458752 | tf_op jit(solution)/shard_map/all_to_all | solution.py:29
  47.6 1.9 %collective-permute-start.1 = (f32[128,128]{1,0:T(8,128)S(1)}, f32[128,128]{1,0:T(8,128)S(1)}, u32[]{:S(2)}, u32[]{:S(2)}) collective-permute-start(f32[128,128]{1,0:T(8,128)S(1)} %get-tuple-element.23.mine), channel_id=1, source_target_pairs={{0,256},{256,0},{1,257},{257,1},{2,258},{258,2},{3,259},{259,3},{4... | collective-permute-start | bytes 196616 | tf_op jit(solution)/shard_map/ppermute | solution.py:33
  49.5 8.1 %collective-permute-done.1.theirs = f32[128,128]{1,0:T(8,128)S(1)} collective-permute-done((f32[128,128]{1,0:T(8,128)S(1)}, f32[128,128]{1,0:T(8,128)S(1)}, u32[]{:S(2)}, u32[]{:S(2)}) %collective-permute-start.1) | collective-permute-done | bytes 65568 | tf_op jit(solution)/shard_map/ppermute | solution.py:33
  57.9 11.4 %all_to_all.42 = f32[4,64,128]{2,1,0:T(8,128)S(1)} all-to-all(f32[4,64,128]{2,1,0:T(8,128)S(1)} %shard_map.65), channel_id=1, replica_groups=mesh['z4'=2,'z2'=2,'z1'=2,'core'=2,'zh'=2,'y'=4,'x'=4] {'z2','z1'}, dimensions={0} | all-to-all | bytes 262144 | tf_op jit(solution)/shard_map/all_to_all | solution.py:29
  69.3 2.0 %all-gather.1 = f32[8,64,128]{2,1,0:T(8,128)S(1)} all-gather(f32[4,64,128]{2,1,0:T(8,128)S(1)} %all_to_all.42), channel_id=3, replica_groups=mesh['z4'=2,'z2'=2,'z1'=2,'core'=2,'zh'=2,'y'=4,'x'=4] {'core'}, dimensions={0}, use_global_device_ids=true | all-gather | bytes 393216 | tf_op jit(solution)/shard_map/all_gather | solution.py:312
  71.7 11.2 %all_to_all.43.got = f32[16,4,768]{2,1,0:T(4,128)S(1)} all-to-all(f32[16,4,768]{2,1,0:T(4,128)S(1)} %shard_map.66), channel_id=1, replica_groups=mesh['z4'=2,'z2'=2,'z1'=2,'core'=2,'zh'=2,'y'=4,'x'=4] {'y','x'}, dimensions={0} | all-to-all | bytes 393216 | tf_op jit(solution)/shard_map/all_to_all | solution.py:29
  83.3 8.2 %collective-permute-start.2 = (f32[5,4,256]{2,1,0:T(4,128)S(1)}, f32[5,4,256]{2,1,0:T(4,128)S(1)}, u32[]{:S(2)}, u32[]{:S(2)}) collective-permute-start(f32[5,4,256]{2,1,0:T(4,128)S(1)} %get-tuple-element.25.mine), channel_id=1, source_target_pairs={{0,16},{16,0},{1,17},{17,1},{2,18},{18,2},{3,19},{19,3},{4,20},{20... | collective-permute-start | bytes 61448 | tf_op jit(solution)/shard_map/ppermute | solution.py:33
  91.6 6.1 %collective-permute-done.2.theirs = f32[5,4,256]{2,1,0:T(4,128)S(1)} collective-permute-done((f32[5,4,256]{2,1,0:T(4,128)S(1)}, f32[5,4,256]{2,1,0:T(4,128)S(1)}, u32[]{:S(2)}, u32[]{:S(2)}) %collective-permute-start.2) | collective-permute-done | bytes 20512 | tf_op jit(solution)/shard_map/ppermute | solution.py:33
  98.0 11.7 %all_to_all.44.w0.w_got = f32[16,4,1024]{2,1,0:T(4,128)S(1)} all-to-all(f32[16,4,1024]{2,1,0:T(4,128)S(1)} %get-tuple-element.27), channel_id=1, replica_groups=mesh['z4'=2,'z2'=2,'z1'=2,'core'=2,'zh'=2,'y'=4,'x'=4] {'y','x'}, dimensions={0} | all-to-all | bytes 524288 | tf_op jit(solution)/shard_map/all_to_all | solution.py:29
  110.0 9.9 %all_to_all.45.got = f32[8,8,640]{2,1,0:T(8,128)S(1)} all-to-all(f32[8,8,640]{2,1,0:T(8,128)S(1)} %shard_map.70), channel_id=1, replica_groups=mesh['z4'=2,'z2'=2,'z1'=2,'core'=2,'zh'=2,'y'=4,'x'=4] {'z2','z1','core'}, dimensions={0} | all-to-all | bytes 327680 | tf_op jit(solution)/shard_map/all_to_all | solution.py:29
  120.1 1.9 %collective-permute-start.3 = (f32[5,8,256]{2,1,0:T(8,128)S(1)}, f32[5,8,256]{2,1,0:T(8,128)S(1)}, u32[]{:S(2)}, u32[]{:S(2)}) collective-permute-start(f32[5,8,256]{2,1,0:T(8,128)S(1)} %shard_map.71.mine), channel_id=1, source_target_pairs={{0,256},{256,0},{1,257},{257,1},{2,258},{258,2},{3,259},{259,3},{4... | collective-permute-start | bytes 122888 | tf_op jit(solution)/shard_map/ppermute | solution.py:33
  122.0 7.9 %collective-permute-done.3.theirs = f32[5,8,256]{2,1,0:T(8,128)S(1)} collective-permute-done((f32[5,8,256]{2,1,0:T(8,128)S(1)}, f32[5,8,256]{2,1,0:T(8,128)S(1)}, u32[]{:S(2)}, u32[]{:S(2)}) %collective-permute-start.3) | collective-permute-done | bytes 40992 | tf_op jit(solution)/shard_map/ppermute | solution.py:33
  130.2 11.2 %all_to_all.46.h_got = f32[8,16,256]{2,1,0:T(8,128)S(1)} all-to-all(f32[8,16,256]{2,1,0:T(8,128)S(1)} %get-tuple-element.30), channel_id=1, replica_groups=mesh['z4'=2,'z2'=2,'z1'=2,'core'=2,'zh'=2,'y'=4,'x'=4] {'z2','z1','core'}, dimensions={0} | all-to-all | bytes 262144 | tf_op jit(solution)/shard_map/all_to_all | solution.py:29
  141.7 11.1 %all_to_all.47.got = f32[16,4,640]{2,1,0:T(4,128)S(1)} all-to-all(f32[16,4,640]{2,1,0:T(4,128)S(1)} %shard_map.73), channel_id=1, replica_groups=mesh['z4'=2,'z2'=2,'z1'=2,'core'=2,'zh'=2,'y'=4,'x'=4] {'y','x'}, dimensions={0} | all-to-all | bytes 327680 | tf_op jit(solution)/shard_map/all_to_all | solution.py:29
  153.2 8.6 %collective-permute-start.4 = (f32[5,2,256]{2,1,0:T(2,128)S(1)}, f32[5,2,256]{2,1,0:T(2,128)S(1)}, u32[]{:S(2)}, u32[]{:S(2)}) collective-permute-start(f32[5,2,256]{2,1,0:T(2,128)S(1)} %get-tuple-element.32), channel_id=1, source_target_pairs={{0,16},{16,0},{1,17},{17,1},{2,18},{18,2},{3,19},{19,3},{4,20},{20... | collective-permute-start | bytes 30728 | tf_op jit(solution)/shard_map/ppermute | solution.py:33
  162.4 5.0 %collective-permute-done.4.theirs = f32[5,2,256]{2,1,0:T(2,128)S(1)} collective-permute-done((f32[5,2,256]{2,1,0:T(2,128)S(1)}, f32[5,2,256]{2,1,0:T(2,128)S(1)}, u32[]{:S(2)}, u32[]{:S(2)}) %collective-permute-start.4) | collective-permute-done | bytes 10272 | tf_op jit(solution)/shard_map/ppermute | solution.py:33
  167.5 0.8 shard_map.75
  (20 shorter events, 4.1 us)
Async XLA Ops:
  0.6 14.5 %collective-permute-start = (f32[2,1024]{1,0:T(2,128)}, f32[2,1024]{1,0:T(2,128)S(1)}, u32[]{:S(2)}, u32[]{:S(2)}) collective-permute-start(f32[2,1024]{1,0:T(2,128)} %w.1), channel_id=1, source_target_pairs={{0,16},{16,0},{1,17},{17,1},{2,18},{18,2},{3,19},{19,3},{4,20},{20... | collective-permute-start | bytes 24584 | tf_op jit(solution)/shard_map/ppermute | solution.py:33
  11.6 1.0 copy-start
  12.6 0.7 copy-start.2
  15.1 15.5 %copy-start.1 = (f32[4,1024]{1,0:T(4,128)S(1)}, f32[4,1024]{1,0:T(4,128)}, u32[]{:S(2)}) copy-start(f32[4,1024]{1,0:T(4,128)} %h.1) | copy-start | bytes 49156
  47.6 10.1 %collective-permute-start.1 = (f32[128,128]{1,0:T(8,128)S(1)}, f32[128,128]{1,0:T(8,128)S(1)}, u32[]{:S(2)}, u32[]{:S(2)}) collective-permute-start(f32[128,128]{1,0:T(8,128)S(1)} %get-tuple-element.23.mine), channel_id=1, source_target_pairs={{0,256},{256,0},{1,257},{257,1},{2,258},{258,2},{3,259},{259,3},{4... | collective-permute-start | bytes 196616 | tf_op jit(solution)/shard_map/ppermute | solution.py:33
  83.3 14.4 %collective-permute-start.2 = (f32[5,4,256]{2,1,0:T(4,128)S(1)}, f32[5,4,256]{2,1,0:T(4,128)S(1)}, u32[]{:S(2)}, u32[]{:S(2)}) collective-permute-start(f32[5,4,256]{2,1,0:T(4,128)S(1)} %get-tuple-element.25.mine), channel_id=1, source_target_pairs={{0,16},{16,0},{1,17},{17,1},{2,18},{18,2},{3,19},{19,3},{4,20},{20... | collective-permute-start | bytes 61448 | tf_op jit(solution)/shard_map/ppermute | solution.py:33
  120.1 9.8 %collective-permute-start.3 = (f32[5,8,256]{2,1,0:T(8,128)S(1)}, f32[5,8,256]{2,1,0:T(8,128)S(1)}, u32[]{:S(2)}, u32[]{:S(2)}) collective-permute-start(f32[5,8,256]{2,1,0:T(8,128)S(1)} %shard_map.71.mine), channel_id=1, source_target_pairs={{0,256},{256,0},{1,257},{257,1},{2,258},{258,2},{3,259},{259,3},{4... | collective-permute-start | bytes 122888 | tf_op jit(solution)/shard_map/ppermute | solution.py:33
  153.2 14.3 %collective-permute-start.4 = (f32[5,2,256]{2,1,0:T(2,128)S(1)}, f32[5,2,256]{2,1,0:T(2,128)S(1)}, u32[]{:S(2)}, u32[]{:S(2)}) collective-permute-start(f32[5,2,256]{2,1,0:T(2,128)S(1)} %get-tuple-element.32), channel_id=1, source_target_pairs={{0,16},{16,0},{1,17},{17,1},{2,18},{18,2},{3,19},{19,3},{4,20},{20... | collective-permute-start | bytes 30728 | tf_op jit(solution)/shard_map/ppermute | solution.py:33

commit v12 on v11

--- a/solution.py
+++ b/solution.py
@@ -50,6 +50,19 @@
     return product(left, values), product(left, whole, NT)
 
 
+def packed(gram):
+    parts = gram[:32, :32], gram[:32, 32:], gram[32:, 32:]
+    rest = jnp.concatenate([p[24:] for p in parts], axis=0)
+    return jnp.concatenate([p[:24] for p in parts] + [rest], axis=1)
+
+
+def unpacked(rows):
+    a, b, c = (
+        jnp.concatenate([rows[:, 32 * i : 32 * i + 32], rows[8 * i : 8 * i + 8, 96:]], axis=0) for i in range(3)
+    )
+    return jnp.concatenate([jnp.concatenate([a, b], axis=1), jnp.concatenate([b.T, c], axis=1)], axis=0)
+
+
 def prepare_kernel(blk, values, w, parts, turned, w_mine, listed):
     for d in range(2):
         for j in range(CAP):
@@ -100,12 +113,12 @@
         for side in range(2):
             at = 128 * j + RANK * side
             out[at : at + RANK, :] = upper[:, COLS * side : COLS * (side + 1)]
-        out[256 + 32 * j : 288 + 32 * j, :] = jnp.concatenate([gram[:32], gram[32:]], axis=1)
+        out[256 + 24 * j : 280 + 24 * j, :] = packed(gram)
     for q in range(NH):
-        at = 320 + 16 * (q % 2) + 4 * (q // 2)
+        at = 304 + 16 * (q % 2) + 4 * (q // 2)
         out[at : at + 4, :] = h[:, COLS * q : COLS * (q + 1)]
     lane = lax.broadcasted_iota(jnp.int32, (8, COLS), 1)
-    out[352:360, :] = jnp.where(lane == 0, blk[CAP], blk[CAP + 1]).astype(jnp.float32)
+    out[336:344, :] = jnp.where(lane == 0, blk[CAP], blk[CAP + 1]).astype(jnp.float32)
     plane = lax.axis_index(PLANE)
     for b in range(NB):
         w_own[b] = w0[plane, :, b * BS : (b + 1) * BS]
@@ -113,37 +126,37 @@
 
 def h1_build_kernel(pair, out, lists):
     core = lax.axis_index("core")
-    out[:, :96, :] = jnp.zeros((NQ, 96, COLS), jnp.float32)
+    out[:, :88, :] = jnp.zeros((NQ, 88, COLS), jnp.float32)
     for i in range(2):
-        read_list(lists, i, pair[i, 352:353, :])
+        read_list(lists, i, pair[i, 336:337, :])
         for j in range(CAP):
             q = lists[CAP * i + j]
             at = pl.multiple_of(128 * j + RANK * core, 8)
             out[q, :64, :] = out[q, :64, :] + pair[i, pl.ds(at, RANK), :]
-            out[q, 64:96, :] = out[q, 64:96, :] + pair[i, 256 + 32 * j : 288 + 32 * j, :]
-        side = pair[i, pl.ds(pl.multiple_of(320 + 16 * core, 8), 16), :]
+            out[q, 64:88, :] = out[q, 64:88, :] + pair[i, 256 + 24 * j : 280 + 24 * j, :]
+        side = pair[i, pl.ds(pl.multiple_of(304 + 16 * core, 8), 16), :]
         for q in range(NQ):
-            out[q, 96 + 4 * i : 100 + 4 * i, :] = side[4 * q : 4 * q + 4]
-            out[q, 104 + 4 * i : 108 + 4 * i, :] = pair[i, 352:356, :]
+            out[q, 88 + 4 * i : 92 + 4 * i, :] = side[4 * q : 4 * q + 4]
+            out[q, 96 + 4 * i : 100 + 4 * i, :] = pair[i, 336:340, :]
 
 
 def h1_collect_kernel(got, out, cols):
-    total = got[0, :96, :]
+    total = got[0, :88, :]
     for q in range(1, NQ):
-        total = total + got[q, :96, :]
-    out[:96, :] = total
+        total = total + got[q, :88, :]
+    out[:88, :] = total
     for q in range(NQ):
-        out[96 + 8 * q : 104 + 8 * q, :] = got[q, 96:104, :]
+        out[88 + 8 * q : 96 + 8 * q, :] = got[q, 88:96, :]
         for i in range(2):
-            read_list(cols, 2 * q + i, got[q, 104 + 4 * i : 105 + 4 * i, :])
+            read_list(cols, 2 * q + i, got[q, 96 + 4 * i : 97 + 4 * i, :])
 
 
 def h1_update_kernel(mine, theirs, out):
-    total = mine[:96, :] + theirs[:96, :]
-    gram = jnp.concatenate([total[64:, :64], total[64:, 64:]], axis=0)
+    total = mine[:88, :] + theirs[:88, :]
+    gram = unpacked(total[64:])
     first = lax.axis_index("z4") == 0
-    low = jnp.where(first, mine[96:, :], theirs[96:, :])
-    high = jnp.where(first, theirs[96:, :], mine[96:, :])
+    low = jnp.where(first, mine[88:, :], theirs[88:, :])
+    high = jnp.where(first, theirs[88:, :], mine[88:, :])
     pairs = []
     for k in range(16):
         pairs += [low[2 * k : 2 * k + 2], high[2 * k : 2 * k + 2]]
@@ -300,12 +313,12 @@
     w_got = exchange(w_pair, PLANE)
 
     w_own, sent = call(
-        h1_terms_kernel, (blk,), (w_got, h_factor, values), [(NB, 4, BS), (360, COLS)], scratch=[(CAP, RANK, BS)]
+        h1_terms_kernel, (blk,), (w_got, h_factor, values), [(NB, 4, BS), (344, COLS)], scratch=[(CAP, RANK, BS)]
     )
     pair = lax.all_gather(sent, "core", axis=0)
-    (sent,) = call(h1_build_kernel, (), (pair,), [(NQ, 112, COLS)], counts=(2 * CAP,))
+    (sent,) = call(h1_build_kernel, (), (pair,), [(NQ, 104, COLS)], counts=(2 * CAP,))
     got = exchange(sent, QUAD)
-    mine, cols = call(h1_collect_kernel, (), (got,), [(128, COLS)], tables=[(NH * CAP,)])
+    mine, cols = call(h1_collect_kernel, (), (got,), [(120, COLS)], tables=[(NH * CAP,)])
     theirs = swap(mine, "z4")
     (w_all,) = call(w_arrange_kernel, (), (w_got,), [(NB, RANK, BS)])
     (out,) = call(h1_update_kernel, (), (mine, theirs), [(NQ, RANK, COLS)])

time: 169 us -> 169 us (level)
  no operation moved by 1% of the time
where the time goes in v12:
time: 169 us; the launch traced here: 168 us
  blocking collectives  99.7 us (59%)
  starting transfers between devices  31.2 us (18%)
  waiting for transfers between devices  28.4 us (17%)
  Pallas kernels  5.44 us (3%)
  local copies, waits for them, and re-layouts  2.35 us (1%)
    all_to_all x8, blocking collectives, exchange(): return lax.all_to_all(x, axes, split_axis=0, concat_axis=0, tiled=True)  95.6 us
    ppermute x5, starting transfers between devices, swap(): return lax.ppermute(x, axis, [(0, 1), (1, 0)])  31.2 us
    ppermute x5, waiting for transfers between devices, swap(): return lax.ppermute(x, axis, [(0, 1), (1, 0)])  28.4 us
    pallas_call x17, Pallas kernels, call(): pl.pallas_call(body, in_specs=[smem] * len(scalars) + [vmem] * len(arrays...  5.44 us
  transfers between devices with their start and end apart: 5, of which 5 were waited for; matrix products, arithmetic and copies ran while one was open for 0% of the time, Pallas kernels for 1%

profile of v12, /device:TPU:128, one launch (start us, length us, event | category | flops | bytes accessed | tf_op | source)
XLA Modules:
  0.0 167.9 jit_solution(15663464303151291381)
XLA Ops:
  0.6 10.9 %collective-permute-start = (f32[2,1024]{1,0:T(2,128)}, f32[2,1024]{1,0:T(2,128)S(1)}, u32[]{:S(2)}, u32[]{:S(2)}) collective-permute-start(f32[2,1024]{1,0:T(2,128)} %w.1), channel_id=1, source_target_pairs={{0,16},{16,0},{1,17},{17,1},{2,18},{18,2},{3,19},{19,3},{4,20},{20... | collective-permute-start | bytes 24584 | tf_op jit(solution)/shard_map/ppermute | solution.py:33
  11.6 1.0 copy-done
  12.6 0.7 copy-done.2
  13.3 0.9 shard_map.59
  14.2 0.9 collective-permute-done.theirs
  15.1 15.5 %all_to_all.40.w0 = f32[16,4,1024]{2,1,0:T(4,128)S(1)} all-to-all(f32[16,4,1024]{2,1,0:T(4,128)S(1)} %shard_map.60), channel_id=1, replica_groups=mesh['z4'=2,'z2'=2,'z1'=2,'core'=2,'zh'=2,'y'=4,'x'=4] {'y','x'}, dimensions={0} | all-to-all | bytes 524288 | tf_op jit(solution)/shard_map/all_to_all | solution.py:29
  31.1 2.1 %all-gather = f32[688,128]{1,0:T(8,128)S(1)} all-gather(f32[344,128]{1,0:T(8,128)S(1)} %get-tuple-element.22), channel_id=2, replica_groups=mesh['z4'=2,'z2'=2,'z1'=2,'core'=2,'zh'=2,'y'=4,'x'=4] {'core'}, dimensions={0}, use_global_device_ids=true | all-gather | bytes 528384 | tf_op jit(solution)/shard_map/all_gather | solution.py:318
  33.3 13.8 %all_to_all.41.got = f32[4,104,128]{2,1,0:T(8,128)S(1)} all-to-all(f32[4,104,128]{2,1,0:T(8,128)S(1)} %shard_map.63), channel_id=1, replica_groups=mesh['z4'=2,'z2'=2,'z1'=2,'core'=2,'zh'=2,'y'=4,'x'=4] {'z2','z1'}, dimensions={0} | all-to-all | bytes 425984 | tf_op jit(solution)/shard_map/all_to_all | solution.py:29
  47.3 1.9 %collective-permute-start.1 = (f32[120,128]{1,0:T(8,128)S(1)}, f32[120,128]{1,0:T(8,128)S(1)}, u32[]{:S(2)}, u32[]{:S(2)}) collective-permute-start(f32[120,128]{1,0:T(8,128)S(1)} %get-tuple-element.23.mine), channel_id=1, source_target_pairs={{0,256},{256,0},{1,257},{257,1},{2,258},{258,2},{3,259},{259,3},{4... | collective-permute-start | bytes 184328 | tf_op jit(solution)/shard_map/ppermute | solution.py:33
  49.2 8.1 %collective-permute-done.1.theirs = f32[120,128]{1,0:T(8,128)S(1)} collective-permute-done((f32[120,128]{1,0:T(8,128)S(1)}, f32[120,128]{1,0:T(8,128)S(1)}, u32[]{:S(2)}, u32[]{:S(2)}) %collective-permute-start.1) | collective-permute-done | bytes 61472 | tf_op jit(solution)/shard_map/ppermute | solution.py:33
  57.6 11.2 %all_to_all.42 = f32[4,64,128]{2,1,0:T(8,128)S(1)} all-to-all(f32[4,64,128]{2,1,0:T(8,128)S(1)} %shard_map.65), channel_id=1, replica_groups=mesh['z4'=2,'z2'=2,'z1'=2,'core'=2,'zh'=2,'y'=4,'x'=4] {'z2','z1'}, dimensions={0} | all-to-all | bytes 262144 | tf_op jit(solution)/shard_map/all_to_all | solution.py:29
  68.9 2.0 %all-gather.1 = f32[8,64,128]{2,1,0:T(8,128)S(1)} all-gather(f32[4,64,128]{2,1,0:T(8,128)S(1)} %all_to_all.42), channel_id=3, replica_groups=mesh['z4'=2,'z2'=2,'z1'=2,'core'=2,'zh'=2,'y'=4,'x'=4] {'core'}, dimensions={0}, use_global_device_ids=true | all-gather | bytes 393216 | tf_op jit(solution)/shard_map/all_gather | solution.py:325
  71.2 11.2 %all_to_all.43.got = f32[16,4,768]{2,1,0:T(4,128)S(1)} all-to-all(f32[16,4,768]{2,1,0:T(4,128)S(1)} %shard_map.66), channel_id=1, replica_groups=mesh['z4'=2,'z2'=2,'z1'=2,'core'=2,'zh'=2,'y'=4,'x'=4] {'y','x'}, dimensions={0} | all-to-all | bytes 393216 | tf_op jit(solution)/shard_map/all_to_all | solution.py:29
  82.9 8.2 %collective-permute-start.2 = (f32[5,4,256]{2,1,0:T(4,128)S(1)}, f32[5,4,256]{2,1,0:T(4,128)S(1)}, u32[]{:S(2)}, u32[]{:S(2)}) collective-permute-start(f32[5,4,256]{2,1,0:T(4,128)S(1)} %get-tuple-element.25.mine), channel_id=1, source_target_pairs={{0,16},{16,0},{1,17},{17,1},{2,18},{18,2},{3,19},{19,3},{4,20},{20... | collective-permute-start | bytes 61448 | tf_op jit(solution)/shard_map/ppermute | solution.py:33
  91.2 6.1 %collective-permute-done.2.theirs = f32[5,4,256]{2,1,0:T(4,128)S(1)} collective-permute-done((f32[5,4,256]{2,1,0:T(4,128)S(1)}, f32[5,4,256]{2,1,0:T(4,128)S(1)}, u32[]{:S(2)}, u32[]{:S(2)}) %collective-permute-start.2) | collective-permute-done | bytes 20512 | tf_op jit(solution)/shard_map/ppermute | solution.py:33
  97.5 11.7 %all_to_all.44.w0.w_got = f32[16,4,1024]{2,1,0:T(4,128)S(1)} all-to-all(f32[16,4,1024]{2,1,0:T(4,128)S(1)} %get-tuple-element.27), channel_id=1, replica_groups=mesh['z4'=2,'z2'=2,'z1'=2,'core'=2,'zh'=2,'y'=4,'x'=4] {'y','x'}, dimensions={0} | all-to-all | bytes 524288 | tf_op jit(solution)/shard_map/all_to_all | solution.py:29
  109.6 9.9 %all_to_all.45.got = f32[8,8,640]{2,1,0:T(8,128)S(1)} all-to-all(f32[8,8,640]{2,1,0:T(8,128)S(1)} %shard_map.70), channel_id=1, replica_groups=mesh['z4'=2,'z2'=2,'z1'=2,'core'=2,'zh'=2,'y'=4,'x'=4] {'z2','z1','core'}, dimensions={0} | all-to-all | bytes 327680 | tf_op jit(solution)/shard_map/all_to_all | solution.py:29
  119.7 1.9 %collective-permute-start.3 = (f32[5,8,256]{2,1,0:T(8,128)S(1)}, f32[5,8,256]{2,1,0:T(8,128)S(1)}, u32[]{:S(2)}, u32[]{:S(2)}) collective-permute-start(f32[5,8,256]{2,1,0:T(8,128)S(1)} %shard_map.71.mine), channel_id=1, source_target_pairs={{0,256},{256,0},{1,257},{257,1},{2,258},{258,2},{3,259},{259,3},{4... | collective-permute-start | bytes 122888 | tf_op jit(solution)/shard_map/ppermute | solution.py:33
  121.6 7.9 %collective-permute-done.3.theirs = f32[5,8,256]{2,1,0:T(8,128)S(1)} collective-permute-done((f32[5,8,256]{2,1,0:T(8,128)S(1)}, f32[5,8,256]{2,1,0:T(8,128)S(1)}, u32[]{:S(2)}, u32[]{:S(2)}) %collective-permute-start.3) | collective-permute-done | bytes 40992 | tf_op jit(solution)/shard_map/ppermute | solution.py:33
  129.7 11.2 %all_to_all.46.h_got = f32[8,16,256]{2,1,0:T(8,128)S(1)} all-to-all(f32[8,16,256]{2,1,0:T(8,128)S(1)} %get-tuple-element.30), channel_id=1, replica_groups=mesh['z4'=2,'z2'=2,'z1'=2,'core'=2,'zh'=2,'y'=4,'x'=4] {'z2','z1','core'}, dimensions={0} | all-to-all | bytes 262144 | tf_op jit(solution)/shard_map/all_to_all | solution.py:29
  141.3 11.1 %all_to_all.47.got = f32[16,4,640]{2,1,0:T(4,128)S(1)} all-to-all(f32[16,4,640]{2,1,0:T(4,128)S(1)} %shard_map.73), channel_id=1, replica_groups=mesh['z4'=2,'z2'=2,'z1'=2,'core'=2,'zh'=2,'y'=4,'x'=4] {'y','x'}, dimensions={0} | all-to-all | bytes 327680 | tf_op jit(solution)/shard_map/all_to_all | solution.py:29
  152.7 8.2 %collective-permute-start.4 = (f32[5,2,256]{2,1,0:T(2,128)S(1)}, f32[5,2,256]{2,1,0:T(2,128)S(1)}, u32[]{:S(2)}, u32[]{:S(2)}) collective-permute-start(f32[5,2,256]{2,1,0:T(2,128)S(1)} %get-tuple-element.32), channel_id=1, source_target_pairs={{0,16},{16,0},{1,17},{17,1},{2,18},{18,2},{3,19},{19,3},{4,20},{20... | collective-permute-start | bytes 30728 | tf_op jit(solution)/shard_map/ppermute | solution.py:33
  161.6 5.4 %collective-permute-done.4.theirs = f32[5,2,256]{2,1,0:T(2,128)S(1)} collective-permute-done((f32[5,2,256]{2,1,0:T(2,128)S(1)}, f32[5,2,256]{2,1,0:T(2,128)S(1)}, u32[]{:S(2)}, u32[]{:S(2)}) %collective-permute-start.4) | collective-permute-done | bytes 10272 | tf_op jit(solution)/shard_map/ppermute | solution.py:33
  167.0 0.8 shard_map.75
  (20 shorter events, 4.3 us)
Async XLA Ops:
  0.6 14.5 %collective-permute-start = (f32[2,1024]{1,0:T(2,128)}, f32[2,1024]{1,0:T(2,128)S(1)}, u32[]{:S(2)}, u32[]{:S(2)}) collective-permute-start(f32[2,1024]{1,0:T(2,128)} %w.1), channel_id=1, source_target_pairs={{0,16},{16,0},{1,17},{17,1},{2,18},{18,2},{3,19},{19,3},{4,20},{20... | collective-permute-start | bytes 24584 | tf_op jit(solution)/shard_map/ppermute | solution.py:33
  11.6 1.0 copy-start
  12.6 0.7 copy-start.2
  15.1 15.5 %copy-start.1 = (f32[4,1024]{1,0:T(4,128)S(1)}, f32[4,1024]{1,0:T(4,128)}, u32[]{:S(2)}) copy-start(f32[4,1024]{1,0:T(4,128)} %h.1) | copy-start | bytes 49156
  47.3 10.0 %collective-permute-start.1 = (f32[120,128]{1,0:T(8,128)S(1)}, f32[120,128]{1,0:T(8,128)S(1)}, u32[]{:S(2)}, u32[]{:S(2)}) collective-permute-start(f32[120,128]{1,0:T(8,128)S(1)} %get-tuple-element.23.mine), channel_id=1, source_target_pairs={{0,256},{256,0},{1,257},{257,1},{2,258},{258,2},{3,259},{259,3},{4... | collective-permute-start | bytes 184328 | tf_op jit(solution)/shard_map/ppermute | solution.py:33
  82.9 14.4 %collective-permute-start.2 = (f32[5,4,256]{2,1,0:T(4,128)S(1)}, f32[5,4,256]{2,1,0:T(4,128)S(1)}, u32[]{:S(2)}, u32[]{:S(2)}) collective-permute-start(f32[5,4,256]{2,1,0:T(4,128)S(1)} %get-tuple-element.25.mine), channel_id=1, source_target_pairs={{0,16},{16,0},{1,17},{17,1},{2,18},{18,2},{3,19},{19,3},{4,20},{20... | collective-permute-start | bytes 61448 | tf_op jit(solution)/shard_map/ppermute | solution.py:33
  119.7 9.8 %collective-permute-start.3 = (f32[5,8,256]{2,1,0:T(8,128)S(1)}, f32[5,8,256]{2,1,0:T(8,128)S(1)}, u32[]{:S(2)}, u32[]{:S(2)}) collective-permute-start(f32[5,8,256]{2,1,0:T(8,128)S(1)} %shard_map.71.mine), channel_id=1, source_target_pairs={{0,256},{256,0},{1,257},{257,1},{2,258},{258,2},{3,259},{259,3},{4... | collective-permute-start | bytes 122888 | tf_op jit(solution)/shard_map/ppermute | solution.py:33
  152.7 14.3 %collective-permute-start.4 = (f32[5,2,256]{2,1,0:T(2,128)S(1)}, f32[5,2,256]{2,1,0:T(2,128)S(1)}, u32[]{:S(2)}, u32[]{:S(2)}) collective-permute-start(f32[5,2,256]{2,1,0:T(2,128)S(1)} %get-tuple-element.32), channel_id=1, source_target_pairs={{0,16},{16,0},{1,17},{17,1},{2,18},{18,2},{3,19},{19,3},{4,20},{20... | collective-permute-start | bytes 30728 | tf_op jit(solution)/shard_map/ppermute | solution.py:33

commit v13 on v12

--- a/solution.py
+++ b/solution.py
@@ -233,32 +233,37 @@
     gram = mine[NB, :, RANK * b : RANK * (b + 1)] + theirs[NB, :, RANK * b : RANK * (b + 1)]
     high = gram.astype(jnp.bfloat16).astype(jnp.float32)
     gram = jnp.concatenate([high, gram - high], axis=0).astype(jnp.bfloat16)
-    whole = halves(whole)
     most = lax.dot_general(gram, whole[0], NN, preferred_element_type=jnp.float32)
     rest = lax.dot_general(gram, whole[1], NN, preferred_element_type=jnp.float32)
     return own * (mine[b] + theirs[b]) / (most[:rows] + (most[rows:] + rest[:rows]))
 
 
-def w_arrange_kernel(w0, w_all):
+def w_arrange_kernel(w0, w_all, block):
     for b in range(NB):
         for q in range(NP):
-            w_all[b, 4 * q : 4 * q + 4, :] = w0[q, :, b * BS : (b + 1) * BS]
+            block[4 * q : 4 * q + 4, :] = w0[q, :, b * BS : (b + 1) * BS]
+        w_all[b, 0], w_all[b, 1] = halves(block[...])
+
+
+def h_arrange_kernel(h_all, h_parts):
+    for b in range(NB):
+        h_parts[b, 0], h_parts[b, 1] = halves(whole_block(h_all, b))
 
 
 def w1_update_kernel(own, w_all, mine, theirs, new, out):
     for b in range(NB):
-        rows = owned(own[b], w_all[b], mine, theirs, b)
+        rows = owned(own[b], both_of(w_all, b), mine, theirs, b)
         new[b] = rows
         for q in range(NP):
             out[q, :, b * BS : (b + 1) * BS] = rows
 
 
-def h2_update_kernel(table, h_all, mine, theirs, final, out, new):
+def h2_update_kernel(table, h_all, h_parts, mine, theirs, final, out, new):
     first = lax.axis_index("z4") == 0
     at = pl.ds(pl.multiple_of(8 * lax.axis_index(HALF), 8), 8)
     for b in range(NB):
         own = jnp.concatenate([h_all[0, b, at, :], h_all[1, b, at, :]], axis=1)
-        rows = owned(own, whole_block(h_all, b), mine, theirs, b)
+        rows = owned(own, both_of(h_parts, b), mine, theirs, b)
         new[b] = rows
         for high in range(2):
             pair = rows[4 * high : 4 * high + 4]
@@ -280,7 +285,7 @@
     first = lax.axis_index("zh") == 0
     for b in range(NB):
         rows = jnp.where(first, own[b, 0:2, :], own[b, 2:4, :])
-        final[:, b * BS : (b + 1) * BS] = owned(rows, w_all[b], mine, theirs, b)
+        final[:, b * BS : (b + 1) * BS] = owned(rows, both_of(w_all, b), mine, theirs, b)
 
 
 def call(body, scalars, arrays, outs, tables=(), scratch=(), counts=(), last=False, dtypes=None):
@@ -299,6 +304,10 @@
     )
 
 
+def arranged(body, factor, scratch=()):
+    return call(body, (), (factor,), [(NB, 2, RANK, BS)], scratch=scratch, dtypes=[jnp.bfloat16])
+
+
 def per_device(blocks, observed, w_factor, h_factor):
     w_other = swap(w_factor, "zh")
     values, turned, w_mine, blk = call(
@@ -320,7 +329,7 @@
     got = exchange(sent, QUAD)
     mine, cols = call(h1_collect_kernel, (), (got,), [(120, COLS)], tables=[(NH * CAP,)])
     theirs = swap(mine, "z4")
-    (w_all,) = call(w_arrange_kernel, (), (w_got,), [(NB, RANK, BS)])
+    (w_all,) = arranged(w_arrange_kernel, w_got, scratch=[(RANK, BS)])
     (out,) = call(h1_update_kernel, (), (mine, theirs), [(NQ, RANK, COLS)])
     h_all = lax.all_gather(exchange(out, QUAD), "core", axis=0)
 
@@ -329,6 +338,7 @@
     got = exchange(sent, PLANE)
     mine, rows = call(w1_collect_kernel, (), (got,), [(NB + 1, 4, BS)], tables=[(NP * CAP,)])
     theirs = swap(mine, "zh")
+    (h_parts,) = arranged(h_arrange_kernel, h_all)
     w_own, out = call(w1_update_kernel, (), (w_own, w_all, mine, theirs), [(NB, 4, BS), (NP, 4, NB * BS)])
     w_got = exchange(out, PLANE)
 
@@ -336,9 +346,9 @@
     got = exchange(sent, HALF)
     (mine,) = call(gram_collect_kernel, (cols,), (got,), [(NB + 1, 8, BS)])
     theirs = swap(mine, "z4")
-    (w_all,) = call(w_arrange_kernel, (), (w_got,), [(NB, RANK, BS)])
+    (w_all,) = arranged(w_arrange_kernel, w_got, scratch=[(RANK, BS)])
     h_final, out = call(
-        h2_update_kernel, (cols,), (h_all, mine, theirs), [(4, NB * BS), (NH, 16, BS)], scratch=[(NB, 8, BS)]
+        h2_update_kernel, (cols,), (h_all, h_parts, mine, theirs), [(4, NB * BS), (NH, 16, BS)], scratch=[(NB, 8, BS)]
     )
     h_got = exchange(out, HALF)
 

time: 169 us -> 169 us (level)
    pallas_call x17 -> x18, Pallas kernels: 5.44 us -> 5.54 us  [call(): pl.pallas_call(body, in_specs=[smem] * len(scalars) + [vmem] * len(arrays...]
where the time goes in v13:
time: 169 us; the launch traced here: 168 us
  blocking collectives  99.7 us (59%)
  starting transfers between devices  31.2 us (18%)
  waiting for transfers between devices  28.3 us (17%)
  Pallas kernels  5.54 us (3%)
  local copies, waits for them, and re-layouts  2.35 us (1%)
    all_to_all x8, blocking collectives, exchange(): return lax.all_to_all(x, axes, split_axis=0, concat_axis=0, tiled=True)  95.6 us
    ppermute x5, starting transfers between devices, swap(): return lax.ppermute(x, axis, [(0, 1), (1, 0)])  31.2 us
    ppermute x5, waiting for transfers between devices, swap(): return lax.ppermute(x, axis, [(0, 1), (1, 0)])  28.3 us
    pallas_call x18, Pallas kernels, call(): pl.pallas_call(body, in_specs=[smem] * len(scalars) + [vmem] * len(arrays...  5.54 us
  transfers between devices with their start and end apart: 5, of which 5 were waited for; matrix products, arithmetic and copies ran while one was open for 0% of the time, Pallas kernels for 1%

profile of v13, /device:TPU:128, one launch (start us, length us, event | category | flops | bytes accessed | tf_op | source)
XLA Modules:
  0.0 167.9 jit_solution(8449102713467672102)
XLA Ops:
  0.6 10.9 %collective-permute-start = (f32[2,1024]{1,0:T(2,128)}, f32[2,1024]{1,0:T(2,128)S(1)}, u32[]{:S(2)}, u32[]{:S(2)}) collective-permute-start(f32[2,1024]{1,0:T(2,128)} %w.1), channel_id=1, source_target_pairs={{0,16},{16,0},{1,17},{17,1},{2,18},{18,2},{3,19},{19,3},{4,20},{20... | collective-permute-start | bytes 24584 | tf_op jit(solution)/shard_map/ppermute | solution.py:33
  11.6 1.0 copy-done
  12.6 0.7 copy-done.2
  13.3 0.9 shard_map.59
  14.2 0.9 collective-permute-done.theirs
  15.1 15.5 %all_to_all.40.w0 = f32[16,4,1024]{2,1,0:T(4,128)S(1)} all-to-all(f32[16,4,1024]{2,1,0:T(4,128)S(1)} %shard_map.60), channel_id=1, replica_groups=mesh['z4'=2,'z2'=2,'z1'=2,'core'=2,'zh'=2,'y'=4,'x'=4] {'y','x'}, dimensions={0} | all-to-all | bytes 524288 | tf_op jit(solution)/shard_map/all_to_all | solution.py:29
  31.1 2.1 %all-gather = f32[688,128]{1,0:T(8,128)S(1)} all-gather(f32[344,128]{1,0:T(8,128)S(1)} %get-tuple-element.22), channel_id=2, replica_groups=mesh['z4'=2,'z2'=2,'z1'=2,'core'=2,'zh'=2,'y'=4,'x'=4] {'core'}, dimensions={0}, use_global_device_ids=true | all-gather | bytes 528384 | tf_op jit(solution)/shard_map/all_gather | solution.py:327
  33.3 13.8 %all_to_all.41.got = f32[4,104,128]{2,1,0:T(8,128)S(1)} all-to-all(f32[4,104,128]{2,1,0:T(8,128)S(1)} %shard_map.63), channel_id=1, replica_groups=mesh['z4'=2,'z2'=2,'z1'=2,'core'=2,'zh'=2,'y'=4,'x'=4] {'z2','z1'}, dimensions={0} | all-to-all | bytes 425984 | tf_op jit(solution)/shard_map/all_to_all | solution.py:29
  47.3 1.9 %collective-permute-start.1 = (f32[120,128]{1,0:T(8,128)S(1)}, f32[120,128]{1,0:T(8,128)S(1)}, u32[]{:S(2)}, u32[]{:S(2)}) collective-permute-start(f32[120,128]{1,0:T(8,128)S(1)} %get-tuple-element.23.mine), channel_id=1, source_target_pairs={{0,256},{256,0},{1,257},{257,1},{2,258},{258,2},{3,259},{259,3},{4... | collective-permute-start | bytes 184328 | tf_op jit(solution)/shard_map/ppermute | solution.py:33
  49.2 8.1 %collective-permute-done.1.theirs = f32[120,128]{1,0:T(8,128)S(1)} collective-permute-done((f32[120,128]{1,0:T(8,128)S(1)}, f32[120,128]{1,0:T(8,128)S(1)}, u32[]{:S(2)}, u32[]{:S(2)}) %collective-permute-start.1) | collective-permute-done | bytes 61472 | tf_op jit(solution)/shard_map/ppermute | solution.py:33
  57.6 11.2 %all_to_all.42 = f32[4,64,128]{2,1,0:T(8,128)S(1)} all-to-all(f32[4,64,128]{2,1,0:T(8,128)S(1)} %shard_map.65), channel_id=1, replica_groups=mesh['z4'=2,'z2'=2,'z1'=2,'core'=2,'zh'=2,'y'=4,'x'=4] {'z2','z1'}, dimensions={0} | all-to-all | bytes 262144 | tf_op jit(solution)/shard_map/all_to_all | solution.py:29
  68.9 2.0 %all-gather.1 = f32[8,64,128]{2,1,0:T(8,128)S(1)} all-gather(f32[4,64,128]{2,1,0:T(8,128)S(1)} %all_to_all.42), channel_id=3, replica_groups=mesh['z4'=2,'z2'=2,'z1'=2,'core'=2,'zh'=2,'y'=4,'x'=4] {'core'}, dimensions={0}, use_global_device_ids=true | all-gather | bytes 393216 | tf_op jit(solution)/shard_map/all_gather | solution.py:334
  71.2 11.2 %all_to_all.43.got = f32[16,4,768]{2,1,0:T(4,128)S(1)} all-to-all(f32[16,4,768]{2,1,0:T(4,128)S(1)} %shard_map.66), channel_id=1, replica_groups=mesh['z4'=2,'z2'=2,'z1'=2,'core'=2,'zh'=2,'y'=4,'x'=4] {'y','x'}, dimensions={0} | all-to-all | bytes 393216 | tf_op jit(solution)/shard_map/all_to_all | solution.py:29
  82.9 8.2 %collective-permute-start.2 = (f32[5,4,256]{2,1,0:T(4,128)S(1)}, f32[5,4,256]{2,1,0:T(4,128)S(1)}, u32[]{:S(2)}, u32[]{:S(2)}) collective-permute-start(f32[5,4,256]{2,1,0:T(4,128)S(1)} %get-tuple-element.25.mine), channel_id=1, source_target_pairs={{0,16},{16,0},{1,17},{17,1},{2,18},{18,2},{3,19},{19,3},{4,20},{20... | collective-permute-start | bytes 61448 | tf_op jit(solution)/shard_map/ppermute | solution.py:33
  91.2 6.1 %collective-permute-done.2.theirs = f32[5,4,256]{2,1,0:T(4,128)S(1)} collective-permute-done((f32[5,4,256]{2,1,0:T(4,128)S(1)}, f32[5,4,256]{2,1,0:T(4,128)S(1)}, u32[]{:S(2)}, u32[]{:S(2)}) %collective-permute-start.2) | collective-permute-done | bytes 20512 | tf_op jit(solution)/shard_map/ppermute | solution.py:33
  97.5 11.7 %all_to_all.44.w0.w_got = f32[16,4,1024]{2,1,0:T(4,128)S(1)} all-to-all(f32[16,4,1024]{2,1,0:T(4,128)S(1)} %get-tuple-element.27), channel_id=1, replica_groups=mesh['z4'=2,'z2'=2,'z1'=2,'core'=2,'zh'=2,'y'=4,'x'=4] {'y','x'}, dimensions={0} | all-to-all | bytes 524288 | tf_op jit(solution)/shard_map/all_to_all | solution.py:29
  109.6 9.9 %all_to_all.45.got = f32[8,8,640]{2,1,0:T(8,128)S(1)} all-to-all(f32[8,8,640]{2,1,0:T(8,128)S(1)} %shard_map.71), channel_id=1, replica_groups=mesh['z4'=2,'z2'=2,'z1'=2,'core'=2,'zh'=2,'y'=4,'x'=4] {'z2','z1','core'}, dimensions={0} | all-to-all | bytes 327680 | tf_op jit(solution)/shard_map/all_to_all | solution.py:29
  119.7 1.9 %collective-permute-start.3 = (f32[5,8,256]{2,1,0:T(8,128)S(1)}, f32[5,8,256]{2,1,0:T(8,128)S(1)}, u32[]{:S(2)}, u32[]{:S(2)}) collective-permute-start(f32[5,8,256]{2,1,0:T(8,128)S(1)} %shard_map.72.mine), channel_id=1, source_target_pairs={{0,256},{256,0},{1,257},{257,1},{2,258},{258,2},{3,259},{259,3},{4... | collective-permute-start | bytes 122888 | tf_op jit(solution)/shard_map/ppermute | solution.py:33
  121.7 7.8 %collective-permute-done.3.theirs = f32[5,8,256]{2,1,0:T(8,128)S(1)} collective-permute-done((f32[5,8,256]{2,1,0:T(8,128)S(1)}, f32[5,8,256]{2,1,0:T(8,128)S(1)}, u32[]{:S(2)}, u32[]{:S(2)}) %collective-permute-start.3) | collective-permute-done | bytes 40992 | tf_op jit(solution)/shard_map/ppermute | solution.py:33
  129.7 11.2 %all_to_all.46.h_got = f32[8,16,256]{2,1,0:T(8,128)S(1)} all-to-all(f32[8,16,256]{2,1,0:T(8,128)S(1)} %get-tuple-element.30), channel_id=1, replica_groups=mesh['z4'=2,'z2'=2,'z1'=2,'core'=2,'zh'=2,'y'=4,'x'=4] {'z2','z1','core'}, dimensions={0} | all-to-all | bytes 262144 | tf_op jit(solution)/shard_map/all_to_all | solution.py:29
  141.3 11.1 %all_to_all.47.got = f32[16,4,640]{2,1,0:T(4,128)S(1)} all-to-all(f32[16,4,640]{2,1,0:T(4,128)S(1)} %shard_map.74), channel_id=1, replica_groups=mesh['z4'=2,'z2'=2,'z1'=2,'core'=2,'zh'=2,'y'=4,'x'=4] {'y','x'}, dimensions={0} | all-to-all | bytes 327680 | tf_op jit(solution)/shard_map/all_to_all | solution.py:29
  152.7 8.2 %collective-permute-start.4 = (f32[5,2,256]{2,1,0:T(2,128)S(1)}, f32[5,2,256]{2,1,0:T(2,128)S(1)}, u32[]{:S(2)}, u32[]{:S(2)}) collective-permute-start(f32[5,2,256]{2,1,0:T(2,128)S(1)} %get-tuple-element.32), channel_id=1, source_target_pairs={{0,16},{16,0},{1,17},{17,1},{2,18},{18,2},{3,19},{19,3},{4,20},{20... | collective-permute-start | bytes 30728 | tf_op jit(solution)/shard_map/ppermute | solution.py:33
  161.7 5.4 %collective-permute-done.4.theirs = f32[5,2,256]{2,1,0:T(2,128)S(1)} collective-permute-done((f32[5,2,256]{2,1,0:T(2,128)S(1)}, f32[5,2,256]{2,1,0:T(2,128)S(1)}, u32[]{:S(2)}, u32[]{:S(2)}) %collective-permute-start.4) | collective-permute-done | bytes 10272 | tf_op jit(solution)/shard_map/ppermute | solution.py:33
  167.0 0.8 shard_map.76
  (21 shorter events, 4.4 us)
Async XLA Ops:
  0.6 14.5 %collective-permute-start = (f32[2,1024]{1,0:T(2,128)}, f32[2,1024]{1,0:T(2,128)S(1)}, u32[]{:S(2)}, u32[]{:S(2)}) collective-permute-start(f32[2,1024]{1,0:T(2,128)} %w.1), channel_id=1, source_target_pairs={{0,16},{16,0},{1,17},{17,1},{2,18},{18,2},{3,19},{19,3},{4,20},{20... | collective-permute-start | bytes 24584 | tf_op jit(solution)/shard_map/ppermute | solution.py:33
  11.6 1.0 copy-start
  12.6 0.7 copy-start.2
  15.1 15.5 %copy-start.1 = (f32[4,1024]{1,0:T(4,128)S(1)}, f32[4,1024]{1,0:T(4,128)}, u32[]{:S(2)}) copy-start(f32[4,1024]{1,0:T(4,128)} %h.1) | copy-start | bytes 49156
  47.3 10.0 %collective-permute-start.1 = (f32[120,128]{1,0:T(8,128)S(1)}, f32[120,128]{1,0:T(8,128)S(1)}, u32[]{:S(2)}, u32[]{:S(2)}) collective-permute-start(f32[120,128]{1,0:T(8,128)S(1)} %get-tuple-element.23.mine), channel_id=1, source_target_pairs={{0,256},{256,0},{1,257},{257,1},{2,258},{258,2},{3,259},{259,3},{4... | collective-permute-start | bytes 184328 | tf_op jit(solution)/shard_map/ppermute | solution.py:33
  82.9 14.4 %collective-permute-start.2 = (f32[5,4,256]{2,1,0:T(4,128)S(1)}, f32[5,4,256]{2,1,0:T(4,128)S(1)}, u32[]{:S(2)}, u32[]{:S(2)}) collective-permute-start(f32[5,4,256]{2,1,0:T(4,128)S(1)} %get-tuple-element.25.mine), channel_id=1, source_target_pairs={{0,16},{16,0},{1,17},{17,1},{2,18},{18,2},{3,19},{19,3},{4,20},{20... | collective-permute-start | bytes 61448 | tf_op jit(solution)/shard_map/ppermute | solution.py:33
  119.7 9.8 %collective-permute-start.3 = (f32[5,8,256]{2,1,0:T(8,128)S(1)}, f32[5,8,256]{2,1,0:T(8,128)S(1)}, u32[]{:S(2)}, u32[]{:S(2)}) collective-permute-start(f32[5,8,256]{2,1,0:T(8,128)S(1)} %shard_map.72.mine), channel_id=1, source_target_pairs={{0,256},{256,0},{1,257},{257,1},{2,258},{258,2},{3,259},{259,3},{4... | collective-permute-start | bytes 122888 | tf_op jit(solution)/shard_map/ppermute | solution.py:33
  152.7 14.3 %collective-permute-start.4 = (f32[5,2,256]{2,1,0:T(2,128)S(1)}, f32[5,2,256]{2,1,0:T(2,128)S(1)}, u32[]{:S(2)}, u32[]{:S(2)}) collective-permute-start(f32[5,2,256]{2,1,0:T(2,128)S(1)} %get-tuple-element.32), channel_id=1, source_target_pairs={{0,16},{16,0},{1,17},{17,1},{2,18},{18,2},{3,19},{19,3},{4,20},{20... | collective-permute-start | bytes 30728 | tf_op jit(solution)/shard_map/ppermute | solution.py:33

commit v14 on v12

--- a/solution.py
+++ b/solution.py
@@ -140,13 +140,18 @@
             out[q, 96 + 4 * i : 100 + 4 * i, :] = pair[i, 336:340, :]
 
 
-def h1_collect_kernel(got, out, cols):
+def h1_collect_kernel(got, out):
     total = got[0, :88, :]
     for q in range(1, NQ):
         total = total + got[q, :88, :]
     out[:88, :] = total
     for q in range(NQ):
         out[88 + 8 * q : 96 + 8 * q, :] = got[q, 88:96, :]
+
+
+def h1_lists_kernel(w0, got, w_all, cols):
+    w_arrange_kernel(w0, w_all)
+    for q in range(NQ):
         for i in range(2):
             read_list(cols, 2 * q + i, got[q, 96 + 4 * i : 97 + 4 * i, :])
 
@@ -318,9 +323,9 @@
     pair = lax.all_gather(sent, "core", axis=0)
     (sent,) = call(h1_build_kernel, (), (pair,), [(NQ, 104, COLS)], counts=(2 * CAP,))
     got = exchange(sent, QUAD)
-    mine, cols = call(h1_collect_kernel, (), (got,), [(120, COLS)], tables=[(NH * CAP,)])
+    (mine,) = call(h1_collect_kernel, (), (got,), [(120, COLS)])
     theirs = swap(mine, "z4")
-    (w_all,) = call(w_arrange_kernel, (), (w_got,), [(NB, RANK, BS)])
+    w_all, cols = call(h1_lists_kernel, (), (w_got, got), [(NB, RANK, BS)], tables=[(NH * CAP,)])
     (out,) = call(h1_update_kernel, (), (mine, theirs), [(NQ, RANK, COLS)])
     h_all = lax.all_gather(exchange(out, QUAD), "core", axis=0)
 

time: 169 us -> 168 us (level)
  no operation moved by 1% of the time
where the time goes in v14:
time: 168 us
  blocking collectives  99.7 us (59%)
  starting transfers between devices  31.2 us (19%)
  waiting for transfers between devices  28.3 us (17%)
  Pallas kernels  5.4 us (3%)
  local copies, waits for them, and re-layouts  2.35 us (1%)
    all_to_all x8, blocking collectives, exchange(): return lax.all_to_all(x, axes, split_axis=0, concat_axis=0, tiled=True)  95.6 us
    ppermute x5, starting transfers between devices, swap(): return lax.ppermute(x, axis, [(0, 1), (1, 0)])  31.2 us
    ppermute x5, waiting for transfers between devices, swap(): return lax.ppermute(x, axis, [(0, 1), (1, 0)])  28.3 us
    pallas_call x17, Pallas kernels, call(): pl.pallas_call(body, in_specs=[smem] * len(scalars) + [vmem] * len(arrays...  5.4 us
  transfers between devices with their start and end apart: 5, of which 5 were waited for; matrix products, arithmetic and copies ran while one was open for 0% of the time, Pallas kernels for 1%

profile of v14, /device:TPU:128, one launch (start us, length us, event | category | flops | bytes accessed | tf_op | source)
XLA Modules:
  0.0 167.7 jit_solution(14976418977139178997)
XLA Ops:
  0.6 10.9 %collective-permute-start = (f32[2,1024]{1,0:T(2,128)}, f32[2,1024]{1,0:T(2,128)S(1)}, u32[]{:S(2)}, u32[]{:S(2)}) collective-permute-start(f32[2,1024]{1,0:T(2,128)} %w.1), channel_id=1, source_target_pairs={{0,16},{16,0},{1,17},{17,1},{2,18},{18,2},{3,19},{19,3},{4,20},{20... | collective-permute-start | bytes 24584 | tf_op jit(solution)/shard_map/ppermute | solution.py:33
  11.6 1.0 copy-done
  12.6 0.7 copy-done.2
  13.3 0.9 shard_map.59
  14.2 0.9 collective-permute-done.theirs
  15.1 15.5 %all_to_all.40.w0 = f32[16,4,1024]{2,1,0:T(4,128)S(1)} all-to-all(f32[16,4,1024]{2,1,0:T(4,128)S(1)} %shard_map.60), channel_id=1, replica_groups=mesh['z4'=2,'z2'=2,'z1'=2,'core'=2,'zh'=2,'y'=4,'x'=4] {'y','x'}, dimensions={0} | all-to-all | bytes 524288 | tf_op jit(solution)/shard_map/all_to_all | solution.py:29
  31.1 2.1 %all-gather = f32[688,128]{1,0:T(8,128)S(1)} all-gather(f32[344,128]{1,0:T(8,128)S(1)} %get-tuple-element.22), channel_id=2, replica_groups=mesh['z4'=2,'z2'=2,'z1'=2,'core'=2,'zh'=2,'y'=4,'x'=4] {'core'}, dimensions={0}, use_global_device_ids=true | all-gather | bytes 528384 | tf_op jit(solution)/shard_map/all_gather | solution.py:323
  33.3 13.8 %all_to_all.41.got = f32[4,104,128]{2,1,0:T(8,128)S(1)} all-to-all(f32[4,104,128]{2,1,0:T(8,128)S(1)} %shard_map.62), channel_id=1, replica_groups=mesh['z4'=2,'z2'=2,'z1'=2,'core'=2,'zh'=2,'y'=4,'x'=4] {'z2','z1'}, dimensions={0} | all-to-all | bytes 425984 | tf_op jit(solution)/shard_map/all_to_all | solution.py:29
  47.1 1.9 %collective-permute-start.1 = (f32[120,128]{1,0:T(8,128)S(1)}, f32[120,128]{1,0:T(8,128)S(1)}, u32[]{:S(2)}, u32[]{:S(2)}) collective-permute-start(f32[120,128]{1,0:T(8,128)S(1)} %shard_map.64.mine), channel_id=1, source_target_pairs={{0,256},{256,0},{1,257},{257,1},{2,258},{258,2},{3,259},{259,3},{4... | collective-permute-start | bytes 184328 | tf_op jit(solution)/shard_map/ppermute | solution.py:33
  49.1 8.1 %collective-permute-done.1.theirs = f32[120,128]{1,0:T(8,128)S(1)} collective-permute-done((f32[120,128]{1,0:T(8,128)S(1)}, f32[120,128]{1,0:T(8,128)S(1)}, u32[]{:S(2)}, u32[]{:S(2)}) %collective-permute-start.1) | collective-permute-done | bytes 61472 | tf_op jit(solution)/shard_map/ppermute | solution.py:33
  57.5 11.2 %all_to_all.42 = f32[4,64,128]{2,1,0:T(8,128)S(1)} all-to-all(f32[4,64,128]{2,1,0:T(8,128)S(1)} %shard_map.65), channel_id=1, replica_groups=mesh['z4'=2,'z2'=2,'z1'=2,'core'=2,'zh'=2,'y'=4,'x'=4] {'z2','z1'}, dimensions={0} | all-to-all | bytes 262144 | tf_op jit(solution)/shard_map/all_to_all | solution.py:29
  68.7 2.0 %all-gather.1 = f32[8,64,128]{2,1,0:T(8,128)S(1)} all-gather(f32[4,64,128]{2,1,0:T(8,128)S(1)} %all_to_all.42), channel_id=3, replica_groups=mesh['z4'=2,'z2'=2,'z1'=2,'core'=2,'zh'=2,'y'=4,'x'=4] {'core'}, dimensions={0}, use_global_device_ids=true | all-gather | bytes 393216 | tf_op jit(solution)/shard_map/all_gather | solution.py:330
  71.1 11.2 %all_to_all.43.got = f32[16,4,768]{2,1,0:T(4,128)S(1)} all-to-all(f32[16,4,768]{2,1,0:T(4,128)S(1)} %shard_map.66), channel_id=1, replica_groups=mesh['z4'=2,'z2'=2,'z1'=2,'core'=2,'zh'=2,'y'=4,'x'=4] {'y','x'}, dimensions={0} | all-to-all | bytes 393216 | tf_op jit(solution)/shard_map/all_to_all | solution.py:29
  82.8 8.2 %collective-permute-start.2 = (f32[5,4,256]{2,1,0:T(4,128)S(1)}, f32[5,4,256]{2,1,0:T(4,128)S(1)}, u32[]{:S(2)}, u32[]{:S(2)}) collective-permute-start(f32[5,4,256]{2,1,0:T(4,128)S(1)} %get-tuple-element.25.mine), channel_id=1, source_target_pairs={{0,16},{16,0},{1,17},{17,1},{2,18},{18,2},{3,19},{19,3},{4,20},{20... | collective-permute-start | bytes 61448 | tf_op jit(solution)/shard_map/ppermute | solution.py:33
  91.2 6.0 %collective-permute-done.2.theirs = f32[5,4,256]{2,1,0:T(4,128)S(1)} collective-permute-done((f32[5,4,256]{2,1,0:T(4,128)S(1)}, f32[5,4,256]{2,1,0:T(4,128)S(1)}, u32[]{:S(2)}, u32[]{:S(2)}) %collective-permute-start.2) | collective-permute-done | bytes 20512 | tf_op jit(solution)/shard_map/ppermute | solution.py:33
  97.4 11.7 %all_to_all.44.w0.w_got = f32[16,4,1024]{2,1,0:T(4,128)S(1)} all-to-all(f32[16,4,1024]{2,1,0:T(4,128)S(1)} %get-tuple-element.27), channel_id=1, replica_groups=mesh['z4'=2,'z2'=2,'z1'=2,'core'=2,'zh'=2,'y'=4,'x'=4] {'y','x'}, dimensions={0} | all-to-all | bytes 524288 | tf_op jit(solution)/shard_map/all_to_all | solution.py:29
  109.5 9.9 %all_to_all.45.got = f32[8,8,640]{2,1,0:T(8,128)S(1)} all-to-all(f32[8,8,640]{2,1,0:T(8,128)S(1)} %shard_map.70), channel_id=1, replica_groups=mesh['z4'=2,'z2'=2,'z1'=2,'core'=2,'zh'=2,'y'=4,'x'=4] {'z2','z1','core'}, dimensions={0} | all-to-all | bytes 327680 | tf_op jit(solution)/shard_map/all_to_all | solution.py:29
  119.6 1.9 %collective-permute-start.3 = (f32[5,8,256]{2,1,0:T(8,128)S(1)}, f32[5,8,256]{2,1,0:T(8,128)S(1)}, u32[]{:S(2)}, u32[]{:S(2)}) collective-permute-start(f32[5,8,256]{2,1,0:T(8,128)S(1)} %shard_map.71.mine), channel_id=1, source_target_pairs={{0,256},{256,0},{1,257},{257,1},{2,258},{258,2},{3,259},{259,3},{4... | collective-permute-start | bytes 122888 | tf_op jit(solution)/shard_map/ppermute | solution.py:33
  121.5 7.9 %collective-permute-done.3.theirs = f32[5,8,256]{2,1,0:T(8,128)S(1)} collective-permute-done((f32[5,8,256]{2,1,0:T(8,128)S(1)}, f32[5,8,256]{2,1,0:T(8,128)S(1)}, u32[]{:S(2)}, u32[]{:S(2)}) %collective-permute-start.3) | collective-permute-done | bytes 40992 | tf_op jit(solution)/shard_map/ppermute | solution.py:33
  129.6 11.2 %all_to_all.46.h_got = f32[8,16,256]{2,1,0:T(8,128)S(1)} all-to-all(f32[8,16,256]{2,1,0:T(8,128)S(1)} %get-tuple-element.30), channel_id=1, replica_groups=mesh['z4'=2,'z2'=2,'z1'=2,'core'=2,'zh'=2,'y'=4,'x'=4] {'z2','z1','core'}, dimensions={0} | all-to-all | bytes 262144 | tf_op jit(solution)/shard_map/all_to_all | solution.py:29
  141.2 11.1 %all_to_all.47.got = f32[16,4,640]{2,1,0:T(4,128)S(1)} all-to-all(f32[16,4,640]{2,1,0:T(4,128)S(1)} %shard_map.73), channel_id=1, replica_groups=mesh['z4'=2,'z2'=2,'z1'=2,'core'=2,'zh'=2,'y'=4,'x'=4] {'y','x'}, dimensions={0} | all-to-all | bytes 327680 | tf_op jit(solution)/shard_map/all_to_all | solution.py:29
  152.6 8.2 %collective-permute-start.4 = (f32[5,2,256]{2,1,0:T(2,128)S(1)}, f32[5,2,256]{2,1,0:T(2,128)S(1)}, u32[]{:S(2)}, u32[]{:S(2)}) collective-permute-start(f32[5,2,256]{2,1,0:T(2,128)S(1)} %get-tuple-element.32), channel_id=1, source_target_pairs={{0,16},{16,0},{1,17},{17,1},{2,18},{18,2},{3,19},{19,3},{4,20},{20... | collective-permute-start | bytes 30728 | tf_op jit(solution)/shard_map/ppermute | solution.py:33
  161.5 5.4 %collective-permute-done.4.theirs = f32[5,2,256]{2,1,0:T(2,128)S(1)} collective-permute-done((f32[5,2,256]{2,1,0:T(2,128)S(1)}, f32[5,2,256]{2,1,0:T(2,128)S(1)}, u32[]{:S(2)}, u32[]{:S(2)}) %collective-permute-start.4) | collective-permute-done | bytes 10272 | tf_op jit(solution)/shard_map/ppermute | solution.py:33
  166.9 0.8 shard_map.75
  (20 shorter events, 4.3 us)
Async XLA Ops:
  0.6 14.5 %collective-permute-start = (f32[2,1024]{1,0:T(2,128)}, f32[2,1024]{1,0:T(2,128)S(1)}, u32[]{:S(2)}, u32[]{:S(2)}) collective-permute-start(f32[2,1024]{1,0:T(2,128)} %w.1), channel_id=1, source_target_pairs={{0,16},{16,0},{1,17},{17,1},{2,18},{18,2},{3,19},{19,3},{4,20},{20... | collective-permute-start | bytes 24584 | tf_op jit(solution)/shard_map/ppermute | solution.py:33
  11.6 1.0 copy-start
  12.6 0.7 copy-start.2
  15.1 15.5 %copy-start.1 = (f32[4,1024]{1,0:T(4,128)S(1)}, f32[4,1024]{1,0:T(4,128)}, u32[]{:S(2)}) copy-start(f32[4,1024]{1,0:T(4,128)} %h.1) | copy-start | bytes 49156
  47.1 10.0 %collective-permute-start.1 = (f32[120,128]{1,0:T(8,128)S(1)}, f32[120,128]{1,0:T(8,128)S(1)}, u32[]{:S(2)}, u32[]{:S(2)}) collective-permute-start(f32[120,128]{1,0:T(8,128)S(1)} %shard_map.64.mine), channel_id=1, source_target_pairs={{0,256},{256,0},{1,257},{257,1},{2,258},{258,2},{3,259},{259,3},{4... | collective-permute-start | bytes 184328 | tf_op jit(solution)/shard_map/ppermute | solution.py:33
  82.8 14.4 %collective-permute-start.2 = (f32[5,4,256]{2,1,0:T(4,128)S(1)}, f32[5,4,256]{2,1,0:T(4,128)S(1)}, u32[]{:S(2)}, u32[]{:S(2)}) collective-permute-start(f32[5,4,256]{2,1,0:T(4,128)S(1)} %get-tuple-element.25.mine), channel_id=1, source_target_pairs={{0,16},{16,0},{1,17},{17,1},{2,18},{18,2},{3,19},{19,3},{4,20},{20... | collective-permute-start | bytes 61448 | tf_op jit(solution)/shard_map/ppermute | solution.py:33
  119.6 9.8 %collective-permute-start.3 = (f32[5,8,256]{2,1,0:T(8,128)S(1)}, f32[5,8,256]{2,1,0:T(8,128)S(1)}, u32[]{:S(2)}, u32[]{:S(2)}) collective-permute-start(f32[5,8,256]{2,1,0:T(8,128)S(1)} %shard_map.71.mine), channel_id=1, source_target_pairs={{0,256},{256,0},{1,257},{257,1},{2,258},{258,2},{3,259},{259,3},{4... | collective-permute-start | bytes 122888 | tf_op jit(solution)/shard_map/ppermute | solution.py:33
  152.6 14.3 %collective-permute-start.4 = (f32[5,2,256]{2,1,0:T(2,128)S(1)}, f32[5,2,256]{2,1,0:T(2,128)S(1)}, u32[]{:S(2)}, u32[]{:S(2)}) collective-permute-start(f32[5,2,256]{2,1,0:T(2,128)S(1)} %get-tuple-element.32), channel_id=1, source_target_pairs={{0,16},{16,0},{1,17},{17,1},{2,18},{18,2},{3,19},{19,3},{4,20},{20... | collective-permute-start | bytes 30728 | tf_op jit(solution)/shard_map/ppermute | solution.py:33
